TPU v7x, 32 devices: a whole 2x2x4 slice. The times are simulated.
32 devices in a mesh: ctx: 16 (over z, x, core), head: 1, tp: 2 (over y).
Axes of the slice: x: 2, y: 2, z: 4, core: 2. Of those that a mesh axis runs over, the one named last changes fastest.
Arguments:
- text_states: bfloat16 [256, 8192], P(None, 'ctx'), may hold values from -6 to 6
- q_weight: bfloat16 [8192, 8192], P('ctx', ('head', 'tp')), may hold values from -0.0625 to 0.0625
- q_gain: float32 [128], replicated, may hold values from 0.1 to 1.9
- visual_key_cache: bfloat16 [8192, 1024], P('ctx', ('head', 'tp')), may hold values from -400 to 400
- visual_value_cache: bfloat16 [8192, 1024], P('ctx', ('head', 'tp')), may hold values from -6 to 6
- block_mask: int32 [256, 32], P(None, 'ctx'), may hold values from 0 to 1, as said below
- lengths: int32 [256], replicated, may hold values from 256 to 8192, as said below
- o_weight: bfloat16 [8192, 8192], P(('head', 'tp'), 'ctx'), may hold values from -0.59765625 to 0.59765625
Outputs:
- updated: bfloat16 [256, 8192], P(('head', 'tp'), 'ctx')
Inputs may be any that keep to these rules, and one draw needn't show every extreme that they name: `block_mask`: segment 0 is visible to every row. `lengths`: some row sees all 8192 tokens.
All inputs are finite; a program needn't handle non-finite values.
Results may differ from a plain program's by a relative error of at most 0.0055.
Values may be sent and summed in bfloat16 or wider, within the bound.
No kernel may reach another device: no remote copies, remote signals or barrier semaphores. Data moves between devices by JAX's collectives and lax.ppermute only.
A program may use at most 64 MiB of HBM per device.

v0:
```python
import functools

import jax
import jax.numpy as jnp
from jax import lax
from jax.experimental import pallas as pl
from jax.experimental.pallas import tpu as pltpu
from jax.sharding import PartitionSpec as P


F32, BF16, I16, I32 = jnp.float32, jnp.bfloat16, jnp.int16, jnp.int32
LANES = 128
TAIL = 16
CODE_TOP = 32000.0
LOW = -1e30
NO_SUM = -32000.0
VM = pl.BlockSpec(memory_space=pltpu.VMEM)
HB = pl.BlockSpec(memory_space=pltpu.HBM)

PROJECT_GRANT = 16


class Position:
    def __getitem__(self, i):
        me = lax.axis_index("ctx")
        if i == 0:
            return lax.rem(me, 2)
        if i == 1:
            return lax.rem(lax.div(me, 2), 2)
        if i == 2:
            return lax.div(me, 4)
        return lax.axis_index("head") * lax.axis_size("tp") + lax.axis_index("tp")


ids = Position()


def call(kernel, out_shape, args, flops=0, specs=None, scratch=(), grant=16):
    moved = sum(a.size * a.dtype.itemsize for a in args)
    moved += sum(o.size * o.dtype.itemsize for o in jax.tree.leaves(out_shape))
    return pl.pallas_call(
        kernel,
        out_shape=out_shape,
        in_specs=specs or [VM] * len(args),
        out_specs=jax.tree.map(lambda _: VM, out_shape),
        scratch_shapes=list(scratch),
        cost_estimate=pl.CostEstimate(flops=int(flops), bytes_accessed=int(moved), transcendentals=0),
        compiler_params=pltpu.CompilerParams(vmem_limit_bytes=grant * 2**20),
    )(*args)


def power_of(top):
    return jnp.floor(jnp.log2(jnp.maximum(top, 1e-30))) + 1.0


def encode_heads(parts, code_ref):
    rows = parts[0].shape[0]
    lane = lax.broadcasted_iota(I32, (rows, LANES), 1)
    tops = jnp.zeros((rows, LANES), F32)
    for h, part in enumerate(parts):
        tops = jnp.where(lane == h, jnp.max(jnp.abs(part), axis=1, keepdims=True), tops)
    power = power_of(tops)
    scale = jnp.exp2(-power) * CODE_TOP
    for h, part in enumerate(parts):
        code = jnp.round(part * scale[:, h : h + 1])
        code_ref[:, h * LANES : (h + 1) * LANES] = code.astype(I32).astype(I16)
    code_ref[:, len(parts) * LANES :] = power.astype(I32).astype(I16)


def scales_of(code_ref):
    width = code_ref.shape[1] - LANES
    return jnp.exp2(code_ref[:, width:].astype(I32).astype(F32)) * (1.0 / CODE_TOP)


def decode_head(code_ref, scales, h):
    return code_ref[:, h * LANES : (h + 1) * LANES].astype(I32).astype(F32) * scales[:, h : h + 1]


def pack_kernel(groups, key_ref, value_ref, mask_ref, *outs):
    keys = key_ref.shape[0]
    for d in range(groups):
        at = pl.multiple_of((ids[2] ^ d) * LANES, LANES)
        outs[d][:keys, :] = key_ref[:, pl.ds(at, LANES)]
        outs[d][keys : 2 * keys, :] = jnp.concatenate(
            [
                jnp.transpose(value_ref[pl.ds(c * LANES, LANES), pl.ds(at, LANES)])
                for c in range(keys // LANES)
            ],
            axis=0,
        )
        outs[d][2 * keys :, :] = mask_ref[...]


def project_kernel(ds, x_ref, w_hbm, send_ref, keep_ref, w_buf, sems):
    half = x_ref.shape[0] // 2
    width = w_buf.shape[2]
    copies = []
    for i, d in enumerate(ds):
        at = pl.multiple_of((ids[2] ^ d) * width, width)
        copies.append(pltpu.make_async_copy(w_hbm.at[:, pl.ds(at, width)], w_buf.at[i], sems.at[i]))
        copies[-1].start()
    peer = pl.multiple_of((1 - ids[0]) * half, half)
    mine = pl.multiple_of(ids[0] * half, half)
    for i in range(len(ds)):
        copies[i].wait()
        cols = slice(i * width, (i + 1) * width)
        w = w_buf[i]
        send_ref[:, cols] = jnp.dot(x_ref[pl.ds(peer, half), :], w, preferred_element_type=F32)
        keep_ref[:, cols] = jnp.dot(x_ref[pl.ds(mine, half), :], w, preferred_element_type=F32)


def split_x_kernel(keep_ref, got_ref, code_ref, own_ref):
    half, width = own_ref.shape
    mine = pl.multiple_of(ids[1] * half, half)
    peer = pl.multiple_of((1 - ids[1]) * half, half)
    parts = []
    for h in range(width // LANES):
        cols = slice(h * LANES, (h + 1) * LANES)
        parts.append(keep_ref[pl.ds(peer, half), cols] + got_ref[pl.ds(peer, half), cols])
    encode_heads(parts, code_ref)
    own_ref[...] = keep_ref[pl.ds(mine, half), :] + got_ref[pl.ds(mine, half), :]


def split_z_kernel(ds, own_ref, got_ref, *outs):
    heads = own_ref.shape[1] // len(ds) // LANES
    scales = scales_of(got_ref)
    for i, d in enumerate(ds):
        parts = []
        for h in range(i * heads, (i + 1) * heads):
            parts.append(own_ref[:, h * LANES : (h + 1) * LANES] + decode_head(got_ref, scales, h))
        if d:
            encode_heads(parts, outs[i])
        else:
            for h, part in enumerate(parts):
                outs[i][:, h * LANES : (h + 1) * LANES] = part


def norm_kernel(own_ref, gain_ref, *rest):
    got, out_ref = rest[:-1], rest[-1]
    gain = gain_ref[...]
    scales = [scales_of(g) for g in got]
    for h in range(out_ref.shape[1] // LANES):
        cols = slice(h * LANES, (h + 1) * LANES)
        total = own_ref[:, cols]
        for g, scale in zip(got, scales):
            total = total + decode_head(g, scale, h)
        mean_sq = jnp.mean(total * total, axis=1, keepdims=True)
        out_ref[:, cols] = (total * lax.rsqrt(mean_sq + 1e-05) * gain).astype(BF16)


def attend_kernel(ds, heads, segments, rel, begin, finish, q_ref, lens_ref, *rest):
    packs, rest = rest[: len(ds)], rest[len(ds) :]
    state, outs = (None, rest) if begin else (rest[:2], rest[2:])
    rows = q_ref.shape[0]
    keys = (packs[0].shape[0] - TAIL) // 2
    seg = keys // segments
    units = heads * rows // LANES
    scale = 1.4426950408889634 / LANES**0.5
    core, x = ids[0] ^ (rel & 1), ids[1] ^ (rel >> 1)
    low_lanes = lax.broadcasted_iota(I32, (8, LANES), 1) < rows
    take_low = jnp.full((8, LANES), 1 - x, I32) == 1

    def twice(row):
        wide = jnp.broadcast_to(row, (8, LANES))
        turned = pltpu.roll(wide, rows, 1)
        return jnp.where(take_low == low_lanes, wide, turned)[:1]

    lens = twice(jnp.where(core == 1, lens_ref[1:2, :], lens_ref[0:1, :]))
    stacked = jnp.concatenate([q_ref[:, h * LANES : (h + 1) * LANES] for h in range(heads)], axis=0)
    highs, sums, nums = [], [], []
    for b, pack in zip(ds, packs):
        raw = lax.dot_general(pack[:keys, :], stacked, (((1,), (1,)), ((), ())), preferred_element_type=F32)
        tail = pack[2 * keys :, :].astype(F32)
        first = ((ids[2] ^ b) * 4 + ids[1] * 2 + ids[0]) * keys
        masks = []
        for s in range(segments):
            seen = twice(jnp.where(core == 1, tail[2 * s + 1 : 2 * s + 2, :], tail[2 * s : 2 * s + 1, :]))
            limit = jnp.where(seen > 0.5, lens - (first + s * seg), 0)
            inside = lax.broadcasted_iota(I32, (seg, LANES), 0) < limit
            masks.append(jnp.where(inside, F32(0.0), F32(LOW)))
        bias = jnp.concatenate(masks, axis=0)
        unit_highs, unit_sums, unit_weights = [], [], []
        for u in range(units):
            scores = raw[:, u * LANES : (u + 1) * LANES] * scale + bias
            high = jnp.maximum(jnp.max(scores, axis=0, keepdims=True), -1e29)
            weights = jnp.exp2(scores - high)
            unit_highs.append(high)
            unit_sums.append(jnp.sum(weights, axis=0, keepdims=True))
            unit_weights.append(weights.astype(BF16))
        highs.append(jnp.concatenate(unit_highs, axis=1))
        sums.append(jnp.concatenate(unit_sums, axis=1))
        value = jnp.concatenate(
            [pack[keys + c * LANES : keys + (c + 1) * LANES, :] for c in range(keys // LANES)], axis=1
        )
        nums.append(jnp.dot(value, jnp.concatenate(unit_weights, axis=1), preferred_element_type=F32))
    if not begin:
        highs.append(state[1][:1, :])
        sums.append(state[1][1:2, :])
        nums.append(state[0][...])
    top = functools.reduce(jnp.maximum, highs)
    factors = [jnp.exp2(h - top) for h in highs]
    total = functools.reduce(jnp.add, [s * f for s, f in zip(sums, factors)])
    num = functools.reduce(jnp.add, [n * f for n, f in zip(nums, factors)])
    if not finish:
        outs[0][...] = num
        line = lax.broadcasted_iota(I32, outs[1].shape, 0)
        outs[1][...] = jnp.where(line == 0, top, total)
        return
    some = total > 0.0
    out = num * jnp.where(some, 1.0 / jnp.where(some, total, 1.0), 0.0)
    level = jnp.where(some, top + jnp.log2(jnp.where(some, total, 1.0)), NO_SUM)
    if rel == 0:
        out_ref, level_ref = outs
        out_ref[...] = out
        level_ref[...] = jnp.broadcast_to(level, level_ref.shape)
        return
    (code_ref,) = outs
    power = power_of(jnp.max(jnp.abs(out), axis=0, keepdims=True))
    code_ref[:LANES, :] = jnp.round(out * (jnp.exp2(-power) * CODE_TOP)).astype(I32).astype(I16)
    whole = jnp.round(level)
    fine = jnp.clip(jnp.round((level - whole) * 65536.0), -32767.0, 32767.0)
    line = lax.broadcasted_iota(I32, (TAIL, heads * rows), 0)
    tail = jnp.where(line == 0, power, jnp.where(line == 1, whole, jnp.where(line == 2, fine, 0.0)))
    code_ref[LANES:, :] = tail.astype(I32).astype(I16)


def merge_kernel(heads, own_ref, level_ref, *rest):
    got, out_ref = rest[:-1], rest[-1]
    rows = out_ref.shape[0]
    tails = [g[LANES:, :].astype(I32).astype(F32) for g in got]
    levels = [level_ref[:1, :]] + [t[1:2] + t[2:3] * (1.0 / 65536.0) for t in tails]
    top = functools.reduce(jnp.maximum, levels)
    shares = [jnp.exp2(level - top) for level in levels]
    inverse = 1.0 / functools.reduce(jnp.add, shares)
    num = own_ref[...] * (shares[0] * inverse)
    for g, tail, share in zip(got, tails, shares[1:]):
        weight = jnp.exp2(tail[:1]) * (1.0 / CODE_TOP) * share * inverse
        num = num + g[:LANES, :].astype(I32).astype(F32) * weight
    per = LANES // rows
    for u in range(heads // per):
        block = jnp.transpose(num[:, u * LANES : (u + 1) * LANES])
        for p in range(per):
            h = u * per + p
            out_ref[:, h * LANES : (h + 1) * LANES] = block[p * rows : (p + 1) * rows].astype(BF16)


def output_part(ds, blocks, w_ref):
    width = blocks[0][0].shape[1]
    total = None
    for d, row_blocks in zip(ds, blocks):
        left = jnp.concatenate([b[...] for b in row_blocks], axis=0)
        base = pl.multiple_of((ids[2] ^ d) * width, width)
        part = jnp.dot(left, w_ref[pl.ds(base, width), :], preferred_element_type=F32)
        total = part if total is None else total + part
    return total


def output_first_kernel(ds, w_ref, *rest):
    blocks = [rest[4 * i : 4 * i + 4] for i in range(len(ds))]
    rest[-1][...] = output_part(ds, blocks, w_ref)


def output_last_kernel(ds, w_ref, before_ref, *rest):
    blocks, (keep_ref, code_ref, send_buf) = [rest[4 * i : 4 * i + 4] for i in range(len(ds))], rest[-3:]
    total = output_part(ds, blocks, w_ref) + before_ref[...]
    rows = total.shape[0] // 4
    swap_core = jnp.full((rows, 1), (ids[0] == ids[3]).astype(I32), I32) == 1
    for xs in range(2):
        at = pl.multiple_of((ids[1] ^ xs) * rows, rows)
        own = total[xs * rows : (xs + 1) * rows]
        other = total[(2 + xs) * rows : (3 + xs) * rows]
        send_buf[pl.ds(at, rows), :] = jnp.where(swap_core, other, own)
        keep_ref[pl.ds(at, rows), :] = jnp.where(swap_core, own, other)
    width = send_buf.shape[1]
    encode_heads([send_buf[:, h * LANES : (h + 1) * LANES] for h in range(width // LANES)], code_ref)


def finish_kernel(keep_ref, got_ref, text_ref, out_ref):
    rows, width = out_ref.shape
    at = pl.multiple_of(ids[3] * rows, rows)
    scales = scales_of(got_ref)
    for h in range(width // LANES):
        cols = slice(h * LANES, (h + 1) * LANES)
        total = keep_ref[:, cols] + decode_head(got_ref, scales, h)
        out_ref[:, cols] = (text_ref[pl.ds(at, rows), cols].astype(F32) + total).astype(BF16)


def fast_shards(text_states, q_weight, q_gain, key_cache, value_cache, block_mask, lengths, o_weight):
    ctx = lax.axis_size("ctx")
    struct = jax.ShapeDtypeStruct
    text_rows, depth = text_states.shape
    columns = q_weight.shape[1]
    keys = key_cache.shape[0]
    groups = key_cache.shape[1] // LANES
    width = columns // groups
    heads = width // LANES
    rows, half = text_rows // 4, text_rows // 2
    pairs = heads * rows
    segments = block_mask.shape[1]
    out_cols = o_weight.shape[1]

    def swap(value, bits):
        return lax.ppermute(value, "ctx", [(i, i ^ bits) for i in range(ctx)])

    def after(value, *others):
        return lax.optimization_barrier((value, *others))[0]

    lines = segments * text_rows // LANES
    mask_rows = jnp.pad(block_mask.T.astype(BF16).reshape(lines, LANES), ((0, TAIL - lines), (0, 0)))
    packs = call(
        functools.partial(pack_kernel, groups),
        (struct((2 * keys + TAIL, LANES), BF16),) * groups,
        (key_cache, value_cache, mask_rows),
    )
    packs = [packs[0]] + [swap(packs[d], 4 * d) for d in range(1, groups)]

    order = list(range(groups - 1, -1, -1))
    chunks = [[d] for d in order[: groups // 2]] + [order[groups // 2 :]]
    sums = {}
    text = text_states
    weight = pltpu.with_memory_space_constraint(q_weight, pltpu.HBM)
    for ds in chunks:
        wide = len(ds) * width
        part = struct((half, wide), F32)
        sent, kept = call(
            functools.partial(project_kernel, ds),
            (part, part),
            (text, weight),
            flops=2 * text_rows * depth * wide,
            specs=[VM, HB],
            scratch=[pltpu.VMEM((len(ds), depth, width), BF16), pltpu.SemaphoreType.DMA((len(ds),))],
            grant=PROJECT_GRANT,
        )
        got = swap(sent, 1)
        code, own = call(split_x_kernel, (struct((rows, wide + LANES), I16), struct((rows, wide), F32)), (kept, got))
        text = after(text_states, code)
        got = swap(code, 2)
        outs = call(
            functools.partial(split_z_kernel, ds),
            tuple(struct((rows, width + LANES), I16) if d else struct((rows, width), F32) for d in ds),
            (own, got),
        )
        for d, out in zip(ds, outs):
            sums[d] = swap(out, 4 * d) if d else out
    normed = call(
        norm_kernel,
        struct((rows, width), BF16),
        (sums[0], q_gain.reshape(1, LANES), *[sums[d] for d in range(1, groups)]),
    )

    lens = lengths.reshape(2, LANES)
    last = groups // 2
    first = [d for d in order[::-1] if d != last]
    queries = {t: swap(normed, t) if t else normed for t in range(4)}
    turns = (0, 2, 3, 1)
    states, previous = {}, ()
    for rel in turns:
        states[rel] = call(
            functools.partial(attend_kernel, first, heads, segments, rel, True, False),
            (struct((LANES, pairs), F32), struct((8, pairs), F32)),
            (after(queries[rel], *previous), lens, *[packs[d] for d in first]),
            flops=4 * pairs * keys * len(first) * LANES,
        )
        previous = states[rel]
    outs = {}
    for rel in turns[1:] + turns[:1]:
        if rel:
            shape = struct((LANES + TAIL, pairs), I16)
        else:
            shape = (struct((LANES, pairs), F32), struct((8, pairs), F32))
        res = call(
            functools.partial(attend_kernel, [last], heads, segments, rel, False, True),
            shape,
            (after(queries[rel], previous), lens, packs[last], *states[rel]),
            flops=4 * pairs * keys * LANES,
        )
        previous = res
        outs[rel] = swap(res, rel) if rel else res
    attended = call(
        functools.partial(merge_kernel, heads), struct((rows, width), BF16), (*outs[0], outs[1], outs[2], outs[3])
    )

    column = {d: swap(attended, 4 * d) if d else attended for d in order}
    beside = {d: swap(column[d], 2) for d in range(groups)}
    early, late = list(range(groups // 2)), list(range(groups // 2, groups))
    tail_d = late[0]

    def over_core(values):
        if len(values) == 1:
            return [swap(values[0], 1)]
        moved = swap(jnp.stack(values), 1)
        return [moved[i] for i in range(len(values))]

    blocks = {}
    moved = over_core([b for d in early for b in (column[d], beside[d])])
    for i, d in enumerate(early):
        blocks[d] = (column[d], beside[d], moved[2 * i], moved[2 * i + 1])
    pairs_late = [(d, side) for d in reversed(late) for side in (column, beside)][:-1]
    moved = over_core([side[d] for d, side in pairs_late])
    end = over_core([beside[tail_d]])
    moved = moved + end
    for i, d in enumerate(reversed(late)):
        blocks[d] = (column[d], beside[d], moved[2 * i], moved[2 * i + 1])
    before = call(
        functools.partial(output_first_kernel, early),
        struct((text_rows, out_cols), F32),
        (o_weight, *[b for d in early for b in blocks[d]]),
        flops=2 * text_rows * width * len(early) * out_cols,
    )
    kept, code = call(
        functools.partial(output_last_kernel, late),
        (struct((half, out_cols), F32), struct((half, out_cols + LANES), I16)),
        (o_weight, before, *[b for d in late for b in blocks[d]]),
        flops=2 * text_rows * width * len(late) * out_cols,
        scratch=[pltpu.VMEM((half, out_cols), F32)],
    )
    got = lax.ppermute(code, ("head", "tp"), [(0, 1), (1, 0)])
    return call(finish_kernel, struct((half, out_cols), BF16), (kept, got, text_states))


def plain_shards(
    text_states,
    q_weight,
    q_gain,
    visual_key_cache,
    visual_value_cache,
    block_mask,
    lengths,
    o_weight,
):
    text_rows = text_states.shape[0]
    columns = q_weight.shape[1]
    head_dim = q_gain.shape[0]
    query_heads = columns // head_dim
    kv_heads = visual_key_cache.shape[1] // head_dim
    query_group_count = query_heads // kv_heads
    row_block = text_states
    query_share = lax.psum_scatter(
        jnp.dot(row_block, q_weight, preferred_element_type=jnp.float32),
        "ctx",
        scatter_dimension=0,
        tiled=True,
    )
    shaped = query_share.reshape(query_share.shape[0], query_heads, head_dim)
    mean_sq = jnp.mean(shaped * shaped, axis=-1, keepdims=True)
    normed = shaped * lax.rsqrt(mean_sq + 1e-05) * q_gain
    queries = lax.all_gather(
        normed.reshape(query_share.shape[0], columns).astype(jnp.bfloat16),
        "ctx",
        axis=0,
        tiled=True,
    )
    keys_local = visual_key_cache.shape[0]
    segment_len = keys_local // block_mask.shape[1]
    key_block_offset = lax.axis_index("ctx") * keys_local
    positions = key_block_offset + jnp.arange(keys_local, dtype=jnp.int32)
    allowed = (jnp.repeat(block_mask, segment_len, axis=1) == 1) & (
        positions[None, :] < lengths[:, None]
    )
    score_scale = 1.0 / head_dim**0.5
    partial_nums = []
    partial_maxes = []
    partial_totals = []
    for q_head in range(query_heads):
        kv_head = q_head // query_group_count
        query_part = queries[:, q_head * head_dim : (q_head + 1) * head_dim]
        key_part = visual_key_cache[:, kv_head * head_dim : (kv_head + 1) * head_dim]
        value_part = visual_value_cache[:, kv_head * head_dim : (kv_head + 1) * head_dim]
        scores = (
            lax.dot_general(
                query_part, key_part, (((1,), (1,)), ((), ())), preferred_element_type=jnp.float32
            )
            * score_scale
        )
        scores = jnp.where(allowed, scores, jnp.float32(-1e30))
        local_max = jnp.max(scores, axis=1)
        weights = jnp.where(allowed, jnp.exp(scores - local_max[:, None]), jnp.float32(0.0))
        partial_totals.append(jnp.sum(weights, axis=1))
        partial_maxes.append(local_max)
        partial_nums.append(
            jnp.dot(weights.astype(jnp.bfloat16), value_part, preferred_element_type=jnp.float32)
        )
    local_num = jnp.concatenate(partial_nums, axis=1)
    local_max = jnp.stack(partial_maxes, axis=1)
    local_total = jnp.stack(partial_totals, axis=1)
    highest = lax.pmax(local_max, "ctx")
    factor = jnp.exp(local_max - highest)
    scaled_num = local_num * jnp.repeat(factor, head_dim, axis=1)
    scaled_total = local_total * factor
    owned_num, owned_total = (
        lax.psum_scatter(scaled_num, "ctx", scatter_dimension=0, tiled=True),
        lax.psum_scatter(scaled_total, "ctx", scatter_dimension=0, tiled=True),
    )
    owned = (owned_num / jnp.repeat(owned_total, head_dim, axis=1)).astype(jnp.bfloat16)
    attended = lax.all_gather(owned, "ctx", axis=0, tiled=True)
    rows_out = text_rows // lax.axis_size(("head", "tp"))
    row_block = attended
    summed = lax.psum_scatter(
        jnp.dot(row_block, o_weight, preferred_element_type=jnp.float32),
        ("head", "tp"),
        scatter_dimension=0,
        tiled=True,
    )
    residual = lax.dynamic_slice_in_dim(
        text_states, lax.axis_index(("head", "tp")) * rows_out, rows_out, 0
    )
    return (residual.astype(jnp.float32) + summed).astype(jnp.bfloat16)


def solution(mesh):
    in_specs = (
        P(None, "ctx"),
        P("ctx", ("head", "tp")),
        P(),
        P("ctx", ("head", "tp")),
        P("ctx", ("head", "tp")),
        P(None, "ctx"),
        P(),
        P(("head", "tp"), "ctx"),
    )
    out_specs = P(("head", "tp"), "ctx")
    ctx, halves = mesh.shape["ctx"], mesh.shape["head"] * mesh.shape["tp"]

    def fits(args):
        text_rows = args[0].shape[0]
        groups = args[3].shape[1] // args[2].shape[0]
        return (
            args[2].shape[0] == LANES
            and halves == 2
            and text_rows == 2 * LANES
            and groups > 1
            and groups & (groups - 1) == 0
            and ctx == 4 * groups
            and args[1].shape[1] % (groups * LANES) == 0
            and args[1].shape[1] // groups <= LANES * LANES
            and 2 * args[5].shape[1] <= TAIL
            and args[3].shape[0] % (args[5].shape[1] * LANES) == 0
        )

    def shards(*args):
        if not fits(args):
            return plain_shards(*args)
        return fast_shards(*args)

    spread = jax.shard_map(shards, mesh=mesh, in_specs=in_specs, out_specs=out_specs, check_vma=False)
    if halves != 2 or ctx != 16:
        return spread
    return spread
```

profile of v0, /device:TPU:0, one launch (start us, length us, event | category | flops | bytes accessed | tf_op | source)
XLA Modules:
  0.0 111.9 jit_solution(12528867173227020841)
XLA Ops:
  0.0 0.9 copy-done.1
  1.0 1.7 %shard_map.82 = (f32[128,1024]{1,0:T(8,128)S(1)}, f32[128,1024]{1,0:T(8,128)S(1)}) custom-call(bf16[256,512]{1,0:T(8,128)(2,1)S(1)} %copy-done.1, bf16[512,4096]{1,0:T(8,128)(2,1)} %w_hbm.5), custom_call_target="tpu_custom_call" | custom-call | flops 268435456 | bytes 5505024 | tf_op jit(solution)/shard_map/pallas_call | solution.py:41
  2.7 0.6 collective-permute-start
  3.2 1.5 %collective-permute-done.got_ref = f32[128,1024]{1,0:T(8,128)S(1)} collective-permute-done((f32[128,1024]{1,0:T(8,128)S(1)}, f32[128,1024]{1,0:T(8,128)S(1)}, u32[]{:S(2)}, u32[]{:S(2)}) %collective-permute-start) | collective-permute-done | bytes 524320 | tf_op jit(solution)/shard_map/ppermute | solution.py:303
  4.8 0.3 shard_map.83
  5.1 1.7 %shard_map.84 = (f32[128,1024]{1,0:T(8,128)S(1)}, f32[128,1024]{1,0:T(8,128)S(1)}) custom-call(bf16[256,512]{1,0:T(8,128)(2,1)S(1)} %copy-done.2, bf16[512,4096]{1,0:T(8,128)(2,1)} %w_hbm.5), custom_call_target="tpu_custom_call" | custom-call | flops 268435456 | bytes 5505024 | tf_op jit(solution)/shard_map/pallas_call | solution.py:41
  6.9 0.4 collective-permute-start.1
  7.3 1.5 %collective-permute-done.1.got_ref = f32[128,1024]{1,0:T(8,128)S(1)} collective-permute-done((f32[128,1024]{1,0:T(8,128)S(1)}, f32[128,1024]{1,0:T(8,128)S(1)}, u32[]{:S(2)}, u32[]{:S(2)}) %collective-permute-start.1) | collective-permute-done | bytes 524320 | tf_op jit(solution)/shard_map/ppermute | solution.py:303
  8.9 0.3 shard_map.85
  9.2 2.2 %shard_map.86 = (f32[128,2048]{1,0:T(8,128)S(1)}, f32[128,2048]{1,0:T(8,128)S(1)}) custom-call(bf16[256,512]{1,0:T(8,128)(2,1)S(1)} %copy-done.2, bf16[512,4096]{1,0:T(8,128)(2,1)} %w_hbm.5), custom_call_target="tpu_custom_call" | custom-call | flops 536870912 | bytes 6553600 | tf_op jit(solution)/shard_map/pallas_call | solution.py:41
  11.4 0.4 collective-permute-start.2
  11.8 2.3 %collective-permute-done.2.got_ref = f32[128,2048]{1,0:T(8,128)S(1)} collective-permute-done((f32[128,2048]{1,0:T(8,128)S(1)}, f32[128,2048]{1,0:T(8,128)S(1)}, u32[]{:S(2)}, u32[]{:S(2)}) %collective-permute-start.2) | collective-permute-done | bytes 1048608 | tf_op jit(solution)/shard_map/ppermute | solution.py:303
  14.1 0.5 shard_map.87
  14.7 2.9 %collective-permute-start.3 = (s16[64,2176]{1,0:T(8,128)(2,1)S(1)}, s16[64,2176]{1,0:T(8,128)(2,1)S(1)}, u32[]{:S(2)}, u32[]{:S(2)}) collective-permute-start(s16[64,2176]{1,0:T(8,128)(2,1)S(1)} %get-tuple-element.55), channel_id=1, source_target_pairs={{0,4},{2,6},{4,0},{6,2},{8,12},{10,14},{12,8},{14,10},{16,20},{18,... | collective-permute-start | bytes 835592 | tf_op jit(solution)/shard_map/ppermute | solution.py:303
  17.6 1.9 %collective-permute-start.5 = (s16[64,1152]{1,0:T(8,128)(2,1)S(1)}, s16[64,1152]{1,0:T(8,128)(2,1)S(1)}, u32[]{:S(2)}, u32[]{:S(2)}) collective-permute-start(s16[64,1152]{1,0:T(8,128)(2,1)S(1)} %get-tuple-element.50), channel_id=1, source_target_pairs={{0,4},{2,6},{4,0},{6,2},{8,12},{10,14},{12,8},{14,10},{16,20},{18,... | collective-permute-start | bytes 442376 | tf_op jit(solution)/shard_map/ppermute | solution.py:303
  19.6 0.2 shard_map.92
  19.9 1.6 %collective-permute-start.12 = (bf16[1040,128]{1,0:T(8,128)(2,1)S(1)}, bf16[1040,128]{1,0:T(8,128)(2,1)S(1)}, u32[]{:S(2)}, u32[]{:S(2)}) collective-permute-start(bf16[1040,128]{1,0:T(8,128)(2,1)S(1)} %get-tuple-element.61), channel_id=1, source_target_pairs={{0,8},{2,10},{4,12},{6,14},{8,0},{10,2},{12,4},{14,6},{16,24},{18,... | collective-permute-start | bytes 798728 | tf_op jit(solution)/shard_map/ppermute | solution.py:303
  21.5 2.5 %collective-permute-start.13 = (bf16[1040,128]{1,0:T(8,128)(2,1)S(1)}, bf16[1040,128]{1,0:T(8,128)(2,1)S(1)}, u32[]{:S(2)}, u32[]{:S(2)}) collective-permute-start(bf16[1040,128]{1,0:T(8,128)(2,1)S(1)} %get-tuple-element.62), channel_id=1, source_target_pairs={{0,24},{2,26},{4,28},{6,30},{8,16},{10,18},{12,20},{14,22},{16,8},... | collective-permute-start | bytes 798728 | tf_op jit(solution)/shard_map/ppermute | solution.py:303
  24.0 4.2 %collective-permute-done.7.got_ref = s16[64,1152]{1,0:T(8,128)(2,1)S(1)} collective-permute-done((s16[64,1152]{1,0:T(8,128)(2,1)S(1)}, s16[64,1152]{1,0:T(8,128)(2,1)S(1)}, u32[]{:S(2)}, u32[]{:S(2)}) %collective-permute-start.7) | collective-permute-done | bytes 147488 | tf_op jit(solution)/shard_map/ppermute | solution.py:303
  28.2 0.4 shard_map.90
  28.7 4.2 %collective-permute-start.8 = (s16[64,1152]{1,0:T(8,128)(2,1)S(1)}, s16[64,1152]{1,0:T(8,128)(2,1)S(1)}, u32[]{:S(2)}, u32[]{:S(2)}) collective-permute-start(s16[64,1152]{1,0:T(8,128)(2,1)S(1)} %shard_map.90), channel_id=1, source_target_pairs={{0,24},{2,26},{4,28},{6,30},{8,16},{10,18},{12,20},{14,22},{16,8},... | collective-permute-start | bytes 442376 | tf_op jit(solution)/shard_map/ppermute | solution.py:303
  32.9 0.4 shard_map.89
  33.3 0.9 collective-permute-start.6
  34.2 0.5 shard_map.88
  34.7 1.6 %collective-permute-start.4 = (s16[64,1152]{1,0:T(8,128)(2,1)S(1)}, s16[64,1152]{1,0:T(8,128)(2,1)S(1)}, u32[]{:S(2)}, u32[]{:S(2)}) collective-permute-start(s16[64,1152]{1,0:T(8,128)(2,1)S(1)} %get-tuple-element.57), channel_id=1, source_target_pairs={{0,8},{2,10},{4,12},{6,14},{8,0},{10,2},{12,4},{14,6},{16,24},{18,... | collective-permute-start | bytes 442376 | tf_op jit(solution)/shard_map/ppermute | solution.py:303
  36.4 3.8 %collective-permute-done.8.rest_2_ = s16[64,1152]{1,0:T(8,128)(2,1)S(1)} collective-permute-done((s16[64,1152]{1,0:T(8,128)(2,1)S(1)}, s16[64,1152]{1,0:T(8,128)(2,1)S(1)}, u32[]{:S(2)}, u32[]{:S(2)}) %collective-permute-start.8) | collective-permute-done | bytes 147488 | tf_op jit(solution)/shard_map/ppermute | solution.py:303
  40.2 7.8 %collective-permute-start.14 = (bf16[1040,128]{1,0:T(8,128)(2,1)S(1)}, bf16[1040,128]{1,0:T(8,128)(2,1)S(1)}, u32[]{:S(2)}, u32[]{:S(2)}) collective-permute-start(bf16[1040,128]{1,0:T(8,128)(2,1)S(1)} %get-tuple-element.75), channel_id=1, source_target_pairs={{0,16},{2,18},{4,20},{6,22},{8,24},{10,26},{12,28},{14,30},{16,0},... | collective-permute-start | bytes 798728 | tf_op jit(solution)/shard_map/ppermute | solution.py:303
  48.1 0.9 shard_map.91.q_ref
  49.0 0.6 collective-permute-start.11
  49.6 0.9 collective-permute-start.10
  50.5 0.8 collective-permute-start.9
  51.2 1.6 %shard_map.93 = (f32[128,512]{1,0:T(8,128)S(1)}, f32[8,512]{1,0:T(8,128)S(1)}) custom-call(bf16[64,1024]{1,0:T(8,128)(2,1)S(1)} %shard_map.91.q_ref, s32[2,128]{1,0:T(2,128)S(1)} %bitcast.32, bf16[1040,128]{1,0:T(8,128)(2,1)S(1)} %get-tuple-element.60.rest_0_, bf16[1040,128]{1,0:T(8,128)(2,1)S(1)} %collective-permute-done.12.rest_1_, ...), custom_call_target="tpu_custom_call" | custom-call | flops 402653184 | bytes 1209344 | tf_op jit(solution)/shard_map/pallas_call | solution.py:41
  52.8 2.6 %collective-permute-done.11.q_ref = bf16[64,1024]{1,0:T(8,128)(2,1)S(1)} collective-permute-done((bf16[64,1024]{1,0:T(8,128)(2,1)S(1)}, bf16[64,1024]{1,0:T(8,128)(2,1)S(1)}, u32[]{:S(2)}, u32[]{:S(2)}) %collective-permute-start.11) | collective-permute-done | bytes 131104 | tf_op jit(solution)/shard_map/ppermute | solution.py:303
  55.4 1.6 %shard_map.94 = (f32[128,512]{1,0:T(8,128)S(1)}, f32[8,512]{1,0:T(8,128)S(1)}) custom-call(bf16[64,1024]{1,0:T(8,128)(2,1)S(1)} %collective-permute-done.11.q_ref, s32[2,128]{1,0:T(2,128)S(1)} %bitcast.33, bf16[1040,128]{1,0:T(8,128)(2,1)S(1)} %get-tuple-element.60.rest_0_, bf16[1040,128]{1,0:T(8,128)(2,1)S(1)} %collective-permute-done.12.rest_1_, ...), custom_call_target="tpu_custom_call" | custom-call | flops 402653184 | bytes 1209344 | tf_op jit(solution)/shard_map/pallas_call | solution.py:41
  57.1 1.6 %shard_map.95 = (f32[128,512]{1,0:T(8,128)S(1)}, f32[8,512]{1,0:T(8,128)S(1)}) custom-call(bf16[64,1024]{1,0:T(8,128)(2,1)S(1)} %collective-permute-done.10.q_ref, s32[2,128]{1,0:T(2,128)S(1)} %bitcast.34, bf16[1040,128]{1,0:T(8,128)(2,1)S(1)} %get-tuple-element.60.rest_0_, bf16[1040,128]{1,0:T(8,128)(2,1)S(1)} %collective-permute-done.12.rest_1_, ...), custom_call_target="tpu_custom_call" | custom-call | flops 402653184 | bytes 1209344 | tf_op jit(solution)/shard_map/pallas_call | solution.py:41
  58.7 1.6 %shard_map.96 = (f32[128,512]{1,0:T(8,128)S(1)}, f32[8,512]{1,0:T(8,128)S(1)}) custom-call(bf16[64,1024]{1,0:T(8,128)(2,1)S(1)} %collective-permute-done.9.q_ref, s32[2,128]{1,0:T(2,128)S(1)} %bitcast.35, bf16[1040,128]{1,0:T(8,128)(2,1)S(1)} %get-tuple-element.60.rest_0_, bf16[1040,128]{1,0:T(8,128)(2,1)S(1)} %collective-permute-done.12.rest_1_, ...), custom_call_target="tpu_custom_call" | custom-call | flops 402653184 | bytes 1209344 | tf_op jit(solution)/shard_map/pallas_call | solution.py:41
  60.3 0.7 shard_map.97
  61.0 0.9 shard_map.98
  61.9 0.7 shard_map.99
  62.6 0.4 collective-permute-start.15
  63.0 0.6 collective-permute-start.16
  63.6 0.9 collective-permute-start.17
  64.5 0.6 shard_map.100
  65.2 4.6 %collective-permute-done.16.rest_1_ = s16[144,512]{1,0:T(8,128)(2,1)S(1)} collective-permute-done((s16[144,512]{1,0:T(8,128)(2,1)S(1)}, s16[144,512]{1,0:T(8,128)(2,1)S(1)}, u32[]{:S(2)}, u32[]{:S(2)}) %collective-permute-start.16) | collective-permute-done | bytes 147488 | tf_op jit(solution)/shard_map/ppermute | solution.py:303
  69.8 1.5 %collective-permute-done.17.rest_2_ = s16[144,512]{1,0:T(8,128)(2,1)S(1)} collective-permute-done((s16[144,512]{1,0:T(8,128)(2,1)S(1)}, s16[144,512]{1,0:T(8,128)(2,1)S(1)}, u32[]{:S(2)}, u32[]{:S(2)}) %collective-permute-start.17) | collective-permute-done | bytes 147488 | tf_op jit(solution)/shard_map/ppermute | solution.py:303
  71.3 0.2 shard_map.101.rest_0_
  71.5 9.9 %collective-permute-start.24 = (bf16[64,1024]{1,0:T(8,128)(2,1)S(1)}, bf16[64,1024]{1,0:T(8,128)(2,1)S(1)}, u32[]{:S(2)}, u32[]{:S(2)}) collective-permute-start(bf16[64,1024]{1,0:T(8,128)(2,1)S(1)} %shard_map.101.rest_0_), channel_id=1, source_target_pairs={{0,24},{2,26},{4,28},{6,30},{8,16},{10,18},{12,20},{14,22},{16,8},... | collective-permute-start | bytes 393224 | tf_op jit(solution)/shard_map/ppermute | solution.py:303
  81.4 0.6 collective-permute-start.22
  82.1 3.8 %collective-permute-done.24.rest_4_ = bf16[64,1024]{1,0:T(8,128)(2,1)S(1)} collective-permute-done((bf16[64,1024]{1,0:T(8,128)(2,1)S(1)}, bf16[64,1024]{1,0:T(8,128)(2,1)S(1)}, u32[]{:S(2)}, u32[]{:S(2)}) %collective-permute-start.24) | collective-permute-done | bytes 131104 | tf_op jit(solution)/shard_map/ppermute | solution.py:303
  85.8 0.5 collective-permute-start.25
  86.3 1.6 %collective-permute-start.18 = (bf16[64,1024]{1,0:T(8,128)(2,1)S(1)}, bf16[64,1024]{1,0:T(8,128)(2,1)S(1)}, u32[]{:S(2)}, u32[]{:S(2)}) collective-permute-start(bf16[64,1024]{1,0:T(8,128)(2,1)S(1)} %shard_map.101.rest_0_), channel_id=1, source_target_pairs={{0,4},{2,6},{4,0},{6,2},{8,12},{10,14},{12,8},{14,10},{16,20},{18,... | collective-permute-start | bytes 393224 | tf_op jit(solution)/shard_map/ppermute | solution.py:303
  87.8 2.3 %collective-permute-done.19.rest_4_ = bf16[64,1024]{1,0:T(8,128)(2,1)S(1)} collective-permute-done((bf16[64,1024]{1,0:T(8,128)(2,1)S(1)}, bf16[64,1024]{1,0:T(8,128)(2,1)S(1)}, u32[]{:S(2)}, u32[]{:S(2)}) %collective-permute-start.19) | collective-permute-done | bytes 131104 | tf_op jit(solution)/shard_map/ppermute | solution.py:303
  90.1 0.3 collective-permute-start.20
  90.4 1.8 %collective-permute-done.22.rest_0_ = bf16[64,1024]{1,0:T(8,128)(2,1)S(1)} collective-permute-done((bf16[64,1024]{1,0:T(8,128)(2,1)S(1)}, bf16[64,1024]{1,0:T(8,128)(2,1)S(1)}, u32[]{:S(2)}, u32[]{:S(2)}) %collective-permute-start.22) | collective-permute-done | bytes 131104 | tf_op jit(solution)/shard_map/ppermute | solution.py:303
  92.4 1.8 %collective-permute-done.18.rest_1_ = bf16[64,1024]{1,0:T(8,128)(2,1)S(1)} collective-permute-done((bf16[64,1024]{1,0:T(8,128)(2,1)S(1)}, bf16[64,1024]{1,0:T(8,128)(2,1)S(1)}, u32[]{:S(2)}, u32[]{:S(2)}) %collective-permute-start.18) | collective-permute-done | bytes 131104 | tf_op jit(solution)/shard_map/ppermute | solution.py:303
  94.2 2.1 %collective-permute-done.20.rest_5_ = bf16[64,1024]{1,0:T(8,128)(2,1)S(1)} collective-permute-done((bf16[64,1024]{1,0:T(8,128)(2,1)S(1)}, bf16[64,1024]{1,0:T(8,128)(2,1)S(1)}, u32[]{:S(2)}, u32[]{:S(2)}) %collective-permute-start.20) | collective-permute-done | bytes 131104 | tf_op jit(solution)/shard_map/ppermute | solution.py:303
  96.4 0.4 collective-permute-start.23
  96.9 5.5 %collective-permute-done.23.rest_1_ = bf16[64,1024]{1,0:T(8,128)(2,1)S(1)} collective-permute-done((bf16[64,1024]{1,0:T(8,128)(2,1)S(1)}, bf16[64,1024]{1,0:T(8,128)(2,1)S(1)}, u32[]{:S(2)}, u32[]{:S(2)}) %collective-permute-start.23) | collective-permute-done | bytes 131104 | tf_op jit(solution)/shard_map/ppermute | solution.py:303
  102.4 0.7 shard_map.102.before_ref
  103.2 0.5 collective-permute-done.27.rest_3_
  103.7 1.0 shard_map.103
  104.7 1.6 %collective-permute-start.28 = (s16[128,640]{1,0:T(8,128)(2,1)S(1)}, s16[128,640]{1,0:T(8,128)(2,1)S(1)}, u32[]{:S(2)}, u32[]{:S(2)}) collective-permute-start(s16[128,640]{1,0:T(8,128)(2,1)S(1)} %get-tuple-element.82), channel_id=1, source_target_pairs={{0,1},{1,0},{2,3},{3,2},{4,5},{5,4},{6,7},{7,6},{8,9},{9,8},{10,11... | collective-permute-start | bytes 491528 | tf_op jit(solution)/shard_map/ppermute | solution.py:417
  106.3 4.7 %collective-permute-done.28.got_ref = s16[128,640]{1,0:T(8,128)(2,1)S(1)} collective-permute-done((s16[128,640]{1,0:T(8,128)(2,1)S(1)}, s16[128,640]{1,0:T(8,128)(2,1)S(1)}, u32[]{:S(2)}, u32[]{:S(2)}) %collective-permute-start.28) | collective-permute-done | bytes 163872 | tf_op jit(solution)/shard_map/ppermute | solution.py:417
  111.1 0.8 shard_map.104
  (40 shorter events, 0.7 us)
Async XLA Ops:
  0.0 0.9 copy-start.1
  1.0 4.2 %copy-start.2 = (bf16[256,512]{1,0:T(8,128)(2,1)S(1)}, bf16[256,512]{1,0:T(8,128)(2,1)}, u32[]{:S(2)}) copy-start(bf16[256,512]{1,0:T(8,128)(2,1)} %text_ref.1) | copy-start | bytes 786436
  2.7 2.1 %collective-permute-start = (f32[128,1024]{1,0:T(8,128)S(1)}, f32[128,1024]{1,0:T(8,128)S(1)}, u32[]{:S(2)}, u32[]{:S(2)}) collective-permute-start(f32[128,1024]{1,0:T(8,128)S(1)} %get-tuple-element.45), channel_id=1, source_target_pairs={{0,2},{2,0},{4,6},{6,4},{8,10},{10,8},{12,14},{14,12},{16,18},{18,... | collective-permute-start | bytes 1572872 | tf_op jit(solution)/shard_map/ppermute | solution.py:303
  6.8 12.8 %copy-start.7 = (s32[256,2]{0,1:T(2,128)S(1)}, s32[256,2]{0,1:T(2,128)}, u32[]{:S(2)}) copy-start(s32[256,2]{0,1:T(2,128)} %param.13) | copy-start | bytes 6148
  6.9 12.8 %copy-start.3 = (bf16[512,512]{1,0:T(8,128)(2,1)S(1)}, bf16[512,512]{1,0:T(8,128)(2,1)}, u32[]{:S(2)}) copy-start(bf16[512,512]{1,0:T(8,128)(2,1)} %key_ref.1) | copy-start | bytes 1572868
  6.9 12.8 %copy-start.4 = (bf16[512,512]{1,0:T(8,128)(2,1)S(1)}, bf16[512,512]{1,0:T(8,128)(2,1)}, u32[]{:S(2)}) copy-start(bf16[512,512]{1,0:T(8,128)(2,1)} %value_ref.1) | copy-start | bytes 1572868
  6.9 2.0 %collective-permute-start.1 = (f32[128,1024]{1,0:T(8,128)S(1)}, f32[128,1024]{1,0:T(8,128)S(1)}, u32[]{:S(2)}, u32[]{:S(2)}) collective-permute-start(f32[128,1024]{1,0:T(8,128)S(1)} %get-tuple-element.49), channel_id=1, source_target_pairs={{0,2},{2,0},{4,6},{6,4},{8,10},{10,8},{12,14},{14,12},{16,18},{18,... | collective-permute-start | bytes 1572872 | tf_op jit(solution)/shard_map/ppermute | solution.py:303
  9.2 38.9 %copy-start.6 = (f32[128]{0:T(128)S(1)}, f32[128]{0:T(128)}, u32[]{:S(2)}) copy-start(f32[128]{0:T(128)} %param.10) | copy-start | bytes 1540
  9.2 42.0 %copy-start.5 = (s32[256]{0:T(256)S(1)}, s32[256]{0:T(256)}, u32[]{:S(2)}) copy-start(s32[256]{0:T(256)} %param.14) | copy-start | bytes 3076
  11.4 2.7 %collective-permute-start.2 = (f32[128,2048]{1,0:T(8,128)S(1)}, f32[128,2048]{1,0:T(8,128)S(1)}, u32[]{:S(2)}, u32[]{:S(2)}) collective-permute-start(f32[128,2048]{1,0:T(8,128)S(1)} %get-tuple-element.53), channel_id=1, source_target_pairs={{0,2},{2,0},{4,6},{6,4},{8,10},{10,8},{12,14},{14,12},{16,18},{18,... | collective-permute-start | bytes 3145736 | tf_op jit(solution)/shard_map/ppermute | solution.py:303
  14.7 19.5 %collective-permute-start.3 = (s16[64,2176]{1,0:T(8,128)(2,1)S(1)}, s16[64,2176]{1,0:T(8,128)(2,1)S(1)}, u32[]{:S(2)}, u32[]{:S(2)}) collective-permute-start(s16[64,2176]{1,0:T(8,128)(2,1)S(1)} %get-tuple-element.55), channel_id=1, source_target_pairs={{0,4},{2,6},{4,0},{6,2},{8,12},{10,14},{12,8},{14,10},{16,20},{18,... | collective-permute-start | bytes 835592 | tf_op jit(solution)/shard_map/ppermute | solution.py:303
  17.6 10.7 %collective-permute-start.7 = (s16[64,1152]{1,0:T(8,128)(2,1)S(1)}, s16[64,1152]{1,0:T(8,128)(2,1)S(1)}, u32[]{:S(2)}, u32[]{:S(2)}) collective-permute-start(s16[64,1152]{1,0:T(8,128)(2,1)S(1)} %get-tuple-element.46), channel_id=1, source_target_pairs={{0,4},{2,6},{4,0},{6,2},{8,12},{10,14},{12,8},{14,10},{16,20},{18,... | collective-permute-start | bytes 442376 | tf_op jit(solution)/shard_map/ppermute | solution.py:303
  17.6 15.2 %collective-permute-start.5 = (s16[64,1152]{1,0:T(8,128)(2,1)S(1)}, s16[64,1152]{1,0:T(8,128)(2,1)S(1)}, u32[]{:S(2)}, u32[]{:S(2)}) collective-permute-start(s16[64,1152]{1,0:T(8,128)(2,1)S(1)} %get-tuple-element.50), channel_id=1, source_target_pairs={{0,4},{2,6},{4,0},{6,2},{8,12},{10,14},{12,8},{14,10},{16,20},{18,... | collective-permute-start | bytes 442376 | tf_op jit(solution)/shard_map/ppermute | solution.py:303
  19.9 30.6 %collective-permute-start.12 = (bf16[1040,128]{1,0:T(8,128)(2,1)S(1)}, bf16[1040,128]{1,0:T(8,128)(2,1)S(1)}, u32[]{:S(2)}, u32[]{:S(2)}) collective-permute-start(bf16[1040,128]{1,0:T(8,128)(2,1)S(1)} %get-tuple-element.61), channel_id=1, source_target_pairs={{0,8},{2,10},{4,12},{6,14},{8,0},{10,2},{12,4},{14,6},{16,24},{18,... | collective-permute-start | bytes 798728 | tf_op jit(solution)/shard_map/ppermute | solution.py:303
  21.5 29.7 %collective-permute-start.13 = (bf16[1040,128]{1,0:T(8,128)(2,1)S(1)}, bf16[1040,128]{1,0:T(8,128)(2,1)S(1)}, u32[]{:S(2)}, u32[]{:S(2)}) collective-permute-start(bf16[1040,128]{1,0:T(8,128)(2,1)S(1)} %get-tuple-element.62), channel_id=1, source_target_pairs={{0,24},{2,26},{4,28},{6,30},{8,16},{10,18},{12,20},{14,22},{16,8},... | collective-permute-start | bytes 798728 | tf_op jit(solution)/shard_map/ppermute | solution.py:303
  28.7 11.5 %collective-permute-start.8 = (s16[64,1152]{1,0:T(8,128)(2,1)S(1)}, s16[64,1152]{1,0:T(8,128)(2,1)S(1)}, u32[]{:S(2)}, u32[]{:S(2)}) collective-permute-start(s16[64,1152]{1,0:T(8,128)(2,1)S(1)} %shard_map.90), channel_id=1, source_target_pairs={{0,24},{2,26},{4,28},{6,30},{8,16},{10,18},{12,20},{14,22},{16,8},... | collective-permute-start | bytes 442376 | tf_op jit(solution)/shard_map/ppermute | solution.py:303
  33.3 14.8 %collective-permute-start.6 = (s16[64,1152]{1,0:T(8,128)(2,1)S(1)}, s16[64,1152]{1,0:T(8,128)(2,1)S(1)}, u32[]{:S(2)}, u32[]{:S(2)}) collective-permute-start(s16[64,1152]{1,0:T(8,128)(2,1)S(1)} %shard_map.89), channel_id=1, source_target_pairs={{0,16},{2,18},{4,20},{6,22},{8,24},{10,26},{12,28},{14,30},{16,0},... | collective-permute-start | bytes 442376 | tf_op jit(solution)/shard_map/ppermute | solution.py:303
  34.7 13.4 %collective-permute-start.4 = (s16[64,1152]{1,0:T(8,128)(2,1)S(1)}, s16[64,1152]{1,0:T(8,128)(2,1)S(1)}, u32[]{:S(2)}, u32[]{:S(2)}) collective-permute-start(s16[64,1152]{1,0:T(8,128)(2,1)S(1)} %get-tuple-element.57), channel_id=1, source_target_pairs={{0,8},{2,10},{4,12},{6,14},{8,0},{10,2},{12,4},{14,6},{16,24},{18,... | collective-permute-start | bytes 442376 | tf_op jit(solution)/shard_map/ppermute | solution.py:303
  40.2 20.2 %collective-permute-start.14 = (bf16[1040,128]{1,0:T(8,128)(2,1)S(1)}, bf16[1040,128]{1,0:T(8,128)(2,1)S(1)}, u32[]{:S(2)}, u32[]{:S(2)}) collective-permute-start(bf16[1040,128]{1,0:T(8,128)(2,1)S(1)} %get-tuple-element.75), channel_id=1, source_target_pairs={{0,16},{2,18},{4,20},{6,22},{8,24},{10,26},{12,28},{14,30},{16,0},... | collective-permute-start | bytes 798728 | tf_op jit(solution)/shard_map/ppermute | solution.py:303
  49.0 6.4 %collective-permute-start.11 = (bf16[64,1024]{1,0:T(8,128)(2,1)S(1)}, bf16[64,1024]{1,0:T(8,128)(2,1)S(1)}, u32[]{:S(2)}, u32[]{:S(2)}) collective-permute-start(bf16[64,1024]{1,0:T(8,128)(2,1)S(1)} %shard_map.91.q_ref), channel_id=1, source_target_pairs={{0,4},{2,6},{4,0},{6,2},{8,12},{10,14},{12,8},{14,10},{16,20},{18,... | collective-permute-start | bytes 393224 | tf_op jit(solution)/shard_map/ppermute | solution.py:303
  49.6 7.5 %collective-permute-start.10 = (bf16[64,1024]{1,0:T(8,128)(2,1)S(1)}, bf16[64,1024]{1,0:T(8,128)(2,1)S(1)}, u32[]{:S(2)}, u32[]{:S(2)}) collective-permute-start(bf16[64,1024]{1,0:T(8,128)(2,1)S(1)} %shard_map.91.q_ref), channel_id=1, source_target_pairs={{0,6},{2,4},{4,2},{6,0},{8,14},{10,12},{12,10},{14,8},{16,22},{18,... | collective-permute-start | bytes 393224 | tf_op jit(solution)/shard_map/ppermute | solution.py:303
  50.5 8.2 %collective-permute-start.9 = (bf16[64,1024]{1,0:T(8,128)(2,1)S(1)}, bf16[64,1024]{1,0:T(8,128)(2,1)S(1)}, u32[]{:S(2)}, u32[]{:S(2)}) collective-permute-start(bf16[64,1024]{1,0:T(8,128)(2,1)S(1)} %shard_map.91.q_ref), channel_id=1, source_target_pairs={{0,2},{2,0},{4,6},{6,4},{8,10},{10,8},{12,14},{14,12},{16,18},{18,... | collective-permute-start | bytes 393224 | tf_op jit(solution)/shard_map/ppermute | solution.py:303
  60.3 42.1 %copy-start = (bf16[4096,512]{1,0:T(8,128)(2,1)S(1)}, bf16[4096,512]{1,0:T(8,128)(2,1)}, u32[]{:S(2)}) copy-start(bf16[4096,512]{1,0:T(8,128)(2,1)} %w_ref.3) | copy-start | bytes 12582916
  62.6 2.6 %collective-permute-start.15 = (s16[144,512]{1,0:T(8,128)(2,1)S(1)}, s16[144,512]{1,0:T(8,128)(2,1)S(1)}, u32[]{:S(2)}, u32[]{:S(2)}) collective-permute-start(s16[144,512]{1,0:T(8,128)(2,1)S(1)} %shard_map.99), channel_id=1, source_target_pairs={{0,2},{2,0},{4,6},{6,4},{8,10},{10,8},{12,14},{14,12},{16,18},{18,... | collective-permute-start | bytes 442376 | tf_op jit(solution)/shard_map/ppermute | solution.py:303
  63.0 6.7 %collective-permute-start.16 = (s16[144,512]{1,0:T(8,128)(2,1)S(1)}, s16[144,512]{1,0:T(8,128)(2,1)S(1)}, u32[]{:S(2)}, u32[]{:S(2)}) collective-permute-start(s16[144,512]{1,0:T(8,128)(2,1)S(1)} %shard_map.97), channel_id=1, source_target_pairs={{0,4},{2,6},{4,0},{6,2},{8,12},{10,14},{12,8},{14,10},{16,20},{18,... | collective-permute-start | bytes 442376 | tf_op jit(solution)/shard_map/ppermute | solution.py:303
  63.6 7.7 %collective-permute-start.17 = (s16[144,512]{1,0:T(8,128)(2,1)S(1)}, s16[144,512]{1,0:T(8,128)(2,1)S(1)}, u32[]{:S(2)}, u32[]{:S(2)}) collective-permute-start(s16[144,512]{1,0:T(8,128)(2,1)S(1)} %shard_map.98), channel_id=1, source_target_pairs={{0,6},{2,4},{4,2},{6,0},{8,14},{10,12},{12,10},{14,8},{16,22},{18,... | collective-permute-start | bytes 442376 | tf_op jit(solution)/shard_map/ppermute | solution.py:303
  71.5 14.3 %collective-permute-start.24 = (bf16[64,1024]{1,0:T(8,128)(2,1)S(1)}, bf16[64,1024]{1,0:T(8,128)(2,1)S(1)}, u32[]{:S(2)}, u32[]{:S(2)}) collective-permute-start(bf16[64,1024]{1,0:T(8,128)(2,1)S(1)} %shard_map.101.rest_0_), channel_id=1, source_target_pairs={{0,24},{2,26},{4,28},{6,30},{8,16},{10,18},{12,20},{14,22},{16,8},... | collective-permute-start | bytes 393224 | tf_op jit(solution)/shard_map/ppermute | solution.py:303
  81.4 8.7 %collective-permute-start.19 = (bf16[64,1024]{1,0:T(8,128)(2,1)S(1)}, bf16[64,1024]{1,0:T(8,128)(2,1)S(1)}, u32[]{:S(2)}, u32[]{:S(2)}) collective-permute-start(bf16[64,1024]{1,0:T(8,128)(2,1)S(1)} %shard_map.101.rest_0_), channel_id=1, source_target_pairs={{0,8},{2,10},{4,12},{6,14},{8,0},{10,2},{12,4},{14,6},{16,24},{18,... | collective-permute-start | bytes 393224 | tf_op jit(solution)/shard_map/ppermute | solution.py:303
  81.4 10.8 %collective-permute-start.22 = (bf16[64,1024]{1,0:T(8,128)(2,1)S(1)}, bf16[64,1024]{1,0:T(8,128)(2,1)S(1)}, u32[]{:S(2)}, u32[]{:S(2)}) collective-permute-start(bf16[64,1024]{1,0:T(8,128)(2,1)S(1)} %shard_map.101.rest_0_), channel_id=1, source_target_pairs={{0,16},{2,18},{4,20},{6,22},{8,24},{10,26},{12,28},{14,30},{16,0},... | collective-permute-start | bytes 393224 | tf_op jit(solution)/shard_map/ppermute | solution.py:303
  85.8 6.4 %collective-permute-start.25 = (bf16[64,1024]{1,0:T(8,128)(2,1)S(1)}, bf16[64,1024]{1,0:T(8,128)(2,1)S(1)}, u32[]{:S(2)}, u32[]{:S(2)}) collective-permute-start(bf16[64,1024]{1,0:T(8,128)(2,1)S(1)} %collective-permute-done.24.rest_4_), channel_id=1, source_target_pairs={{0,4},{2,6},{4,0},{6,2},{8,12},{10,14},{12,8},{14,10},{16,20},{18,... | collective-permute-start | bytes 393224 | tf_op jit(solution)/shard_map/ppermute | solution.py:303
  86.3 7.9 %collective-permute-start.18 = (bf16[64,1024]{1,0:T(8,128)(2,1)S(1)}, bf16[64,1024]{1,0:T(8,128)(2,1)S(1)}, u32[]{:S(2)}, u32[]{:S(2)}) collective-permute-start(bf16[64,1024]{1,0:T(8,128)(2,1)S(1)} %shard_map.101.rest_0_), channel_id=1, source_target_pairs={{0,4},{2,6},{4,0},{6,2},{8,12},{10,14},{12,8},{14,10},{16,20},{18,... | collective-permute-start | bytes 393224 | tf_op jit(solution)/shard_map/ppermute | solution.py:303
  90.1 6.2 %collective-permute-start.20 = (bf16[64,1024]{1,0:T(8,128)(2,1)S(1)}, bf16[64,1024]{1,0:T(8,128)(2,1)S(1)}, u32[]{:S(2)}, u32[]{:S(2)}) collective-permute-start(bf16[64,1024]{1,0:T(8,128)(2,1)S(1)} %collective-permute-done.19.rest_4_), channel_id=1, source_target_pairs={{0,4},{2,6},{4,0},{6,2},{8,12},{10,14},{12,8},{14,10},{16,20},{18,... | collective-permute-start | bytes 393224 | tf_op jit(solution)/shard_map/ppermute | solution.py:303
  92.3 10.1 %collective-permute-start.26 = (bf16[3,64,1024]{2,1,0:T(8,128)(2,1)S(1)}, bf16[3,64,1024]{2,1,0:T(8,128)(2,1)S(1)}, u32[]{:S(2)}, u32[]{:S(2)}) collective-permute-start(bf16[3,64,1024]{2,1,0:T(8,128)(2,1)S(1)} %pad_maximum_fusion.1), channel_id=1, source_target_pairs={{0,2},{2,0},{4,6},{6,4},{8,10},{10,8},{12,14},{14,12},{16,18},{18,... | collective-permute-start | bytes 1179656 | tf_op jit(solution)/shard_map/ppermute | solution.py:303
  96.4 6.0 %collective-permute-start.21 = (bf16[4,64,1024]{2,1,0:T(8,128)(2,1)S(1)}, bf16[4,64,1024]{2,1,0:T(8,128)(2,1)S(1)}, u32[]{:S(2)}, u32[]{:S(2)}) collective-permute-start(bf16[4,64,1024]{2,1,0:T(8,128)(2,1)S(1)} %pad_maximum_fusion), channel_id=1, source_target_pairs={{0,2},{2,0},{4,6},{6,4},{8,10},{10,8},{12,14},{14,12},{16,18},{18,... | collective-permute-start | bytes 1572872 | tf_op jit(solution)/shard_map/ppermute | solution.py:303
  96.4 5.9 %collective-permute-start.23 = (bf16[64,1024]{1,0:T(8,128)(2,1)S(1)}, bf16[64,1024]{1,0:T(8,128)(2,1)S(1)}, u32[]{:S(2)}, u32[]{:S(2)}) collective-permute-start(bf16[64,1024]{1,0:T(8,128)(2,1)S(1)} %collective-permute-done.22.rest_0_), channel_id=1, source_target_pairs={{0,4},{2,6},{4,0},{6,2},{8,12},{10,14},{12,8},{14,10},{16,20},{18,... | collective-permute-start | bytes 393224 | tf_op jit(solution)/shard_map/ppermute | solution.py:303
  102.3 1.3 %collective-permute-start.27 = (bf16[64,1024]{1,0:T(8,128)(2,1)S(1)}, bf16[64,1024]{1,0:T(8,128)(2,1)S(1)}, u32[]{:S(2)}, u32[]{:S(2)}) collective-permute-start(bf16[64,1024]{1,0:T(8,128)(2,1)S(1)} %collective-permute-done.23.rest_1_), channel_id=1, source_target_pairs={{0,2},{2,0},{4,6},{6,4},{8,10},{10,8},{12,14},{14,12},{16,18},{18,... | collective-permute-start | bytes 393224 | tf_op jit(solution)/shard_map/ppermute | solution.py:303
  104.7 6.3 %collective-permute-start.28 = (s16[128,640]{1,0:T(8,128)(2,1)S(1)}, s16[128,640]{1,0:T(8,128)(2,1)S(1)}, u32[]{:S(2)}, u32[]{:S(2)}) collective-permute-start(s16[128,640]{1,0:T(8,128)(2,1)S(1)} %get-tuple-element.82), channel_id=1, source_target_pairs={{0,1},{1,0},{2,3},{3,2},{4,5},{5,4},{6,7},{7,6},{8,9},{9,8},{10,11... | collective-permute-start | bytes 491528 | tf_op jit(solution)/shard_map/ppermute | solution.py:417
where the time goes:
time: 112 us
  waiting for transfers between devices  44.8 us (40%)
  starting transfers between devices  44.1 us (39%)
  Pallas kernels  21.5 us (19%)
    ppermute x28, starting transfers between devices, swap(): return lax.ppermute(value, 'ctx', [(i, i ^ bits) for i in range(ctx)])  42.5 us
    ppermute x28, waiting for transfers between devices, swap(): return lax.ppermute(value, 'ctx', [(i, i ^ bits) for i in range(ctx)])  40 us
    pallas_call x23, Pallas kernels, call(): pl.pallas_call(kernel, out_shape=out_shape, in_specs=specs or [VM] * len(...  21.5 us
    ppermute x1, waiting for transfers between devices, fast_shards(): got = lax.ppermute(code, ('head', 'tp'), [(0, 1), (1, 0)])  4.74 us
  transfers between devices with their start and end apart: 29, of which 17 were waited for; matrix products, arithmetic and copies ran while one was open for 0% of the time, Pallas kernels for 9%

commit v1 on v0

--- a/solution.py
+++ b/solution.py
@@ -16,8 +16,6 @@
 NO_SUM = -32000.0
 VM = pl.BlockSpec(memory_space=pltpu.VMEM)
 HB = pl.BlockSpec(memory_space=pltpu.HBM)
-
-PROJECT_GRANT = 16
 
 
 class Position:
@@ -63,67 +61,94 @@
     scale = jnp.exp2(-power) * CODE_TOP
     for h, part in enumerate(parts):
         code = jnp.round(part * scale[:, h : h + 1])
-        code_ref[:, h * LANES : (h + 1) * LANES] = code.astype(I32).astype(I16)
-    code_ref[:, len(parts) * LANES :] = power.astype(I32).astype(I16)
-
-
-def scales_of(code_ref):
-    width = code_ref.shape[1] - LANES
-    return jnp.exp2(code_ref[:, width:].astype(I32).astype(F32)) * (1.0 / CODE_TOP)
+        code_ref[h * rows : (h + 1) * rows, :] = code.astype(I32).astype(I16)
+    square = jnp.concatenate([power, jnp.zeros((LANES - rows, LANES), F32)], axis=0)
+    code_ref[len(parts) * rows :, :] = jnp.transpose(square)[:TAIL].astype(I32).astype(I16)
+
+
+def scales_of(code_ref, rows):
+    lines = code_ref[code_ref.shape[0] - TAIL :, :].astype(I32).astype(F32)
+    square = jnp.concatenate([lines, jnp.zeros((LANES - TAIL, LANES), F32)], axis=0)
+    return jnp.exp2(jnp.transpose(square)[:rows]) * (1.0 / CODE_TOP)
 
 
 def decode_head(code_ref, scales, h):
-    return code_ref[:, h * LANES : (h + 1) * LANES].astype(I32).astype(F32) * scales[:, h : h + 1]
-
-
-def pack_kernel(groups, key_ref, value_ref, mask_ref, *outs):
-    keys = key_ref.shape[0]
-    for d in range(groups):
-        at = pl.multiple_of((ids[2] ^ d) * LANES, LANES)
-        outs[d][:keys, :] = key_ref[:, pl.ds(at, LANES)]
-        outs[d][keys : 2 * keys, :] = jnp.concatenate(
-            [
-                jnp.transpose(value_ref[pl.ds(c * LANES, LANES), pl.ds(at, LANES)])
-                for c in range(keys // LANES)
-            ],
-            axis=0,
-        )
-        outs[d][2 * keys :, :] = mask_ref[...]
-
-
-def project_kernel(ds, x_ref, w_hbm, send_ref, keep_ref, w_buf, sems):
+    rows = scales.shape[0]
+    return code_ref[h * rows : (h + 1) * rows, :].astype(I32).astype(F32) * scales[:, h : h + 1]
+
+
+def begin_kernel(ds, x_hbm, w_hbm, key_hbm, value_hbm, mask_hbm, *rest):
+    groups = len(ds)
+    first, other, packs = rest[:2], rest[2:4], rest[4 : 4 + groups]
+    x_ref, w_buf, key_ref, value_ref, mask_ref, sems = rest[4 + groups :]
     half = x_ref.shape[0] // 2
     width = w_buf.shape[2]
-    copies = []
-    for i, d in enumerate(ds):
-        at = pl.multiple_of((ids[2] ^ d) * width, width)
-        copies.append(pltpu.make_async_copy(w_hbm.at[:, pl.ds(at, width)], w_buf.at[i], sems.at[i]))
-        copies[-1].start()
+    keys = key_ref.shape[0]
+
+    def fetch(source, target, n):
+        copy = pltpu.make_async_copy(source, target, sems.at[n])
+        copy.start()
+        return copy
+
+    def weights(i):
+        at = pl.multiple_of((ids[2] ^ ds[i]) * width, width)
+        return fetch(w_hbm.at[:, pl.ds(at, width)], w_buf.at[i], i)
+
+    text = fetch(x_hbm, x_ref, groups)
+    copies = [weights(0)]
+    tokens = [fetch(key_hbm, key_ref, groups + 1), fetch(value_hbm, value_ref, groups + 2)]
+    tokens.append(fetch(mask_hbm, mask_ref, groups + 3))
+    copies += [weights(i) for i in range(1, groups)]
     peer = pl.multiple_of((1 - ids[0]) * half, half)
     mine = pl.multiple_of(ids[0] * half, half)
-    for i in range(len(ds)):
+
+    def project(i, send_ref, keep_ref, at):
         copies[i].wait()
-        cols = slice(i * width, (i + 1) * width)
+        cols = slice(at * width, (at + 1) * width)
         w = w_buf[i]
         send_ref[:, cols] = jnp.dot(x_ref[pl.ds(peer, half), :], w, preferred_element_type=F32)
         keep_ref[:, cols] = jnp.dot(x_ref[pl.ds(mine, half), :], w, preferred_element_type=F32)
 
-
-def split_x_kernel(keep_ref, got_ref, code_ref, own_ref):
+    text.wait()
+    project(0, *first, 0)
+    for copy in tokens:
+        copy.wait()
+    line = lax.broadcasted_iota(I32, (TAIL, LANES), 0)
+    tail = jnp.zeros((TAIL, LANES), F32)
+    segments, text_rows = mask_ref.shape
+    for s in range(segments):
+        for j in range(text_rows // LANES):
+            row = mask_ref[s : s + 1, j * LANES : (j + 1) * LANES]
+            here = line == s * (text_rows // LANES) + j
+            tail = jnp.where(here & (row == 1), F32(1.0), tail)
+    for d in range(groups):
+        at = pl.multiple_of((ids[2] ^ d) * LANES, LANES)
+        packs[d][:keys, :] = key_ref[:, pl.ds(at, LANES)]
+        for c in range(keys // LANES):
+            block = value_ref[c * LANES : (c + 1) * LANES, pl.ds(at, LANES)]
+            packs[d][keys + c * LANES : keys + (c + 1) * LANES, :] = jnp.transpose(block)
+        packs[d][2 * keys :, :] = tail.astype(BF16)
+    for i in range(1, groups):
+        project(i, *other, i - 1)
+
+
+def split_x_kernel(first, keep_ref, got_ref, code_ref, own_ref):
     half, width = own_ref.shape
+    first *= width
     mine = pl.multiple_of(ids[1] * half, half)
     peer = pl.multiple_of((1 - ids[1]) * half, half)
     parts = []
     for h in range(width // LANES):
-        cols = slice(h * LANES, (h + 1) * LANES)
+        cols = slice(first + h * LANES, first + (h + 1) * LANES)
         parts.append(keep_ref[pl.ds(peer, half), cols] + got_ref[pl.ds(peer, half), cols])
     encode_heads(parts, code_ref)
-    own_ref[...] = keep_ref[pl.ds(mine, half), :] + got_ref[pl.ds(mine, half), :]
+    cols = slice(first, first + width)
+    own_ref[...] = keep_ref[pl.ds(mine, half), cols] + got_ref[pl.ds(mine, half), cols]
 
 
 def split_z_kernel(ds, own_ref, got_ref, *outs):
     heads = own_ref.shape[1] // len(ds) // LANES
-    scales = scales_of(got_ref)
+    scales = scales_of(got_ref, own_ref.shape[0])
     for i, d in enumerate(ds):
         parts = []
         for h in range(i * heads, (i + 1) * heads):
@@ -138,7 +163,7 @@
 def norm_kernel(own_ref, gain_ref, *rest):
     got, out_ref = rest[:-1], rest[-1]
     gain = gain_ref[...]
-    scales = [scales_of(g) for g in got]
+    scales = [scales_of(g, own_ref.shape[0]) for g in got]
     for h in range(out_ref.shape[1] // LANES):
         cols = slice(h * LANES, (h + 1) * LANES)
         total = own_ref[:, cols]
@@ -249,7 +274,8 @@
     total = None
     for d, row_blocks in zip(ds, blocks):
         left = jnp.concatenate([b[...] for b in row_blocks], axis=0)
-        base = pl.multiple_of((ids[2] ^ d) * width, width)
+        groups = w_ref.shape[0] // width
+        base = pl.multiple_of(lax.rem(ids[2] + groups - d, groups) * width, width)
         part = jnp.dot(left, w_ref[pl.ds(base, width), :], preferred_element_type=F32)
         total = part if total is None else total + part
     return total
@@ -272,17 +298,18 @@
         send_buf[pl.ds(at, rows), :] = jnp.where(swap_core, other, own)
         keep_ref[pl.ds(at, rows), :] = jnp.where(swap_core, own, other)
     width = send_buf.shape[1]
-    encode_heads([send_buf[:, h * LANES : (h + 1) * LANES] for h in range(width // LANES)], code_ref)
+    send = send_buf[...]
+    power = power_of(jnp.max(jnp.abs(send), axis=0, keepdims=True))
+    code_ref[: 2 * rows, :] = jnp.round(send * (jnp.exp2(-power) * CODE_TOP)).astype(I32).astype(I16)
+    code_ref[2 * rows :, :] = jnp.broadcast_to(power, (TAIL, width)).astype(I32).astype(I16)
 
 
 def finish_kernel(keep_ref, got_ref, text_ref, out_ref):
-    rows, width = out_ref.shape
+    rows = out_ref.shape[0]
     at = pl.multiple_of(ids[3] * rows, rows)
-    scales = scales_of(got_ref)
-    for h in range(width // LANES):
-        cols = slice(h * LANES, (h + 1) * LANES)
-        total = keep_ref[:, cols] + decode_head(got_ref, scales, h)
-        out_ref[:, cols] = (text_ref[pl.ds(at, rows), cols].astype(F32) + total).astype(BF16)
+    scale = jnp.exp2(got_ref[rows:, :].astype(I32).astype(F32)[:1]) * (1.0 / CODE_TOP)
+    total = keep_ref[...] + got_ref[:rows, :].astype(I32).astype(F32) * scale
+    out_ref[...] = (text_ref[pl.ds(at, rows), :].astype(F32) + total).astype(BF16)
 
 
 def fast_shards(text_states, q_weight, q_gain, key_cache, value_cache, block_mask, lengths, o_weight):
@@ -302,46 +329,49 @@
     def swap(value, bits):
         return lax.ppermute(value, "ctx", [(i, i ^ bits) for i in range(ctx)])
 
+    def turn(value, shift):
+        return lax.ppermute(value, "ctx", [(i, (i + shift) % ctx) for i in range(ctx)])
+
     def after(value, *others):
         return lax.optimization_barrier((value, *others))[0]
 
-    lines = segments * text_rows // LANES
-    mask_rows = jnp.pad(block_mask.T.astype(BF16).reshape(lines, LANES), ((0, TAIL - lines), (0, 0)))
-    packs = call(
-        functools.partial(pack_kernel, groups),
-        (struct((2 * keys + TAIL, LANES), BF16),) * groups,
-        (key_cache, value_cache, mask_rows),
+    in_hbm = functools.partial(pltpu.with_memory_space_constraint, memory_space=pltpu.HBM)
+    order = list(range(groups - 1, -1, -1))
+    chunks = [groups - 1, *[d for d in range(1, groups - 1)], 0]
+    parts = [struct((half, width), F32)] * 2 + [struct((half, (groups - 1) * width), F32)] * 2
+    sent, kept, sent_more, kept_more, *packs = call(
+        functools.partial(begin_kernel, chunks),
+        (*parts, *[struct((2 * keys + TAIL, LANES), BF16)] * groups),
+        (in_hbm(text_states), in_hbm(q_weight), in_hbm(key_cache), in_hbm(value_cache), in_hbm(block_mask.T)),
+        flops=2 * text_rows * depth * columns,
+        specs=[HB] * 5,
+        scratch=[
+            pltpu.VMEM(text_states.shape, BF16),
+            pltpu.VMEM((groups, depth, width), BF16),
+            pltpu.VMEM(key_cache.shape, BF16),
+            pltpu.VMEM(value_cache.shape, BF16),
+            pltpu.VMEM((segments, text_rows), I32),
+            pltpu.SemaphoreType.DMA((groups + 4,)),
+        ],
     )
     packs = [packs[0]] + [swap(packs[d], 4 * d) for d in range(1, groups)]
-
-    order = list(range(groups - 1, -1, -1))
-    chunks = [[d] for d in order[: groups // 2]] + [order[groups // 2 :]]
+    halves = (kept, swap(sent, 1))
+    more = (kept_more, swap(sent_more, 1))
+
     sums = {}
-    text = text_states
-    weight = pltpu.with_memory_space_constraint(q_weight, pltpu.HBM)
-    for ds in chunks:
-        wide = len(ds) * width
-        part = struct((half, wide), F32)
-        sent, kept = call(
-            functools.partial(project_kernel, ds),
-            (part, part),
-            (text, weight),
-            flops=2 * text_rows * depth * wide,
-            specs=[VM, HB],
-            scratch=[pltpu.VMEM((len(ds), depth, width), BF16), pltpu.SemaphoreType.DMA((len(ds),))],
-            grant=PROJECT_GRANT,
-        )
-        got = swap(sent, 1)
-        code, own = call(split_x_kernel, (struct((rows, wide + LANES), I16), struct((rows, wide), F32)), (kept, got))
-        text = after(text_states, code)
+    for n, d in enumerate(chunks):
+        code, own = call(
+            functools.partial(split_x_kernel, max(n - 1, 0)),
+            (struct((pairs + TAIL, LANES), I16), struct((rows, width), F32)),
+            more if n else halves,
+        )
         got = swap(code, 2)
-        outs = call(
-            functools.partial(split_z_kernel, ds),
-            tuple(struct((rows, width + LANES), I16) if d else struct((rows, width), F32) for d in ds),
+        (out,) = call(
+            functools.partial(split_z_kernel, [d]),
+            (struct((pairs + TAIL, LANES), I16) if d else struct((rows, width), F32),),
             (own, got),
         )
-        for d, out in zip(ds, outs):
-            sums[d] = swap(out, 4 * d) if d else out
+        sums[d] = swap(out, 4 * d) if d else out
     normed = call(
         norm_kernel,
         struct((rows, width), BF16),
@@ -352,9 +382,8 @@
     last = groups // 2
     first = [d for d in order[::-1] if d != last]
     queries = {t: swap(normed, t) if t else normed for t in range(4)}
-    turns = (0, 2, 3, 1)
     states, previous = {}, ()
-    for rel in turns:
+    for rel in range(4):
         states[rel] = call(
             functools.partial(attend_kernel, first, heads, segments, rel, True, False),
             (struct((LANES, pairs), F32), struct((8, pairs), F32)),
@@ -363,7 +392,7 @@
         )
         previous = states[rel]
     outs = {}
-    for rel in turns[1:] + turns[:1]:
+    for rel in (2, 3, 1, 0):
         if rel:
             shape = struct((LANES + TAIL, pairs), I16)
         else:
@@ -380,7 +409,7 @@
         functools.partial(merge_kernel, heads), struct((rows, width), BF16), (*outs[0], outs[1], outs[2], outs[3])
     )
 
-    column = {d: swap(attended, 4 * d) if d else attended for d in order}
+    column = {d: turn(attended, 4 * d) if d else attended for d in order}
     beside = {d: swap(column[d], 2) for d in range(groups)}
     early, late = list(range(groups // 2)), list(range(groups // 2, groups))
     tail_d = late[0]
@@ -409,7 +438,7 @@
     )
     kept, code = call(
         functools.partial(output_last_kernel, late),
-        (struct((half, out_cols), F32), struct((half, out_cols + LANES), I16)),
+        (struct((half, out_cols), F32), struct((half + TAIL, out_cols), I16)),
         (o_weight, before, *[b for d in late for b in blocks[d]]),
         flops=2 * text_rows * width * len(late) * out_cols,
         scratch=[pltpu.VMEM((half, out_cols), F32)],
@@ -528,8 +557,7 @@
             args[2].shape[0] == LANES
             and halves == 2
             and text_rows == 2 * LANES
-            and groups > 1
-            and groups & (groups - 1) == 0
+            and groups == 4
             and ctx == 4 * groups
             and args[1].shape[1] % (groups * LANES) == 0
             and args[1].shape[1] // groups <= LANES * LANES

time: 112 us -> 103 us (0.920)
  starting transfers between devices: 44.1 us -> 32.4 us
  waiting for transfers between devices: 44.8 us -> 50.8 us
  Pallas kernels: 21.5 us -> 19.3 us
    ppermute x28 -> x25, starting transfers between devices: 42.5 us -> 26.8 us  [swap(): return lax.ppermute(value, 'ctx', [(i, i ^ bits) for i in range(ctx)])]
    ppermute x0 -> x3, waiting for transfers between devices: none -> 7.28 us  [turn(): lax.ppermute(value, 'ctx', [(i, (i + shift) % ctx) for i in range(ctx)])]
    ppermute x0 -> x3, starting transfers between devices: none -> 4.03 us  [turn(): lax.ppermute(value, 'ctx', [(i, (i + shift) % ctx) for i in range(ctx)])]
    pallas_call x23 -> x22, Pallas kernels: 21.5 us -> 19.3 us  [call(): pl.pallas_call(kernel, out_shape=out_shape, in_specs=specs or [VM] * len(...]
    ppermute x28 -> x25, waiting for transfers between devices: 40 us -> 39.1 us  [swap(): return lax.ppermute(value, 'ctx', [(i, i ^ bits) for i in range(ctx)])]
  transfers between devices with their start and end apart: 29 -> 29, of which waited for: 17 -> 15; matrix products, arithmetic and copies ran while one was open for 0% -> 0% of each run, Pallas kernels for 9% -> 12%
where the time goes in v1:
time: 103 us
  waiting for transfers between devices  50.8 us (49%)
  starting transfers between devices  32.4 us (31%)
  Pallas kernels  19.3 us (19%)
    ppermute x25, waiting for transfers between devices, swap(): return lax.ppermute(value, 'ctx', [(i, i ^ bits) for i in range(ctx)])  39.1 us
    ppermute x25, starting transfers between devices, swap(): return lax.ppermute(value, 'ctx', [(i, i ^ bits) for i in range(ctx)])  26.8 us
    pallas_call x22, Pallas kernels, call(): pl.pallas_call(kernel, out_shape=out_shape, in_specs=specs or [VM] * len(...  19.3 us
    ppermute x3, waiting for transfers between devices, turn(): lax.ppermute(value, 'ctx', [(i, (i + shift) % ctx) for i in range(ctx)])  7.28 us
    ppermute x1, waiting for transfers between devices, fast_shards(): got = lax.ppermute(code, ('head', 'tp'), [(0, 1), (1, 0)])  4.39 us
    ppermute x3, starting transfers between devices, turn(): lax.ppermute(value, 'ctx', [(i, (i + shift) % ctx) for i in range(ctx)])  4.03 us
  transfers between devices with their start and end apart: 29, of which 15 were waited for; matrix products, arithmetic and copies ran while one was open for 0% of the time, Pallas kernels for 12%

profile of v1, /device:TPU:0, one launch (start us, length us, event | category | flops | bytes accessed | tf_op | source)
XLA Modules:
  0.0 102.9 jit_solution(9029072842782665629)
XLA Ops:
  0.0 3.4 %shard_map.82 = (f32[128,1024]{1,0:T(8,128)S(1)}, f32[128,1024]{1,0:T(8,128)S(1)}, f32[128,3072]{1,0:T(8,128)S(1)}, f32[128,3072]{1,0:T(8,128)S(1)}, bf16[1040,1...) custom-call(bf16[256,512]{1,0:T(8,128)(2,1)} %text_ref.1, ...), custom_call_target="tpu_custom_call" | custom-call | flops 1073741824 | bytes 10766336 | tf_op jit(solution)/shard_map/pallas_call | solution.py:39
  3.4 0.6 collective-permute-start
  4.0 0.1 collective-permute-start.6
  4.1 3.7 %collective-permute-done.6.got_ref = f32[128,1024]{1,0:T(8,128)S(1)} collective-permute-done((f32[128,1024]{1,0:T(8,128)S(1)}, f32[128,1024]{1,0:T(8,128)S(1)}, u32[]{:S(2)}, u32[]{:S(2)}) %collective-permute-start.6) | collective-permute-done | bytes 524320 | tf_op jit(solution)/shard_map/ppermute | solution.py:330
  7.8 0.3 shard_map.89
  8.1 2.9 %collective-permute-start.7 = (s16[528,128]{1,0:T(8,128)(2,1)S(1)}, s16[528,128]{1,0:T(8,128)(2,1)S(1)}, u32[]{:S(2)}, u32[]{:S(2)}) collective-permute-start(s16[528,128]{1,0:T(8,128)(2,1)S(1)} %get-tuple-element.51), channel_id=1, source_target_pairs={{0,4},{2,6},{4,0},{6,2},{8,12},{10,14},{12,8},{14,10},{16,20},{18,... | collective-permute-start | bytes 405512 | tf_op jit(solution)/shard_map/ppermute | solution.py:330
  11.0 0.4 shard_map.87
  11.4 0.1 collective-permute-start.4
  11.5 0.4 shard_map.85
  11.9 2.1 %collective-permute-start.2 = (s16[528,128]{1,0:T(8,128)(2,1)S(1)}, s16[528,128]{1,0:T(8,128)(2,1)S(1)}, u32[]{:S(2)}, u32[]{:S(2)}) collective-permute-start(s16[528,128]{1,0:T(8,128)(2,1)S(1)} %get-tuple-element.45), channel_id=1, source_target_pairs={{0,4},{2,6},{4,0},{6,2},{8,12},{10,14},{12,8},{14,10},{16,20},{18,... | collective-permute-start | bytes 405512 | tf_op jit(solution)/shard_map/ppermute | solution.py:330
  13.9 1.6 %collective-permute-done.7.got_ref = s16[528,128]{1,0:T(8,128)(2,1)S(1)} collective-permute-done((s16[528,128]{1,0:T(8,128)(2,1)S(1)}, s16[528,128]{1,0:T(8,128)(2,1)S(1)}, u32[]{:S(2)}, u32[]{:S(2)}) %collective-permute-start.7) | collective-permute-done | bytes 135200 | tf_op jit(solution)/shard_map/ppermute | solution.py:330
  15.5 0.5 shard_map.90
  16.0 4.2 %collective-permute-start.8 = (s16[528,128]{1,0:T(8,128)(2,1)S(1)}, s16[528,128]{1,0:T(8,128)(2,1)S(1)}, u32[]{:S(2)}, u32[]{:S(2)}) collective-permute-start(s16[528,128]{1,0:T(8,128)(2,1)S(1)} %shard_map.90), channel_id=1, source_target_pairs={{0,24},{2,26},{4,28},{6,30},{8,16},{10,18},{12,20},{14,22},{16,8},... | collective-permute-start | bytes 405512 | tf_op jit(solution)/shard_map/ppermute | solution.py:330
  20.2 0.9 collective-permute-start.13
  21.1 0.4 shard_map.83
  21.5 1.6 %collective-permute-start.1 = (s16[528,128]{1,0:T(8,128)(2,1)S(1)}, s16[528,128]{1,0:T(8,128)(2,1)S(1)}, u32[]{:S(2)}, u32[]{:S(2)}) collective-permute-start(s16[528,128]{1,0:T(8,128)(2,1)S(1)} %get-tuple-element.43), channel_id=1, source_target_pairs={{0,4},{2,6},{4,0},{6,2},{8,12},{10,14},{12,8},{14,10},{16,20},{18,... | collective-permute-start | bytes 405512 | tf_op jit(solution)/shard_map/ppermute | solution.py:330
  23.0 0.5 shard_map.88
  23.6 2.7 %collective-permute-start.5 = (s16[528,128]{1,0:T(8,128)(2,1)S(1)}, s16[528,128]{1,0:T(8,128)(2,1)S(1)}, u32[]{:S(2)}, u32[]{:S(2)}) collective-permute-start(s16[528,128]{1,0:T(8,128)(2,1)S(1)} %shard_map.88), channel_id=1, source_target_pairs={{0,16},{2,18},{4,20},{6,22},{8,24},{10,26},{12,28},{14,30},{16,0},... | collective-permute-start | bytes 405512 | tf_op jit(solution)/shard_map/ppermute | solution.py:330
  26.2 0.5 shard_map.86
  26.7 1.0 collective-permute-start.3
  27.7 1.4 %collective-permute-start.14 = (bf16[1040,128]{1,0:T(8,128)(2,1)S(1)}, bf16[1040,128]{1,0:T(8,128)(2,1)S(1)}, u32[]{:S(2)}, u32[]{:S(2)}) collective-permute-start(bf16[1040,128]{1,0:T(8,128)(2,1)S(1)} %get-tuple-element.67), channel_id=1, source_target_pairs={{0,16},{2,18},{4,20},{6,22},{8,24},{10,26},{12,28},{14,30},{16,0},... | collective-permute-start | bytes 798728 | tf_op jit(solution)/shard_map/ppermute | solution.py:330
  29.1 0.3 shard_map.84.own_ref
  29.4 19.0 %collective-permute-done.5.rest_1_ = s16[528,128]{1,0:T(8,128)(2,1)S(1)} collective-permute-done((s16[528,128]{1,0:T(8,128)(2,1)S(1)}, s16[528,128]{1,0:T(8,128)(2,1)S(1)}, u32[]{:S(2)}, u32[]{:S(2)}) %collective-permute-start.5) | collective-permute-done | bytes 135200 | tf_op jit(solution)/shard_map/ppermute | solution.py:330
  48.4 1.0 shard_map.91.q_ref
  49.4 0.1 collective-permute-start.9
  49.5 1.4 %collective-permute-start.11 = (bf16[64,1024]{1,0:T(8,128)(2,1)S(1)}, bf16[64,1024]{1,0:T(8,128)(2,1)S(1)}, u32[]{:S(2)}, u32[]{:S(2)}) collective-permute-start(bf16[64,1024]{1,0:T(8,128)(2,1)S(1)} %shard_map.91.q_ref), channel_id=1, source_target_pairs={{0,4},{2,6},{4,0},{6,2},{8,12},{10,14},{12,8},{14,10},{16,20},{18,... | collective-permute-start | bytes 393224 | tf_op jit(solution)/shard_map/ppermute | solution.py:330
  50.9 0.4 collective-permute-start.10
  51.3 1.6 %shard_map.92 = (f32[128,512]{1,0:T(8,128)S(1)}, f32[8,512]{1,0:T(8,128)S(1)}) custom-call(bf16[64,1024]{1,0:T(8,128)(2,1)S(1)} %shard_map.91.q_ref, s32[2,128]{1,0:T(2,128)S(1)} %bitcast.31, bf16[1040,128]{1,0:T(8,128)(2,1)S(1)} %get-tuple-element.52.rest_0_, bf16[1040,128]{1,0:T(8,128)(2,1)S(1)} %collective-permute-done.12.rest_1_, ...), custom_call_target="tpu_custom_call" | custom-call | flops 402653184 | bytes 1209344 | tf_op jit(solution)/shard_map/pallas_call | solution.py:39
  53.0 1.6 %shard_map.93 = (f32[128,512]{1,0:T(8,128)S(1)}, f32[8,512]{1,0:T(8,128)S(1)}) custom-call(bf16[64,1024]{1,0:T(8,128)(2,1)S(1)} %collective-permute-done.9.q_ref, s32[2,128]{1,0:T(2,128)S(1)} %bitcast.32, bf16[1040,128]{1,0:T(8,128)(2,1)S(1)} %get-tuple-element.52.rest_0_, bf16[1040,128]{1,0:T(8,128)(2,1)S(1)} %collective-permute-done.12.rest_1_, ...), custom_call_target="tpu_custom_call" | custom-call | flops 402653184 | bytes 1209344 | tf_op jit(solution)/shard_map/pallas_call | solution.py:39
  54.6 1.3 %collective-permute-done.11.q_ref = bf16[64,1024]{1,0:T(8,128)(2,1)S(1)} collective-permute-done((bf16[64,1024]{1,0:T(8,128)(2,1)S(1)}, bf16[64,1024]{1,0:T(8,128)(2,1)S(1)}, u32[]{:S(2)}, u32[]{:S(2)}) %collective-permute-start.11) | collective-permute-done | bytes 131104 | tf_op jit(solution)/shard_map/ppermute | solution.py:330
  55.9 1.6 %shard_map.94 = (f32[128,512]{1,0:T(8,128)S(1)}, f32[8,512]{1,0:T(8,128)S(1)}) custom-call(bf16[64,1024]{1,0:T(8,128)(2,1)S(1)} %collective-permute-done.11.q_ref, s32[2,128]{1,0:T(2,128)S(1)} %bitcast.33, bf16[1040,128]{1,0:T(8,128)(2,1)S(1)} %get-tuple-element.52.rest_0_, bf16[1040,128]{1,0:T(8,128)(2,1)S(1)} %collective-permute-done.12.rest_1_, ...), custom_call_target="tpu_custom_call" | custom-call | flops 402653184 | bytes 1209344 | tf_op jit(solution)/shard_map/pallas_call | solution.py:39
  57.5 0.1 collective-permute-done.10.q_ref
  57.6 1.6 %shard_map.95 = (f32[128,512]{1,0:T(8,128)S(1)}, f32[8,512]{1,0:T(8,128)S(1)}) custom-call(bf16[64,1024]{1,0:T(8,128)(2,1)S(1)} %collective-permute-done.10.q_ref, s32[2,128]{1,0:T(2,128)S(1)} %bitcast.34, bf16[1040,128]{1,0:T(8,128)(2,1)S(1)} %get-tuple-element.52.rest_0_, bf16[1040,128]{1,0:T(8,128)(2,1)S(1)} %collective-permute-done.12.rest_1_, ...), custom_call_target="tpu_custom_call" | custom-call | flops 402653184 | bytes 1209344 | tf_op jit(solution)/shard_map/pallas_call | solution.py:39
  59.2 0.7 shard_map.96
  59.9 0.9 shard_map.97
  60.8 0.7 shard_map.98
  61.5 0.4 collective-permute-start.15
  61.9 1.1 %collective-permute-start.17 = (s16[144,512]{1,0:T(8,128)(2,1)S(1)}, s16[144,512]{1,0:T(8,128)(2,1)S(1)}, u32[]{:S(2)}, u32[]{:S(2)}) collective-permute-start(s16[144,512]{1,0:T(8,128)(2,1)S(1)} %shard_map.97), channel_id=1, source_target_pairs={{0,6},{2,4},{4,2},{6,0},{8,14},{10,12},{12,10},{14,8},{16,22},{18,... | collective-permute-start | bytes 442376 | tf_op jit(solution)/shard_map/ppermute | solution.py:330
  63.1 0.6 collective-permute-start.16
  63.7 0.6 shard_map.99
  64.4 3.4 %collective-permute-done.17.rest_2_ = s16[144,512]{1,0:T(8,128)(2,1)S(1)} collective-permute-done((s16[144,512]{1,0:T(8,128)(2,1)S(1)}, s16[144,512]{1,0:T(8,128)(2,1)S(1)}, u32[]{:S(2)}, u32[]{:S(2)}) %collective-permute-start.17) | collective-permute-done | bytes 147488 | tf_op jit(solution)/shard_map/ppermute | solution.py:330
  67.8 3.5 %collective-permute-done.16.rest_1_ = s16[144,512]{1,0:T(8,128)(2,1)S(1)} collective-permute-done((s16[144,512]{1,0:T(8,128)(2,1)S(1)}, s16[144,512]{1,0:T(8,128)(2,1)S(1)}, u32[]{:S(2)}, u32[]{:S(2)}) %collective-permute-start.16) | collective-permute-done | bytes 147488 | tf_op jit(solution)/shard_map/ppermute | solution.py:330
  71.3 0.2 shard_map.100.rest_0_
  71.5 3.4 %collective-permute-start.24 = (bf16[64,1024]{1,0:T(8,128)(2,1)S(1)}, bf16[64,1024]{1,0:T(8,128)(2,1)S(1)}, u32[]{:S(2)}, u32[]{:S(2)}) collective-permute-start(bf16[64,1024]{1,0:T(8,128)(2,1)S(1)} %shard_map.100.rest_0_), channel_id=1, source_target_pairs={{0,24},{2,26},{4,28},{6,30},{8,0},{10,2},{12,4},{14,6},{16,8},{18,... | collective-permute-start | bytes 393224 | tf_op jit(solution)/shard_map/ppermute | solution.py:333
  74.9 0.6 collective-permute-start.22
  75.5 3.3 %collective-permute-done.24.rest_4_ = bf16[64,1024]{1,0:T(8,128)(2,1)S(1)} collective-permute-done((bf16[64,1024]{1,0:T(8,128)(2,1)S(1)}, bf16[64,1024]{1,0:T(8,128)(2,1)S(1)}, u32[]{:S(2)}, u32[]{:S(2)}) %collective-permute-start.24) | collective-permute-done | bytes 131104 | tf_op jit(solution)/shard_map/ppermute | solution.py:333
  78.8 1.5 %collective-permute-start.25 = (bf16[64,1024]{1,0:T(8,128)(2,1)S(1)}, bf16[64,1024]{1,0:T(8,128)(2,1)S(1)}, u32[]{:S(2)}, u32[]{:S(2)}) collective-permute-start(bf16[64,1024]{1,0:T(8,128)(2,1)S(1)} %collective-permute-done.24.rest_4_), channel_id=1, source_target_pairs={{0,4},{2,6},{4,0},{6,2},{8,12},{10,14},{12,8},{14,10},{16,20},{18,... | collective-permute-start | bytes 393224 | tf_op jit(solution)/shard_map/ppermute | solution.py:330
  80.3 0.5 collective-permute-start.18
  80.8 2.3 %collective-permute-done.19.rest_4_ = bf16[64,1024]{1,0:T(8,128)(2,1)S(1)} collective-permute-done((bf16[64,1024]{1,0:T(8,128)(2,1)S(1)}, bf16[64,1024]{1,0:T(8,128)(2,1)S(1)}, u32[]{:S(2)}, u32[]{:S(2)}) %collective-permute-start.19) | collective-permute-done | bytes 131104 | tf_op jit(solution)/shard_map/ppermute | solution.py:333
  83.1 1.5 %collective-permute-start.20 = (bf16[64,1024]{1,0:T(8,128)(2,1)S(1)}, bf16[64,1024]{1,0:T(8,128)(2,1)S(1)}, u32[]{:S(2)}, u32[]{:S(2)}) collective-permute-start(bf16[64,1024]{1,0:T(8,128)(2,1)S(1)} %collective-permute-done.19.rest_4_), channel_id=1, source_target_pairs={{0,4},{2,6},{4,0},{6,2},{8,12},{10,14},{12,8},{14,10},{16,20},{18,... | collective-permute-start | bytes 393224 | tf_op jit(solution)/shard_map/ppermute | solution.py:330
  84.6 1.7 %collective-permute-done.22.rest_0_ = bf16[64,1024]{1,0:T(8,128)(2,1)S(1)} collective-permute-done((bf16[64,1024]{1,0:T(8,128)(2,1)S(1)}, bf16[64,1024]{1,0:T(8,128)(2,1)S(1)}, u32[]{:S(2)}, u32[]{:S(2)}) %collective-permute-start.22) | collective-permute-done | bytes 131104 | tf_op jit(solution)/shard_map/ppermute | solution.py:333
  86.4 0.1 collective-permute-start.26
  86.4 0.1 collective-permute-done.18.rest_1_
  86.5 1.5 %collective-permute-done.20.rest_5_ = bf16[64,1024]{1,0:T(8,128)(2,1)S(1)} collective-permute-done((bf16[64,1024]{1,0:T(8,128)(2,1)S(1)}, bf16[64,1024]{1,0:T(8,128)(2,1)S(1)}, u32[]{:S(2)}, u32[]{:S(2)}) %collective-permute-start.20) | collective-permute-done | bytes 131104 | tf_op jit(solution)/shard_map/ppermute | solution.py:330
  88.1 0.1 pad_maximum_fusion
  88.1 0.1 collective-permute-start.21
  88.2 1.6 %collective-permute-start.23 = (bf16[64,1024]{1,0:T(8,128)(2,1)S(1)}, bf16[64,1024]{1,0:T(8,128)(2,1)S(1)}, u32[]{:S(2)}, u32[]{:S(2)}) collective-permute-start(bf16[64,1024]{1,0:T(8,128)(2,1)S(1)} %collective-permute-done.22.rest_0_), channel_id=1, source_target_pairs={{0,4},{2,6},{4,0},{6,2},{8,12},{10,14},{12,8},{14,10},{16,20},{18,... | collective-permute-start | bytes 393224 | tf_op jit(solution)/shard_map/ppermute | solution.py:330
  89.8 4.3 %collective-permute-done.23.rest_1_ = bf16[64,1024]{1,0:T(8,128)(2,1)S(1)} collective-permute-done((bf16[64,1024]{1,0:T(8,128)(2,1)S(1)}, bf16[64,1024]{1,0:T(8,128)(2,1)S(1)}, u32[]{:S(2)}, u32[]{:S(2)}) %collective-permute-start.23) | collective-permute-done | bytes 131104 | tf_op jit(solution)/shard_map/ppermute | solution.py:330
  94.2 0.7 shard_map.101.before_ref
  94.9 0.5 collective-permute-done.27.rest_3_
  95.5 0.8 shard_map.102
  96.2 1.6 %collective-permute-start.28 = (s16[144,512]{1,0:T(8,128)(2,1)S(1)}, s16[144,512]{1,0:T(8,128)(2,1)S(1)}, u32[]{:S(2)}, u32[]{:S(2)}) collective-permute-start(s16[144,512]{1,0:T(8,128)(2,1)S(1)} %get-tuple-element.74), channel_id=1, source_target_pairs={{0,1},{1,0},{2,3},{3,2},{4,5},{5,4},{6,7},{7,6},{8,9},{9,8},{10,11... | collective-permute-start | bytes 442376 | tf_op jit(solution)/shard_map/ppermute | solution.py:446
  97.8 4.4 %collective-permute-done.28.got_ref = s16[144,512]{1,0:T(8,128)(2,1)S(1)} collective-permute-done((s16[144,512]{1,0:T(8,128)(2,1)S(1)}, s16[144,512]{1,0:T(8,128)(2,1)S(1)}, u32[]{:S(2)}, u32[]{:S(2)}) %collective-permute-start.28) | collective-permute-done | bytes 147488 | tf_op jit(solution)/shard_map/ppermute | solution.py:446
  102.2 0.7 shard_map.103
  (28 shorter events, 0.2 us)
Async XLA Ops:
  3.4 7.6 %collective-permute-start = (f32[128,3072]{1,0:T(8,128)S(1)}, f32[128,3072]{1,0:T(8,128)S(1)}, u32[]{:S(2)}, u32[]{:S(2)}) collective-permute-start(f32[128,3072]{1,0:T(8,128)S(1)} %get-tuple-element.41), channel_id=1, source_target_pairs={{0,2},{2,0},{4,6},{6,4},{8,10},{10,8},{12,14},{14,12},{16,18},{18,... | collective-permute-start | bytes 4718600 | tf_op jit(solution)/shard_map/ppermute | solution.py:330
  4.0 3.8 %collective-permute-start.6 = (f32[128,1024]{1,0:T(8,128)S(1)}, f32[128,1024]{1,0:T(8,128)S(1)}, u32[]{:S(2)}, u32[]{:S(2)}) collective-permute-start(f32[128,1024]{1,0:T(8,128)S(1)} %get-tuple-element.49), channel_id=1, source_target_pairs={{0,2},{2,0},{4,6},{6,4},{8,10},{10,8},{12,14},{14,12},{16,18},{18,... | collective-permute-start | bytes 1572872 | tf_op jit(solution)/shard_map/ppermute | solution.py:330
  8.1 7.4 %collective-permute-start.7 = (s16[528,128]{1,0:T(8,128)(2,1)S(1)}, s16[528,128]{1,0:T(8,128)(2,1)S(1)}, u32[]{:S(2)}, u32[]{:S(2)}) collective-permute-start(s16[528,128]{1,0:T(8,128)(2,1)S(1)} %get-tuple-element.51), channel_id=1, source_target_pairs={{0,4},{2,6},{4,0},{6,2},{8,12},{10,14},{12,8},{14,10},{16,20},{18,... | collective-permute-start | bytes 405512 | tf_op jit(solution)/shard_map/ppermute | solution.py:330
  11.4 10.1 %collective-permute-start.4 = (s16[528,128]{1,0:T(8,128)(2,1)S(1)}, s16[528,128]{1,0:T(8,128)(2,1)S(1)}, u32[]{:S(2)}, u32[]{:S(2)}) collective-permute-start(s16[528,128]{1,0:T(8,128)(2,1)S(1)} %get-tuple-element.47), channel_id=1, source_target_pairs={{0,4},{2,6},{4,0},{6,2},{8,12},{10,14},{12,8},{14,10},{16,20},{18,... | collective-permute-start | bytes 405512 | tf_op jit(solution)/shard_map/ppermute | solution.py:330
  11.9 11.7 %collective-permute-start.2 = (s16[528,128]{1,0:T(8,128)(2,1)S(1)}, s16[528,128]{1,0:T(8,128)(2,1)S(1)}, u32[]{:S(2)}, u32[]{:S(2)}) collective-permute-start(s16[528,128]{1,0:T(8,128)(2,1)S(1)} %get-tuple-element.45), channel_id=1, source_target_pairs={{0,4},{2,6},{4,0},{6,2},{8,12},{10,14},{12,8},{14,10},{16,20},{18,... | collective-permute-start | bytes 405512 | tf_op jit(solution)/shard_map/ppermute | solution.py:330
  16.0 10.7 %collective-permute-start.8 = (s16[528,128]{1,0:T(8,128)(2,1)S(1)}, s16[528,128]{1,0:T(8,128)(2,1)S(1)}, u32[]{:S(2)}, u32[]{:S(2)}) collective-permute-start(s16[528,128]{1,0:T(8,128)(2,1)S(1)} %shard_map.90), channel_id=1, source_target_pairs={{0,24},{2,26},{4,28},{6,30},{8,16},{10,18},{12,20},{14,22},{16,8},... | collective-permute-start | bytes 405512 | tf_op jit(solution)/shard_map/ppermute | solution.py:330
  20.2 30.7 %collective-permute-start.12 = (bf16[1040,128]{1,0:T(8,128)(2,1)S(1)}, bf16[1040,128]{1,0:T(8,128)(2,1)S(1)}, u32[]{:S(2)}, u32[]{:S(2)}) collective-permute-start(bf16[1040,128]{1,0:T(8,128)(2,1)S(1)} %get-tuple-element.53), channel_id=1, source_target_pairs={{0,8},{2,10},{4,12},{6,14},{8,0},{10,2},{12,4},{14,6},{16,24},{18,... | collective-permute-start | bytes 798728 | tf_op jit(solution)/shard_map/ppermute | solution.py:330
  20.2 31.1 %collective-permute-start.13 = (bf16[1040,128]{1,0:T(8,128)(2,1)S(1)}, bf16[1040,128]{1,0:T(8,128)(2,1)S(1)}, u32[]{:S(2)}, u32[]{:S(2)}) collective-permute-start(bf16[1040,128]{1,0:T(8,128)(2,1)S(1)} %get-tuple-element.54), channel_id=1, source_target_pairs={{0,24},{2,26},{4,28},{6,30},{8,16},{10,18},{12,20},{14,22},{16,8},... | collective-permute-start | bytes 798728 | tf_op jit(solution)/shard_map/ppermute | solution.py:330
  21.4 27.0 %copy-start.3 = (f32[128]{0:T(128)S(1)}, f32[128]{0:T(128)}, u32[]{:S(2)}) copy-start(f32[128]{0:T(128)} %param.10) | copy-start | bytes 1540
  21.5 29.9 %copy-start.2 = (s32[256]{0:T(256)S(1)}, s32[256]{0:T(256)}, u32[]{:S(2)}) copy-start(s32[256]{0:T(256)} %param.14) | copy-start | bytes 3076
  21.5 6.2 %collective-permute-start.1 = (s16[528,128]{1,0:T(8,128)(2,1)S(1)}, s16[528,128]{1,0:T(8,128)(2,1)S(1)}, u32[]{:S(2)}, u32[]{:S(2)}) collective-permute-start(s16[528,128]{1,0:T(8,128)(2,1)S(1)} %get-tuple-element.43), channel_id=1, source_target_pairs={{0,4},{2,6},{4,0},{6,2},{8,12},{10,14},{12,8},{14,10},{16,20},{18,... | collective-permute-start | bytes 405512 | tf_op jit(solution)/shard_map/ppermute | solution.py:330
  23.6 24.8 %collective-permute-start.5 = (s16[528,128]{1,0:T(8,128)(2,1)S(1)}, s16[528,128]{1,0:T(8,128)(2,1)S(1)}, u32[]{:S(2)}, u32[]{:S(2)}) collective-permute-start(s16[528,128]{1,0:T(8,128)(2,1)S(1)} %shard_map.88), channel_id=1, source_target_pairs={{0,16},{2,18},{4,20},{6,22},{8,24},{10,26},{12,28},{14,30},{16,0},... | collective-permute-start | bytes 405512 | tf_op jit(solution)/shard_map/ppermute | solution.py:330
  26.7 21.7 %collective-permute-start.3 = (s16[528,128]{1,0:T(8,128)(2,1)S(1)}, s16[528,128]{1,0:T(8,128)(2,1)S(1)}, u32[]{:S(2)}, u32[]{:S(2)}) collective-permute-start(s16[528,128]{1,0:T(8,128)(2,1)S(1)} %shard_map.86), channel_id=1, source_target_pairs={{0,8},{2,10},{4,12},{6,14},{8,0},{10,2},{12,4},{14,6},{16,24},{18,... | collective-permute-start | bytes 405512 | tf_op jit(solution)/shard_map/ppermute | solution.py:330
  27.7 31.5 %collective-permute-start.14 = (bf16[1040,128]{1,0:T(8,128)(2,1)S(1)}, bf16[1040,128]{1,0:T(8,128)(2,1)S(1)}, u32[]{:S(2)}, u32[]{:S(2)}) collective-permute-start(bf16[1040,128]{1,0:T(8,128)(2,1)S(1)} %get-tuple-element.67), channel_id=1, source_target_pairs={{0,16},{2,18},{4,20},{6,22},{8,24},{10,26},{12,28},{14,30},{16,0},... | collective-permute-start | bytes 798728 | tf_op jit(solution)/shard_map/ppermute | solution.py:330
  49.4 3.6 %collective-permute-start.9 = (bf16[64,1024]{1,0:T(8,128)(2,1)S(1)}, bf16[64,1024]{1,0:T(8,128)(2,1)S(1)}, u32[]{:S(2)}, u32[]{:S(2)}) collective-permute-start(bf16[64,1024]{1,0:T(8,128)(2,1)S(1)} %shard_map.91.q_ref), channel_id=1, source_target_pairs={{0,2},{2,0},{4,6},{6,4},{8,10},{10,8},{12,14},{14,12},{16,18},{18,... | collective-permute-start | bytes 393224 | tf_op jit(solution)/shard_map/ppermute | solution.py:330
  49.5 6.4 %collective-permute-start.11 = (bf16[64,1024]{1,0:T(8,128)(2,1)S(1)}, bf16[64,1024]{1,0:T(8,128)(2,1)S(1)}, u32[]{:S(2)}, u32[]{:S(2)}) collective-permute-start(bf16[64,1024]{1,0:T(8,128)(2,1)S(1)} %shard_map.91.q_ref), channel_id=1, source_target_pairs={{0,4},{2,6},{4,0},{6,2},{8,12},{10,14},{12,8},{14,10},{16,20},{18,... | collective-permute-start | bytes 393224 | tf_op jit(solution)/shard_map/ppermute | solution.py:330
  50.9 6.7 %collective-permute-start.10 = (bf16[64,1024]{1,0:T(8,128)(2,1)S(1)}, bf16[64,1024]{1,0:T(8,128)(2,1)S(1)}, u32[]{:S(2)}, u32[]{:S(2)}) collective-permute-start(bf16[64,1024]{1,0:T(8,128)(2,1)S(1)} %shard_map.91.q_ref), channel_id=1, source_target_pairs={{0,6},{2,4},{4,2},{6,0},{8,14},{10,12},{12,10},{14,8},{16,22},{18,... | collective-permute-start | bytes 393224 | tf_op jit(solution)/shard_map/ppermute | solution.py:330
  61.5 2.9 %collective-permute-start.15 = (s16[144,512]{1,0:T(8,128)(2,1)S(1)}, s16[144,512]{1,0:T(8,128)(2,1)S(1)}, u32[]{:S(2)}, u32[]{:S(2)}) collective-permute-start(s16[144,512]{1,0:T(8,128)(2,1)S(1)} %shard_map.98), channel_id=1, source_target_pairs={{0,2},{2,0},{4,6},{6,4},{8,10},{10,8},{12,14},{14,12},{16,18},{18,... | collective-permute-start | bytes 442376 | tf_op jit(solution)/shard_map/ppermute | solution.py:330
  61.9 5.8 %collective-permute-start.17 = (s16[144,512]{1,0:T(8,128)(2,1)S(1)}, s16[144,512]{1,0:T(8,128)(2,1)S(1)}, u32[]{:S(2)}, u32[]{:S(2)}) collective-permute-start(s16[144,512]{1,0:T(8,128)(2,1)S(1)} %shard_map.97), channel_id=1, source_target_pairs={{0,6},{2,4},{4,2},{6,0},{8,14},{10,12},{12,10},{14,8},{16,22},{18,... | collective-permute-start | bytes 442376 | tf_op jit(solution)/shard_map/ppermute | solution.py:330
  63.1 8.2 %collective-permute-start.16 = (s16[144,512]{1,0:T(8,128)(2,1)S(1)}, s16[144,512]{1,0:T(8,128)(2,1)S(1)}, u32[]{:S(2)}, u32[]{:S(2)}) collective-permute-start(s16[144,512]{1,0:T(8,128)(2,1)S(1)} %shard_map.96), channel_id=1, source_target_pairs={{0,4},{2,6},{4,0},{6,2},{8,12},{10,14},{12,8},{14,10},{16,20},{18,... | collective-permute-start | bytes 442376 | tf_op jit(solution)/shard_map/ppermute | solution.py:330
  71.3 23.0 %copy-start = (bf16[4096,512]{1,0:T(8,128)(2,1)S(1)}, bf16[4096,512]{1,0:T(8,128)(2,1)}, u32[]{:S(2)}) copy-start(bf16[4096,512]{1,0:T(8,128)(2,1)} %w_ref.3) | copy-start | bytes 12582916
  71.5 7.3 %collective-permute-start.24 = (bf16[64,1024]{1,0:T(8,128)(2,1)S(1)}, bf16[64,1024]{1,0:T(8,128)(2,1)S(1)}, u32[]{:S(2)}, u32[]{:S(2)}) collective-permute-start(bf16[64,1024]{1,0:T(8,128)(2,1)S(1)} %shard_map.100.rest_0_), channel_id=1, source_target_pairs={{0,24},{2,26},{4,28},{6,30},{8,0},{10,2},{12,4},{14,6},{16,8},{18,... | collective-permute-start | bytes 393224 | tf_op jit(solution)/shard_map/ppermute | solution.py:333
  74.9 8.2 %collective-permute-start.19 = (bf16[64,1024]{1,0:T(8,128)(2,1)S(1)}, bf16[64,1024]{1,0:T(8,128)(2,1)S(1)}, u32[]{:S(2)}, u32[]{:S(2)}) collective-permute-start(bf16[64,1024]{1,0:T(8,128)(2,1)S(1)} %shard_map.100.rest_0_), channel_id=1, source_target_pairs={{0,8},{2,10},{4,12},{6,14},{8,16},{10,18},{12,20},{14,22},{16,24},... | collective-permute-start | bytes 393224 | tf_op jit(solution)/shard_map/ppermute | solution.py:333
  74.9 11.4 %collective-permute-start.22 = (bf16[64,1024]{1,0:T(8,128)(2,1)S(1)}, bf16[64,1024]{1,0:T(8,128)(2,1)S(1)}, u32[]{:S(2)}, u32[]{:S(2)}) collective-permute-start(bf16[64,1024]{1,0:T(8,128)(2,1)S(1)} %shard_map.100.rest_0_), channel_id=1, source_target_pairs={{0,16},{2,18},{4,20},{6,22},{8,24},{10,26},{12,28},{14,30},{16,0},... | collective-permute-start | bytes 393224 | tf_op jit(solution)/shard_map/ppermute | solution.py:333
  78.8 7.5 %collective-permute-start.25 = (bf16[64,1024]{1,0:T(8,128)(2,1)S(1)}, bf16[64,1024]{1,0:T(8,128)(2,1)S(1)}, u32[]{:S(2)}, u32[]{:S(2)}) collective-permute-start(bf16[64,1024]{1,0:T(8,128)(2,1)S(1)} %collective-permute-done.24.rest_4_), channel_id=1, source_target_pairs={{0,4},{2,6},{4,0},{6,2},{8,12},{10,14},{12,8},{14,10},{16,20},{18,... | collective-permute-start | bytes 393224 | tf_op jit(solution)/shard_map/ppermute | solution.py:330
  80.3 6.3 %collective-permute-start.18 = (bf16[64,1024]{1,0:T(8,128)(2,1)S(1)}, bf16[64,1024]{1,0:T(8,128)(2,1)S(1)}, u32[]{:S(2)}, u32[]{:S(2)}) collective-permute-start(bf16[64,1024]{1,0:T(8,128)(2,1)S(1)} %shard_map.100.rest_0_), channel_id=1, source_target_pairs={{0,4},{2,6},{4,0},{6,2},{8,12},{10,14},{12,8},{14,10},{16,20},{18,... | collective-permute-start | bytes 393224 | tf_op jit(solution)/shard_map/ppermute | solution.py:330
  83.1 5.0 %collective-permute-start.20 = (bf16[64,1024]{1,0:T(8,128)(2,1)S(1)}, bf16[64,1024]{1,0:T(8,128)(2,1)S(1)}, u32[]{:S(2)}, u32[]{:S(2)}) collective-permute-start(bf16[64,1024]{1,0:T(8,128)(2,1)S(1)} %collective-permute-done.19.rest_4_), channel_id=1, source_target_pairs={{0,4},{2,6},{4,0},{6,2},{8,12},{10,14},{12,8},{14,10},{16,20},{18,... | collective-permute-start | bytes 393224 | tf_op jit(solution)/shard_map/ppermute | solution.py:330
  86.4 7.8 %collective-permute-start.26 = (bf16[3,64,1024]{2,1,0:T(8,128)(2,1)S(1)}, bf16[3,64,1024]{2,1,0:T(8,128)(2,1)S(1)}, u32[]{:S(2)}, u32[]{:S(2)}) collective-permute-start(bf16[3,64,1024]{2,1,0:T(8,128)(2,1)S(1)} %pad_maximum_fusion.1), channel_id=1, source_target_pairs={{0,2},{2,0},{4,6},{6,4},{8,10},{10,8},{12,14},{14,12},{16,18},{18,... | collective-permute-start | bytes 1179656 | tf_op jit(solution)/shard_map/ppermute | solution.py:330
  88.1 6.0 %collective-permute-start.21 = (bf16[4,64,1024]{2,1,0:T(8,128)(2,1)S(1)}, bf16[4,64,1024]{2,1,0:T(8,128)(2,1)S(1)}, u32[]{:S(2)}, u32[]{:S(2)}) collective-permute-start(bf16[4,64,1024]{2,1,0:T(8,128)(2,1)S(1)} %pad_maximum_fusion), channel_id=1, source_target_pairs={{0,2},{2,0},{4,6},{6,4},{8,10},{10,8},{12,14},{14,12},{16,18},{18,... | collective-permute-start | bytes 1572872 | tf_op jit(solution)/shard_map/ppermute | solution.py:330
  88.2 5.9 %collective-permute-start.23 = (bf16[64,1024]{1,0:T(8,128)(2,1)S(1)}, bf16[64,1024]{1,0:T(8,128)(2,1)S(1)}, u32[]{:S(2)}, u32[]{:S(2)}) collective-permute-start(bf16[64,1024]{1,0:T(8,128)(2,1)S(1)} %collective-permute-done.22.rest_0_), channel_id=1, source_target_pairs={{0,4},{2,6},{4,0},{6,2},{8,12},{10,14},{12,8},{14,10},{16,20},{18,... | collective-permute-start | bytes 393224 | tf_op jit(solution)/shard_map/ppermute | solution.py:330
  94.1 1.3 %collective-permute-start.27 = (bf16[64,1024]{1,0:T(8,128)(2,1)S(1)}, bf16[64,1024]{1,0:T(8,128)(2,1)S(1)}, u32[]{:S(2)}, u32[]{:S(2)}) collective-permute-start(bf16[64,1024]{1,0:T(8,128)(2,1)S(1)} %collective-permute-done.23.rest_1_), channel_id=1, source_target_pairs={{0,2},{2,0},{4,6},{6,4},{8,10},{10,8},{12,14},{14,12},{16,18},{18,... | collective-permute-start | bytes 393224 | tf_op jit(solution)/shard_map/ppermute | solution.py:330
  95.5 6.8 %copy-start.1 = (bf16[256,512]{1,0:T(8,128)(2,1)S(1)}, bf16[256,512]{1,0:T(8,128)(2,1)}, u32[]{:S(2)}) copy-start(bf16[256,512]{1,0:T(8,128)(2,1)} %text_ref.1) | copy-start | bytes 786436
  96.2 6.0 %collective-permute-start.28 = (s16[144,512]{1,0:T(8,128)(2,1)S(1)}, s16[144,512]{1,0:T(8,128)(2,1)S(1)}, u32[]{:S(2)}, u32[]{:S(2)}) collective-permute-start(s16[144,512]{1,0:T(8,128)(2,1)S(1)} %get-tuple-element.74), channel_id=1, source_target_pairs={{0,1},{1,0},{2,3},{3,2},{4,5},{5,4},{6,7},{7,6},{8,9},{9,8},{10,11... | collective-permute-start | bytes 442376 | tf_op jit(solution)/shard_map/ppermute | solution.py:446

commit v2 on v1

--- a/solution.py
+++ b/solution.py
@@ -271,45 +271,47 @@
 
 def output_part(ds, blocks, w_ref):
     width = blocks[0][0].shape[1]
+    groups = w_ref.shape[0] // width
     total = None
     for d, row_blocks in zip(ds, blocks):
         left = jnp.concatenate([b[...] for b in row_blocks], axis=0)
-        groups = w_ref.shape[0] // width
         base = pl.multiple_of(lax.rem(ids[2] + groups - d, groups) * width, width)
         part = jnp.dot(left, w_ref[pl.ds(base, width), :], preferred_element_type=F32)
         total = part if total is None else total + part
     return total
 
 
-def output_first_kernel(ds, w_ref, *rest):
-    blocks = [rest[4 * i : 4 * i + 4] for i in range(len(ds))]
-    rest[-1][...] = output_part(ds, blocks, w_ref)
-
-
-def output_last_kernel(ds, w_ref, before_ref, *rest):
-    blocks, (keep_ref, code_ref, send_buf) = [rest[4 * i : 4 * i + 4] for i in range(len(ds))], rest[-3:]
-    total = output_part(ds, blocks, w_ref) + before_ref[...]
-    rows = total.shape[0] // 4
-    swap_core = jnp.full((rows, 1), (ids[0] == ids[3]).astype(I32), I32) == 1
-    for xs in range(2):
-        at = pl.multiple_of((ids[1] ^ xs) * rows, rows)
-        own = total[xs * rows : (xs + 1) * rows]
-        other = total[(2 + xs) * rows : (3 + xs) * rows]
-        send_buf[pl.ds(at, rows), :] = jnp.where(swap_core, other, own)
-        keep_ref[pl.ds(at, rows), :] = jnp.where(swap_core, own, other)
-    width = send_buf.shape[1]
-    send = send_buf[...]
+def output_kernel(ds, begin, finish, w_ref, *rest):
+    count = 2 * len(ds)
+    blocks = [rest[2 * i : 2 * i + 2] for i in range(len(ds))]
+    rest = rest[count:]
+    total = output_part(ds, blocks, w_ref)
+    if not begin:
+        total = total + rest[0][...]
+        rest = rest[1:]
+    if not finish:
+        rest[0][...] = total
+        return
+    keep_ref, code_ref = rest
+    rows, width = keep_ref.shape
+    own, other = total[:rows], total[rows:]
+    keep_own = jnp.full((rows, 1), (ids[0] == ids[3]).astype(I32), I32) == 1
+    keep_ref[...] = jnp.where(keep_own, own, other)
+    send = jnp.where(keep_own, other, own)
     power = power_of(jnp.max(jnp.abs(send), axis=0, keepdims=True))
-    code_ref[: 2 * rows, :] = jnp.round(send * (jnp.exp2(-power) * CODE_TOP)).astype(I32).astype(I16)
-    code_ref[2 * rows :, :] = jnp.broadcast_to(power, (TAIL, width)).astype(I32).astype(I16)
-
-
-def finish_kernel(keep_ref, got_ref, text_ref, out_ref):
-    rows = out_ref.shape[0]
-    at = pl.multiple_of(ids[3] * rows, rows)
-    scale = jnp.exp2(got_ref[rows:, :].astype(I32).astype(F32)[:1]) * (1.0 / CODE_TOP)
-    total = keep_ref[...] + got_ref[:rows, :].astype(I32).astype(F32) * scale
-    out_ref[...] = (text_ref[pl.ds(at, rows), :].astype(F32) + total).astype(BF16)
+    code_ref[:rows, :] = jnp.round(send * (jnp.exp2(-power) * CODE_TOP)).astype(I32).astype(I16)
+    code_ref[rows:, :] = jnp.broadcast_to(power, (TAIL, width)).astype(I32).astype(I16)
+
+
+def finish_kernel(keep_near, got_near, keep_far, got_far, text_ref, out_ref):
+    half = out_ref.shape[0]
+    rows = half // 2
+    for far, (keep_ref, got_ref) in enumerate(((keep_near, got_near), (keep_far, got_far))):
+        at = pl.multiple_of((ids[1] ^ far) * rows, rows)
+        scale = jnp.exp2(got_ref[rows:, :].astype(I32).astype(F32)[:1]) * (1.0 / CODE_TOP)
+        total = keep_ref[...] + got_ref[:rows, :].astype(I32).astype(F32) * scale
+        text = text_ref[pl.ds(pl.multiple_of(ids[3] * half + at, rows), rows), :]
+        out_ref[pl.ds(at, rows), :] = (text.astype(F32) + total).astype(BF16)
 
 
 def fast_shards(text_states, q_weight, q_gain, key_cache, value_cache, block_mask, lengths, o_weight):
@@ -406,7 +408,9 @@
         previous = res
         outs[rel] = swap(res, rel) if rel else res
     attended = call(
-        functools.partial(merge_kernel, heads), struct((rows, width), BF16), (*outs[0], outs[1], outs[2], outs[3])
+        functools.partial(merge_kernel, heads),
+        struct((rows, width), BF16),
+        (*outs[0], outs[1], outs[2], outs[3]),
     )
 
     column = {d: turn(attended, 4 * d) if d else attended for d in order}
@@ -430,21 +434,31 @@
     moved = moved + end
     for i, d in enumerate(reversed(late)):
         blocks[d] = (column[d], beside[d], moved[2 * i], moved[2 * i + 1])
-    before = call(
-        functools.partial(output_first_kernel, early),
-        struct((text_rows, out_cols), F32),
-        (o_weight, *[b for d in early for b in blocks[d]]),
-        flops=2 * text_rows * width * len(early) * out_cols,
-    )
-    kept, code = call(
-        functools.partial(output_last_kernel, late),
-        (struct((half, out_cols), F32), struct((half + TAIL, out_cols), I16)),
-        (o_weight, before, *[b for d in late for b in blocks[d]]),
-        flops=2 * text_rows * width * len(late) * out_cols,
-        scratch=[pltpu.VMEM((half, out_cols), F32)],
-    )
-    got = lax.ppermute(code, ("head", "tp"), [(0, 1), (1, 0)])
-    return call(finish_kernel, struct((half, out_cols), BF16), (kept, got, text_states))
+    near = {d: (blocks[d][0], blocks[d][2]) for d in range(groups)}
+    far = {d: (blocks[d][1], blocks[d][3]) for d in range(groups)}
+
+    def output(ds, rows_of, begin, finish, *before):
+        done = (struct((rows, out_cols), F32), struct((rows + TAIL, out_cols), I16))
+        return call(
+            functools.partial(output_kernel, ds, begin, finish),
+            done if finish else struct((2 * rows, out_cols), F32),
+            (o_weight, *[b for d in ds for b in rows_of[d]], *before),
+            flops=4 * rows * width * len(ds) * out_cols,
+        )
+
+    def trade(code):
+        return lax.ppermute(code, ("head", "tp"), [(0, 1), (1, 0)])
+
+    before = output([d for d in range(groups) if d != tail_d], far, True, False)
+    keep_near, code = output(list(range(groups)), near, True, True)
+    got_near = trade(code)
+    keep_far, code = output([tail_d], far, False, True, before)
+    got_far = trade(code)
+    return call(
+        finish_kernel,
+        struct((half, out_cols), BF16),
+        (keep_near, got_near, keep_far, got_far, text_states),
+    )
 
 
 def plain_shards(

time: 103 us -> 104 us (level)
    ppermute x1 -> x2, starting transfers between devices: 1.58 us -> 2.16 us  [trade(): return lax.ppermute(code, ('head', 'tp'), [(0, 1), (1, 0)])]
    ppermute x1 -> x2, waiting for transfers between devices: 4.39 us -> 3.92 us  [trade(): return lax.ppermute(code, ('head', 'tp'), [(0, 1), (1, 0)])]
    pallas_call x22 -> x23, Pallas kernels: 19.3 us -> 19.5 us  [call(): pl.pallas_call(kernel, out_shape=out_shape, in_specs=specs or [VM] * len(...]
  transfers between devices with their start and end apart: 29 -> 30, of which waited for: 15 -> 16; matrix products, arithmetic and copies ran while one was open for 0% -> 0% of each run, Pallas kernels for 12% -> 12%
where the time goes in v2:
time: 104 us; the launch traced here: 103 us
  waiting for transfers between devices  50.5 us (49%)
  starting transfers between devices  32.9 us (32%)
  Pallas kernels  19.5 us (19%)
    ppermute x25, waiting for transfers between devices, swap(): return lax.ppermute(value, 'ctx', [(i, i ^ bits) for i in range(ctx)])  39.3 us
    ppermute x25, starting transfers between devices, swap(): return lax.ppermute(value, 'ctx', [(i, i ^ bits) for i in range(ctx)])  26.7 us
    pallas_call x23, Pallas kernels, call(): pl.pallas_call(kernel, out_shape=out_shape, in_specs=specs or [VM] * len(...  19.5 us
    ppermute x3, waiting for transfers between devices, turn(): lax.ppermute(value, 'ctx', [(i, (i + shift) % ctx) for i in range(ctx)])  7.3 us
    ppermute x3, starting transfers between devices, turn(): lax.ppermute(value, 'ctx', [(i, (i + shift) % ctx) for i in range(ctx)])  4.03 us
    ppermute x2, waiting for transfers between devices, trade(): return lax.ppermute(code, ('head', 'tp'), [(0, 1), (1, 0)])  3.92 us
    ppermute x2, starting transfers between devices, trade(): return lax.ppermute(code, ('head', 'tp'), [(0, 1), (1, 0)])  2.16 us
  transfers between devices with their start and end apart: 30, of which 16 were waited for; matrix products, arithmetic and copies ran while one was open for 0% of the time, Pallas kernels for 12%

profile of v2, /device:TPU:0, one launch (start us, length us, event | category | flops | bytes accessed | tf_op | source)
XLA Modules:
  0.0 103.4 jit_solution(12333900289768162191)
XLA Ops:
  0.0 3.4 %shard_map.82 = (f32[128,1024]{1,0:T(8,128)S(1)}, f32[128,1024]{1,0:T(8,128)S(1)}, f32[128,3072]{1,0:T(8,128)S(1)}, f32[128,3072]{1,0:T(8,128)S(1)}, bf16[1040,1...) custom-call(bf16[256,512]{1,0:T(8,128)(2,1)} %text_ref.1, ...), custom_call_target="tpu_custom_call" | custom-call | flops 1073741824 | bytes 10766336 | tf_op jit(solution)/shard_map/pallas_call | solution.py:39
  3.4 0.6 collective-permute-start
  4.0 0.1 collective-permute-start.6
  4.1 3.7 %collective-permute-done.6.got_ref = f32[128,1024]{1,0:T(8,128)S(1)} collective-permute-done((f32[128,1024]{1,0:T(8,128)S(1)}, f32[128,1024]{1,0:T(8,128)S(1)}, u32[]{:S(2)}, u32[]{:S(2)}) %collective-permute-start.6) | collective-permute-done | bytes 524320 | tf_op jit(solution)/shard_map/ppermute | solution.py:332
  7.8 0.3 shard_map.89
  8.1 2.9 %collective-permute-start.7 = (s16[528,128]{1,0:T(8,128)(2,1)S(1)}, s16[528,128]{1,0:T(8,128)(2,1)S(1)}, u32[]{:S(2)}, u32[]{:S(2)}) collective-permute-start(s16[528,128]{1,0:T(8,128)(2,1)S(1)} %get-tuple-element.53), channel_id=1, source_target_pairs={{0,4},{2,6},{4,0},{6,2},{8,12},{10,14},{12,8},{14,10},{16,20},{18,... | collective-permute-start | bytes 405512 | tf_op jit(solution)/shard_map/ppermute | solution.py:332
  11.0 0.4 shard_map.87
  11.4 0.1 collective-permute-start.4
  11.5 0.4 shard_map.85
  11.9 2.1 %collective-permute-start.2 = (s16[528,128]{1,0:T(8,128)(2,1)S(1)}, s16[528,128]{1,0:T(8,128)(2,1)S(1)}, u32[]{:S(2)}, u32[]{:S(2)}) collective-permute-start(s16[528,128]{1,0:T(8,128)(2,1)S(1)} %get-tuple-element.47), channel_id=1, source_target_pairs={{0,4},{2,6},{4,0},{6,2},{8,12},{10,14},{12,8},{14,10},{16,20},{18,... | collective-permute-start | bytes 405512 | tf_op jit(solution)/shard_map/ppermute | solution.py:332
  13.9 1.6 %collective-permute-done.7.got_ref = s16[528,128]{1,0:T(8,128)(2,1)S(1)} collective-permute-done((s16[528,128]{1,0:T(8,128)(2,1)S(1)}, s16[528,128]{1,0:T(8,128)(2,1)S(1)}, u32[]{:S(2)}, u32[]{:S(2)}) %collective-permute-start.7) | collective-permute-done | bytes 135200 | tf_op jit(solution)/shard_map/ppermute | solution.py:332
  15.5 0.5 shard_map.90
  16.0 4.2 %collective-permute-start.8 = (s16[528,128]{1,0:T(8,128)(2,1)S(1)}, s16[528,128]{1,0:T(8,128)(2,1)S(1)}, u32[]{:S(2)}, u32[]{:S(2)}) collective-permute-start(s16[528,128]{1,0:T(8,128)(2,1)S(1)} %shard_map.90), channel_id=1, source_target_pairs={{0,24},{2,26},{4,28},{6,30},{8,16},{10,18},{12,20},{14,22},{16,8},... | collective-permute-start | bytes 405512 | tf_op jit(solution)/shard_map/ppermute | solution.py:332
  20.2 0.9 collective-permute-start.13
  21.1 0.4 shard_map.83
  21.5 1.6 %collective-permute-start.1 = (s16[528,128]{1,0:T(8,128)(2,1)S(1)}, s16[528,128]{1,0:T(8,128)(2,1)S(1)}, u32[]{:S(2)}, u32[]{:S(2)}) collective-permute-start(s16[528,128]{1,0:T(8,128)(2,1)S(1)} %get-tuple-element.45), channel_id=1, source_target_pairs={{0,4},{2,6},{4,0},{6,2},{8,12},{10,14},{12,8},{14,10},{16,20},{18,... | collective-permute-start | bytes 405512 | tf_op jit(solution)/shard_map/ppermute | solution.py:332
  23.0 0.5 shard_map.88
  23.6 2.7 %collective-permute-start.5 = (s16[528,128]{1,0:T(8,128)(2,1)S(1)}, s16[528,128]{1,0:T(8,128)(2,1)S(1)}, u32[]{:S(2)}, u32[]{:S(2)}) collective-permute-start(s16[528,128]{1,0:T(8,128)(2,1)S(1)} %shard_map.88), channel_id=1, source_target_pairs={{0,16},{2,18},{4,20},{6,22},{8,24},{10,26},{12,28},{14,30},{16,0},... | collective-permute-start | bytes 405512 | tf_op jit(solution)/shard_map/ppermute | solution.py:332
  26.2 0.5 shard_map.86
  26.7 1.0 collective-permute-start.3
  27.7 1.4 %collective-permute-start.14 = (bf16[1040,128]{1,0:T(8,128)(2,1)S(1)}, bf16[1040,128]{1,0:T(8,128)(2,1)S(1)}, u32[]{:S(2)}, u32[]{:S(2)}) collective-permute-start(bf16[1040,128]{1,0:T(8,128)(2,1)S(1)} %get-tuple-element.69), channel_id=1, source_target_pairs={{0,16},{2,18},{4,20},{6,22},{8,24},{10,26},{12,28},{14,30},{16,0},... | collective-permute-start | bytes 798728 | tf_op jit(solution)/shard_map/ppermute | solution.py:332
  29.1 0.3 shard_map.84.own_ref
  29.4 19.0 %collective-permute-done.5.rest_1_ = s16[528,128]{1,0:T(8,128)(2,1)S(1)} collective-permute-done((s16[528,128]{1,0:T(8,128)(2,1)S(1)}, s16[528,128]{1,0:T(8,128)(2,1)S(1)}, u32[]{:S(2)}, u32[]{:S(2)}) %collective-permute-start.5) | collective-permute-done | bytes 135200 | tf_op jit(solution)/shard_map/ppermute | solution.py:332
  48.4 1.0 shard_map.91.q_ref
  49.4 0.1 collective-permute-start.9
  49.5 1.4 %collective-permute-start.11 = (bf16[64,1024]{1,0:T(8,128)(2,1)S(1)}, bf16[64,1024]{1,0:T(8,128)(2,1)S(1)}, u32[]{:S(2)}, u32[]{:S(2)}) collective-permute-start(bf16[64,1024]{1,0:T(8,128)(2,1)S(1)} %shard_map.91.q_ref), channel_id=1, source_target_pairs={{0,4},{2,6},{4,0},{6,2},{8,12},{10,14},{12,8},{14,10},{16,20},{18,... | collective-permute-start | bytes 393224 | tf_op jit(solution)/shard_map/ppermute | solution.py:332
  50.9 0.4 collective-permute-start.10
  51.3 1.6 %shard_map.92 = (f32[128,512]{1,0:T(8,128)S(1)}, f32[8,512]{1,0:T(8,128)S(1)}) custom-call(bf16[64,1024]{1,0:T(8,128)(2,1)S(1)} %shard_map.91.q_ref, s32[2,128]{1,0:T(2,128)S(1)} %bitcast.31, bf16[1040,128]{1,0:T(8,128)(2,1)S(1)} %get-tuple-element.54.rest_0_, bf16[1040,128]{1,0:T(8,128)(2,1)S(1)} %collective-permute-done.12.rest_1_, ...), custom_call_target="tpu_custom_call" | custom-call | flops 402653184 | bytes 1209344 | tf_op jit(solution)/shard_map/pallas_call | solution.py:39
  52.9 1.6 %shard_map.93 = (f32[128,512]{1,0:T(8,128)S(1)}, f32[8,512]{1,0:T(8,128)S(1)}) custom-call(bf16[64,1024]{1,0:T(8,128)(2,1)S(1)} %collective-permute-done.9.q_ref, s32[2,128]{1,0:T(2,128)S(1)} %bitcast.32, bf16[1040,128]{1,0:T(8,128)(2,1)S(1)} %get-tuple-element.54.rest_0_, bf16[1040,128]{1,0:T(8,128)(2,1)S(1)} %collective-permute-done.12.rest_1_, ...), custom_call_target="tpu_custom_call" | custom-call | flops 402653184 | bytes 1209344 | tf_op jit(solution)/shard_map/pallas_call | solution.py:39
  54.6 1.3 %collective-permute-done.11.q_ref = bf16[64,1024]{1,0:T(8,128)(2,1)S(1)} collective-permute-done((bf16[64,1024]{1,0:T(8,128)(2,1)S(1)}, bf16[64,1024]{1,0:T(8,128)(2,1)S(1)}, u32[]{:S(2)}, u32[]{:S(2)}) %collective-permute-start.11) | collective-permute-done | bytes 131104 | tf_op jit(solution)/shard_map/ppermute | solution.py:332
  55.9 1.6 %shard_map.94 = (f32[128,512]{1,0:T(8,128)S(1)}, f32[8,512]{1,0:T(8,128)S(1)}) custom-call(bf16[64,1024]{1,0:T(8,128)(2,1)S(1)} %collective-permute-done.11.q_ref, s32[2,128]{1,0:T(2,128)S(1)} %bitcast.33, bf16[1040,128]{1,0:T(8,128)(2,1)S(1)} %get-tuple-element.54.rest_0_, bf16[1040,128]{1,0:T(8,128)(2,1)S(1)} %collective-permute-done.12.rest_1_, ...), custom_call_target="tpu_custom_call" | custom-call | flops 402653184 | bytes 1209344 | tf_op jit(solution)/shard_map/pallas_call | solution.py:39
  57.5 0.1 collective-permute-done.10.q_ref
  57.6 1.6 %shard_map.95 = (f32[128,512]{1,0:T(8,128)S(1)}, f32[8,512]{1,0:T(8,128)S(1)}) custom-call(bf16[64,1024]{1,0:T(8,128)(2,1)S(1)} %collective-permute-done.10.q_ref, s32[2,128]{1,0:T(2,128)S(1)} %bitcast.34, bf16[1040,128]{1,0:T(8,128)(2,1)S(1)} %get-tuple-element.54.rest_0_, bf16[1040,128]{1,0:T(8,128)(2,1)S(1)} %collective-permute-done.12.rest_1_, ...), custom_call_target="tpu_custom_call" | custom-call | flops 402653184 | bytes 1209344 | tf_op jit(solution)/shard_map/pallas_call | solution.py:39
  59.2 0.7 shard_map.96
  59.9 0.9 shard_map.97
  60.8 0.7 shard_map.98
  61.5 0.4 collective-permute-start.15
  62.0 1.1 %collective-permute-start.17 = (s16[144,512]{1,0:T(8,128)(2,1)S(1)}, s16[144,512]{1,0:T(8,128)(2,1)S(1)}, u32[]{:S(2)}, u32[]{:S(2)}) collective-permute-start(s16[144,512]{1,0:T(8,128)(2,1)S(1)} %shard_map.97), channel_id=1, source_target_pairs={{0,6},{2,4},{4,2},{6,0},{8,14},{10,12},{12,10},{14,8},{16,22},{18,... | collective-permute-start | bytes 442376 | tf_op jit(solution)/shard_map/ppermute | solution.py:332
  63.1 0.6 collective-permute-start.16
  63.7 0.6 shard_map.99
  64.4 3.4 %collective-permute-done.17.rest_2_ = s16[144,512]{1,0:T(8,128)(2,1)S(1)} collective-permute-done((s16[144,512]{1,0:T(8,128)(2,1)S(1)}, s16[144,512]{1,0:T(8,128)(2,1)S(1)}, u32[]{:S(2)}, u32[]{:S(2)}) %collective-permute-start.17) | collective-permute-done | bytes 147488 | tf_op jit(solution)/shard_map/ppermute | solution.py:332
  67.8 3.5 %collective-permute-done.16.rest_1_ = s16[144,512]{1,0:T(8,128)(2,1)S(1)} collective-permute-done((s16[144,512]{1,0:T(8,128)(2,1)S(1)}, s16[144,512]{1,0:T(8,128)(2,1)S(1)}, u32[]{:S(2)}, u32[]{:S(2)}) %collective-permute-start.16) | collective-permute-done | bytes 147488 | tf_op jit(solution)/shard_map/ppermute | solution.py:332
  71.3 0.2 shard_map.100.rest_0_
  71.5 3.4 %collective-permute-start.23 = (bf16[64,1024]{1,0:T(8,128)(2,1)S(1)}, bf16[64,1024]{1,0:T(8,128)(2,1)S(1)}, u32[]{:S(2)}, u32[]{:S(2)}) collective-permute-start(bf16[64,1024]{1,0:T(8,128)(2,1)S(1)} %shard_map.100.rest_0_), channel_id=1, source_target_pairs={{0,24},{2,26},{4,28},{6,30},{8,0},{10,2},{12,4},{14,6},{16,8},{18,... | collective-permute-start | bytes 393224 | tf_op jit(solution)/shard_map/ppermute | solution.py:335
  74.9 0.6 collective-permute-start.22
  75.5 3.3 %collective-permute-done.23.rest_6_ = bf16[64,1024]{1,0:T(8,128)(2,1)S(1)} collective-permute-done((bf16[64,1024]{1,0:T(8,128)(2,1)S(1)}, bf16[64,1024]{1,0:T(8,128)(2,1)S(1)}, u32[]{:S(2)}, u32[]{:S(2)}) %collective-permute-start.23) | collective-permute-done | bytes 131104 | tf_op jit(solution)/shard_map/ppermute | solution.py:335
  78.8 1.5 %collective-permute-start.24 = (bf16[64,1024]{1,0:T(8,128)(2,1)S(1)}, bf16[64,1024]{1,0:T(8,128)(2,1)S(1)}, u32[]{:S(2)}, u32[]{:S(2)}) collective-permute-start(bf16[64,1024]{1,0:T(8,128)(2,1)S(1)} %collective-permute-done.23.rest_6_), channel_id=1, source_target_pairs={{0,4},{2,6},{4,0},{6,2},{8,12},{10,14},{12,8},{14,10},{16,20},{18,... | collective-permute-start | bytes 393224 | tf_op jit(solution)/shard_map/ppermute | solution.py:332
  80.3 0.5 collective-permute-start.18
  80.8 2.3 %collective-permute-done.19.rest_2_ = bf16[64,1024]{1,0:T(8,128)(2,1)S(1)} collective-permute-done((bf16[64,1024]{1,0:T(8,128)(2,1)S(1)}, bf16[64,1024]{1,0:T(8,128)(2,1)S(1)}, u32[]{:S(2)}, u32[]{:S(2)}) %collective-permute-start.19) | collective-permute-done | bytes 131104 | tf_op jit(solution)/shard_map/ppermute | solution.py:335
  83.1 1.5 %collective-permute-start.20 = (bf16[64,1024]{1,0:T(8,128)(2,1)S(1)}, bf16[64,1024]{1,0:T(8,128)(2,1)S(1)}, u32[]{:S(2)}, u32[]{:S(2)}) collective-permute-start(bf16[64,1024]{1,0:T(8,128)(2,1)S(1)} %collective-permute-done.19.rest_2_), channel_id=1, source_target_pairs={{0,4},{2,6},{4,0},{6,2},{8,12},{10,14},{12,8},{14,10},{16,20},{18,... | collective-permute-start | bytes 393224 | tf_op jit(solution)/shard_map/ppermute | solution.py:332
  84.6 1.7 %collective-permute-done.22.rest_4_ = bf16[64,1024]{1,0:T(8,128)(2,1)S(1)} collective-permute-done((bf16[64,1024]{1,0:T(8,128)(2,1)S(1)}, bf16[64,1024]{1,0:T(8,128)(2,1)S(1)}, u32[]{:S(2)}, u32[]{:S(2)}) %collective-permute-start.22) | collective-permute-done | bytes 131104 | tf_op jit(solution)/shard_map/ppermute | solution.py:335
  86.5 0.1 collective-permute-done.18.rest_0_
  86.6 1.5 %collective-permute-done.20.rest_2_ = bf16[64,1024]{1,0:T(8,128)(2,1)S(1)} collective-permute-done((bf16[64,1024]{1,0:T(8,128)(2,1)S(1)}, bf16[64,1024]{1,0:T(8,128)(2,1)S(1)}, u32[]{:S(2)}, u32[]{:S(2)}) %collective-permute-start.20) | collective-permute-done | bytes 131104 | tf_op jit(solution)/shard_map/ppermute | solution.py:332
  88.2 1.5 %collective-permute-start.27 = (bf16[64,1024]{1,0:T(8,128)(2,1)S(1)}, bf16[64,1024]{1,0:T(8,128)(2,1)S(1)}, u32[]{:S(2)}, u32[]{:S(2)}) collective-permute-start(bf16[64,1024]{1,0:T(8,128)(2,1)S(1)} %collective-permute-done.22.rest_4_), channel_id=1, source_target_pairs={{0,4},{2,6},{4,0},{6,2},{8,12},{10,14},{12,8},{14,10},{16,20},{18,... | collective-permute-start | bytes 393224 | tf_op jit(solution)/shard_map/ppermute | solution.py:332
  89.8 4.3 %collective-permute-done.27.rest_0_ = bf16[64,1024]{1,0:T(8,128)(2,1)S(1)} collective-permute-done((bf16[64,1024]{1,0:T(8,128)(2,1)S(1)}, bf16[64,1024]{1,0:T(8,128)(2,1)S(1)}, u32[]{:S(2)}, u32[]{:S(2)}) %collective-permute-start.27) | collective-permute-done | bytes 131104 | tf_op jit(solution)/shard_map/ppermute | solution.py:332
  94.2 0.6 shard_map.102.rest_2_
  94.8 0.6 collective-permute-done.28.rest_1_
  95.5 0.4 shard_map.103
  95.8 1.6 %collective-permute-start.29 = (s16[80,512]{1,0:T(8,128)(2,1)S(1)}, s16[80,512]{1,0:T(8,128)(2,1)S(1)}, u32[]{:S(2)}, u32[]{:S(2)}) collective-permute-start(s16[80,512]{1,0:T(8,128)(2,1)S(1)} %get-tuple-element.78), channel_id=1, source_target_pairs={{0,1},{1,0},{2,3},{3,2},{4,5},{5,4},{6,7},{7,6},{8,9},{9,8},{10,11... | collective-permute-start | bytes 245768 | tf_op jit(solution)/shard_map/ppermute | solution.py:450
  97.4 0.8 shard_map.101
  98.2 0.6 collective-permute-start.26
  98.8 1.6 %collective-permute-done.29.got_far = s16[80,512]{1,0:T(8,128)(2,1)S(1)} collective-permute-done((s16[80,512]{1,0:T(8,128)(2,1)S(1)}, s16[80,512]{1,0:T(8,128)(2,1)S(1)}, u32[]{:S(2)}, u32[]{:S(2)}) %collective-permute-start.29) | collective-permute-done | bytes 81952 | tf_op jit(solution)/shard_map/ppermute | solution.py:450
  100.4 2.3 %collective-permute-done.26.got_near = s16[80,512]{1,0:T(8,128)(2,1)S(1)} collective-permute-done((s16[80,512]{1,0:T(8,128)(2,1)S(1)}, s16[80,512]{1,0:T(8,128)(2,1)S(1)}, u32[]{:S(2)}, u32[]{:S(2)}) %collective-permute-start.26) | collective-permute-done | bytes 81952 | tf_op jit(solution)/shard_map/ppermute | solution.py:450
  102.7 0.7 shard_map.104
  (31 shorter events, 0.4 us)
Async XLA Ops:
  3.4 7.6 %collective-permute-start = (f32[128,3072]{1,0:T(8,128)S(1)}, f32[128,3072]{1,0:T(8,128)S(1)}, u32[]{:S(2)}, u32[]{:S(2)}) collective-permute-start(f32[128,3072]{1,0:T(8,128)S(1)} %get-tuple-element.43), channel_id=1, source_target_pairs={{0,2},{2,0},{4,6},{6,4},{8,10},{10,8},{12,14},{14,12},{16,18},{18,... | collective-permute-start | bytes 4718600 | tf_op jit(solution)/shard_map/ppermute | solution.py:332
  4.0 3.8 %collective-permute-start.6 = (f32[128,1024]{1,0:T(8,128)S(1)}, f32[128,1024]{1,0:T(8,128)S(1)}, u32[]{:S(2)}, u32[]{:S(2)}) collective-permute-start(f32[128,1024]{1,0:T(8,128)S(1)} %get-tuple-element.51), channel_id=1, source_target_pairs={{0,2},{2,0},{4,6},{6,4},{8,10},{10,8},{12,14},{14,12},{16,18},{18,... | collective-permute-start | bytes 1572872 | tf_op jit(solution)/shard_map/ppermute | solution.py:332
  8.1 7.4 %collective-permute-start.7 = (s16[528,128]{1,0:T(8,128)(2,1)S(1)}, s16[528,128]{1,0:T(8,128)(2,1)S(1)}, u32[]{:S(2)}, u32[]{:S(2)}) collective-permute-start(s16[528,128]{1,0:T(8,128)(2,1)S(1)} %get-tuple-element.53), channel_id=1, source_target_pairs={{0,4},{2,6},{4,0},{6,2},{8,12},{10,14},{12,8},{14,10},{16,20},{18,... | collective-permute-start | bytes 405512 | tf_op jit(solution)/shard_map/ppermute | solution.py:332
  11.4 10.1 %collective-permute-start.4 = (s16[528,128]{1,0:T(8,128)(2,1)S(1)}, s16[528,128]{1,0:T(8,128)(2,1)S(1)}, u32[]{:S(2)}, u32[]{:S(2)}) collective-permute-start(s16[528,128]{1,0:T(8,128)(2,1)S(1)} %get-tuple-element.49), channel_id=1, source_target_pairs={{0,4},{2,6},{4,0},{6,2},{8,12},{10,14},{12,8},{14,10},{16,20},{18,... | collective-permute-start | bytes 405512 | tf_op jit(solution)/shard_map/ppermute | solution.py:332
  11.9 11.7 %collective-permute-start.2 = (s16[528,128]{1,0:T(8,128)(2,1)S(1)}, s16[528,128]{1,0:T(8,128)(2,1)S(1)}, u32[]{:S(2)}, u32[]{:S(2)}) collective-permute-start(s16[528,128]{1,0:T(8,128)(2,1)S(1)} %get-tuple-element.47), channel_id=1, source_target_pairs={{0,4},{2,6},{4,0},{6,2},{8,12},{10,14},{12,8},{14,10},{16,20},{18,... | collective-permute-start | bytes 405512 | tf_op jit(solution)/shard_map/ppermute | solution.py:332
  16.0 10.7 %collective-permute-start.8 = (s16[528,128]{1,0:T(8,128)(2,1)S(1)}, s16[528,128]{1,0:T(8,128)(2,1)S(1)}, u32[]{:S(2)}, u32[]{:S(2)}) collective-permute-start(s16[528,128]{1,0:T(8,128)(2,1)S(1)} %shard_map.90), channel_id=1, source_target_pairs={{0,24},{2,26},{4,28},{6,30},{8,16},{10,18},{12,20},{14,22},{16,8},... | collective-permute-start | bytes 405512 | tf_op jit(solution)/shard_map/ppermute | solution.py:332
  20.2 30.7 %collective-permute-start.12 = (bf16[1040,128]{1,0:T(8,128)(2,1)S(1)}, bf16[1040,128]{1,0:T(8,128)(2,1)S(1)}, u32[]{:S(2)}, u32[]{:S(2)}) collective-permute-start(bf16[1040,128]{1,0:T(8,128)(2,1)S(1)} %get-tuple-element.55), channel_id=1, source_target_pairs={{0,8},{2,10},{4,12},{6,14},{8,0},{10,2},{12,4},{14,6},{16,24},{18,... | collective-permute-start | bytes 798728 | tf_op jit(solution)/shard_map/ppermute | solution.py:332
  20.2 31.1 %collective-permute-start.13 = (bf16[1040,128]{1,0:T(8,128)(2,1)S(1)}, bf16[1040,128]{1,0:T(8,128)(2,1)S(1)}, u32[]{:S(2)}, u32[]{:S(2)}) collective-permute-start(bf16[1040,128]{1,0:T(8,128)(2,1)S(1)} %get-tuple-element.56), channel_id=1, source_target_pairs={{0,24},{2,26},{4,28},{6,30},{8,16},{10,18},{12,20},{14,22},{16,8},... | collective-permute-start | bytes 798728 | tf_op jit(solution)/shard_map/ppermute | solution.py:332
  21.4 27.0 %copy-start.3 = (f32[128]{0:T(128)S(1)}, f32[128]{0:T(128)}, u32[]{:S(2)}) copy-start(f32[128]{0:T(128)} %param.10) | copy-start | bytes 1540
  21.5 29.9 %copy-start.2 = (s32[256]{0:T(256)S(1)}, s32[256]{0:T(256)}, u32[]{:S(2)}) copy-start(s32[256]{0:T(256)} %param.14) | copy-start | bytes 3076
  21.5 6.2 %collective-permute-start.1 = (s16[528,128]{1,0:T(8,128)(2,1)S(1)}, s16[528,128]{1,0:T(8,128)(2,1)S(1)}, u32[]{:S(2)}, u32[]{:S(2)}) collective-permute-start(s16[528,128]{1,0:T(8,128)(2,1)S(1)} %get-tuple-element.45), channel_id=1, source_target_pairs={{0,4},{2,6},{4,0},{6,2},{8,12},{10,14},{12,8},{14,10},{16,20},{18,... | collective-permute-start | bytes 405512 | tf_op jit(solution)/shard_map/ppermute | solution.py:332
  23.6 24.8 %collective-permute-start.5 = (s16[528,128]{1,0:T(8,128)(2,1)S(1)}, s16[528,128]{1,0:T(8,128)(2,1)S(1)}, u32[]{:S(2)}, u32[]{:S(2)}) collective-permute-start(s16[528,128]{1,0:T(8,128)(2,1)S(1)} %shard_map.88), channel_id=1, source_target_pairs={{0,16},{2,18},{4,20},{6,22},{8,24},{10,26},{12,28},{14,30},{16,0},... | collective-permute-start | bytes 405512 | tf_op jit(solution)/shard_map/ppermute | solution.py:332
  26.7 21.7 %collective-permute-start.3 = (s16[528,128]{1,0:T(8,128)(2,1)S(1)}, s16[528,128]{1,0:T(8,128)(2,1)S(1)}, u32[]{:S(2)}, u32[]{:S(2)}) collective-permute-start(s16[528,128]{1,0:T(8,128)(2,1)S(1)} %shard_map.86), channel_id=1, source_target_pairs={{0,8},{2,10},{4,12},{6,14},{8,0},{10,2},{12,4},{14,6},{16,24},{18,... | collective-permute-start | bytes 405512 | tf_op jit(solution)/shard_map/ppermute | solution.py:332
  27.7 31.5 %collective-permute-start.14 = (bf16[1040,128]{1,0:T(8,128)(2,1)S(1)}, bf16[1040,128]{1,0:T(8,128)(2,1)S(1)}, u32[]{:S(2)}, u32[]{:S(2)}) collective-permute-start(bf16[1040,128]{1,0:T(8,128)(2,1)S(1)} %get-tuple-element.69), channel_id=1, source_target_pairs={{0,16},{2,18},{4,20},{6,22},{8,24},{10,26},{12,28},{14,30},{16,0},... | collective-permute-start | bytes 798728 | tf_op jit(solution)/shard_map/ppermute | solution.py:332
  49.4 3.6 %collective-permute-start.9 = (bf16[64,1024]{1,0:T(8,128)(2,1)S(1)}, bf16[64,1024]{1,0:T(8,128)(2,1)S(1)}, u32[]{:S(2)}, u32[]{:S(2)}) collective-permute-start(bf16[64,1024]{1,0:T(8,128)(2,1)S(1)} %shard_map.91.q_ref), channel_id=1, source_target_pairs={{0,2},{2,0},{4,6},{6,4},{8,10},{10,8},{12,14},{14,12},{16,18},{18,... | collective-permute-start | bytes 393224 | tf_op jit(solution)/shard_map/ppermute | solution.py:332
  49.5 6.4 %collective-permute-start.11 = (bf16[64,1024]{1,0:T(8,128)(2,1)S(1)}, bf16[64,1024]{1,0:T(8,128)(2,1)S(1)}, u32[]{:S(2)}, u32[]{:S(2)}) collective-permute-start(bf16[64,1024]{1,0:T(8,128)(2,1)S(1)} %shard_map.91.q_ref), channel_id=1, source_target_pairs={{0,4},{2,6},{4,0},{6,2},{8,12},{10,14},{12,8},{14,10},{16,20},{18,... | collective-permute-start | bytes 393224 | tf_op jit(solution)/shard_map/ppermute | solution.py:332
  50.9 6.7 %collective-permute-start.10 = (bf16[64,1024]{1,0:T(8,128)(2,1)S(1)}, bf16[64,1024]{1,0:T(8,128)(2,1)S(1)}, u32[]{:S(2)}, u32[]{:S(2)}) collective-permute-start(bf16[64,1024]{1,0:T(8,128)(2,1)S(1)} %shard_map.91.q_ref), channel_id=1, source_target_pairs={{0,6},{2,4},{4,2},{6,0},{8,14},{10,12},{12,10},{14,8},{16,22},{18,... | collective-permute-start | bytes 393224 | tf_op jit(solution)/shard_map/ppermute | solution.py:332
  61.5 2.9 %collective-permute-start.15 = (s16[144,512]{1,0:T(8,128)(2,1)S(1)}, s16[144,512]{1,0:T(8,128)(2,1)S(1)}, u32[]{:S(2)}, u32[]{:S(2)}) collective-permute-start(s16[144,512]{1,0:T(8,128)(2,1)S(1)} %shard_map.98), channel_id=1, source_target_pairs={{0,2},{2,0},{4,6},{6,4},{8,10},{10,8},{12,14},{14,12},{16,18},{18,... | collective-permute-start | bytes 442376 | tf_op jit(solution)/shard_map/ppermute | solution.py:332
  62.0 5.8 %collective-permute-start.17 = (s16[144,512]{1,0:T(8,128)(2,1)S(1)}, s16[144,512]{1,0:T(8,128)(2,1)S(1)}, u32[]{:S(2)}, u32[]{:S(2)}) collective-permute-start(s16[144,512]{1,0:T(8,128)(2,1)S(1)} %shard_map.97), channel_id=1, source_target_pairs={{0,6},{2,4},{4,2},{6,0},{8,14},{10,12},{12,10},{14,8},{16,22},{18,... | collective-permute-start | bytes 442376 | tf_op jit(solution)/shard_map/ppermute | solution.py:332
  63.1 8.2 %collective-permute-start.16 = (s16[144,512]{1,0:T(8,128)(2,1)S(1)}, s16[144,512]{1,0:T(8,128)(2,1)S(1)}, u32[]{:S(2)}, u32[]{:S(2)}) collective-permute-start(s16[144,512]{1,0:T(8,128)(2,1)S(1)} %shard_map.96), channel_id=1, source_target_pairs={{0,4},{2,6},{4,0},{6,2},{8,12},{10,14},{12,8},{14,10},{16,20},{18,... | collective-permute-start | bytes 442376 | tf_op jit(solution)/shard_map/ppermute | solution.py:332
  71.3 23.0 %copy-start = (bf16[4096,512]{1,0:T(8,128)(2,1)S(1)}, bf16[4096,512]{1,0:T(8,128)(2,1)}, u32[]{:S(2)}) copy-start(bf16[4096,512]{1,0:T(8,128)(2,1)} %w_ref.5) | copy-start | bytes 12582916
  71.5 7.3 %collective-permute-start.23 = (bf16[64,1024]{1,0:T(8,128)(2,1)S(1)}, bf16[64,1024]{1,0:T(8,128)(2,1)S(1)}, u32[]{:S(2)}, u32[]{:S(2)}) collective-permute-start(bf16[64,1024]{1,0:T(8,128)(2,1)S(1)} %shard_map.100.rest_0_), channel_id=1, source_target_pairs={{0,24},{2,26},{4,28},{6,30},{8,0},{10,2},{12,4},{14,6},{16,8},{18,... | collective-permute-start | bytes 393224 | tf_op jit(solution)/shard_map/ppermute | solution.py:335
  74.9 8.2 %collective-permute-start.19 = (bf16[64,1024]{1,0:T(8,128)(2,1)S(1)}, bf16[64,1024]{1,0:T(8,128)(2,1)S(1)}, u32[]{:S(2)}, u32[]{:S(2)}) collective-permute-start(bf16[64,1024]{1,0:T(8,128)(2,1)S(1)} %shard_map.100.rest_0_), channel_id=1, source_target_pairs={{0,8},{2,10},{4,12},{6,14},{8,16},{10,18},{12,20},{14,22},{16,24},... | collective-permute-start | bytes 393224 | tf_op jit(solution)/shard_map/ppermute | solution.py:335
  74.9 11.4 %collective-permute-start.22 = (bf16[64,1024]{1,0:T(8,128)(2,1)S(1)}, bf16[64,1024]{1,0:T(8,128)(2,1)S(1)}, u32[]{:S(2)}, u32[]{:S(2)}) collective-permute-start(bf16[64,1024]{1,0:T(8,128)(2,1)S(1)} %shard_map.100.rest_0_), channel_id=1, source_target_pairs={{0,16},{2,18},{4,20},{6,22},{8,24},{10,26},{12,28},{14,30},{16,0},... | collective-permute-start | bytes 393224 | tf_op jit(solution)/shard_map/ppermute | solution.py:335
  78.8 7.6 %collective-permute-start.24 = (bf16[64,1024]{1,0:T(8,128)(2,1)S(1)}, bf16[64,1024]{1,0:T(8,128)(2,1)S(1)}, u32[]{:S(2)}, u32[]{:S(2)}) collective-permute-start(bf16[64,1024]{1,0:T(8,128)(2,1)S(1)} %collective-permute-done.23.rest_6_), channel_id=1, source_target_pairs={{0,4},{2,6},{4,0},{6,2},{8,12},{10,14},{12,8},{14,10},{16,20},{18,... | collective-permute-start | bytes 393224 | tf_op jit(solution)/shard_map/ppermute | solution.py:332
  80.3 6.3 %collective-permute-start.18 = (bf16[64,1024]{1,0:T(8,128)(2,1)S(1)}, bf16[64,1024]{1,0:T(8,128)(2,1)S(1)}, u32[]{:S(2)}, u32[]{:S(2)}) collective-permute-start(bf16[64,1024]{1,0:T(8,128)(2,1)S(1)} %shard_map.100.rest_0_), channel_id=1, source_target_pairs={{0,4},{2,6},{4,0},{6,2},{8,12},{10,14},{12,8},{14,10},{16,20},{18,... | collective-permute-start | bytes 393224 | tf_op jit(solution)/shard_map/ppermute | solution.py:332
  83.1 5.0 %collective-permute-start.20 = (bf16[64,1024]{1,0:T(8,128)(2,1)S(1)}, bf16[64,1024]{1,0:T(8,128)(2,1)S(1)}, u32[]{:S(2)}, u32[]{:S(2)}) collective-permute-start(bf16[64,1024]{1,0:T(8,128)(2,1)S(1)} %collective-permute-done.19.rest_2_), channel_id=1, source_target_pairs={{0,4},{2,6},{4,0},{6,2},{8,12},{10,14},{12,8},{14,10},{16,20},{18,... | collective-permute-start | bytes 393224 | tf_op jit(solution)/shard_map/ppermute | solution.py:332
  86.4 7.8 %collective-permute-start.25 = (bf16[3,64,1024]{2,1,0:T(8,128)(2,1)S(1)}, bf16[3,64,1024]{2,1,0:T(8,128)(2,1)S(1)}, u32[]{:S(2)}, u32[]{:S(2)}) collective-permute-start(bf16[3,64,1024]{2,1,0:T(8,128)(2,1)S(1)} %pad_maximum_fusion.1), channel_id=1, source_target_pairs={{0,2},{2,0},{4,6},{6,4},{8,10},{10,8},{12,14},{14,12},{16,18},{18,... | collective-permute-start | bytes 1179656 | tf_op jit(solution)/shard_map/ppermute | solution.py:332
  88.2 6.0 %collective-permute-start.21 = (bf16[4,64,1024]{2,1,0:T(8,128)(2,1)S(1)}, bf16[4,64,1024]{2,1,0:T(8,128)(2,1)S(1)}, u32[]{:S(2)}, u32[]{:S(2)}) collective-permute-start(bf16[4,64,1024]{2,1,0:T(8,128)(2,1)S(1)} %pad_maximum_fusion), channel_id=1, source_target_pairs={{0,2},{2,0},{4,6},{6,4},{8,10},{10,8},{12,14},{14,12},{16,18},{18,... | collective-permute-start | bytes 1572872 | tf_op jit(solution)/shard_map/ppermute | solution.py:332
  88.2 5.9 %collective-permute-start.27 = (bf16[64,1024]{1,0:T(8,128)(2,1)S(1)}, bf16[64,1024]{1,0:T(8,128)(2,1)S(1)}, u32[]{:S(2)}, u32[]{:S(2)}) collective-permute-start(bf16[64,1024]{1,0:T(8,128)(2,1)S(1)} %collective-permute-done.22.rest_4_), channel_id=1, source_target_pairs={{0,4},{2,6},{4,0},{6,2},{8,12},{10,14},{12,8},{14,10},{16,20},{18,... | collective-permute-start | bytes 393224 | tf_op jit(solution)/shard_map/ppermute | solution.py:332
  94.1 1.3 %collective-permute-start.28 = (bf16[64,1024]{1,0:T(8,128)(2,1)S(1)}, bf16[64,1024]{1,0:T(8,128)(2,1)S(1)}, u32[]{:S(2)}, u32[]{:S(2)}) collective-permute-start(bf16[64,1024]{1,0:T(8,128)(2,1)S(1)} %collective-permute-done.27.rest_0_), channel_id=1, source_target_pairs={{0,2},{2,0},{4,6},{6,4},{8,10},{10,8},{12,14},{14,12},{16,18},{18,... | collective-permute-start | bytes 393224 | tf_op jit(solution)/shard_map/ppermute | solution.py:332
  95.8 4.6 %collective-permute-start.29 = (s16[80,512]{1,0:T(8,128)(2,1)S(1)}, s16[80,512]{1,0:T(8,128)(2,1)S(1)}, u32[]{:S(2)}, u32[]{:S(2)}) collective-permute-start(s16[80,512]{1,0:T(8,128)(2,1)S(1)} %get-tuple-element.78), channel_id=1, source_target_pairs={{0,1},{1,0},{2,3},{3,2},{4,5},{5,4},{6,7},{7,6},{8,9},{9,8},{10,11... | collective-permute-start | bytes 245768 | tf_op jit(solution)/shard_map/ppermute | solution.py:450
  97.4 5.3 %copy-start.1 = (bf16[256,512]{1,0:T(8,128)(2,1)S(1)}, bf16[256,512]{1,0:T(8,128)(2,1)}, u32[]{:S(2)}) copy-start(bf16[256,512]{1,0:T(8,128)(2,1)} %text_ref.1) | copy-start | bytes 786436
  98.2 4.5 %collective-permute-start.26 = (s16[80,512]{1,0:T(8,128)(2,1)S(1)}, s16[80,512]{1,0:T(8,128)(2,1)S(1)}, u32[]{:S(2)}, u32[]{:S(2)}) collective-permute-start(s16[80,512]{1,0:T(8,128)(2,1)S(1)} %get-tuple-element.76), channel_id=1, source_target_pairs={{0,1},{1,0},{2,3},{3,2},{4,5},{5,4},{6,7},{7,6},{8,9},{9,8},{10,11... | collective-permute-start | bytes 245768 | tf_op jit(solution)/shard_map/ppermute | solution.py:450

commit v3 on v2

--- a/solution.py
+++ b/solution.py
@@ -77,41 +77,14 @@
     return code_ref[h * rows : (h + 1) * rows, :].astype(I32).astype(F32) * scales[:, h : h + 1]
 
 
-def begin_kernel(ds, x_hbm, w_hbm, key_hbm, value_hbm, mask_hbm, *rest):
-    groups = len(ds)
-    first, other, packs = rest[:2], rest[2:4], rest[4 : 4 + groups]
-    x_ref, w_buf, key_ref, value_ref, mask_ref, sems = rest[4 + groups :]
-    half = x_ref.shape[0] // 2
-    width = w_buf.shape[2]
+def pack_kernel(key_hbm, value_hbm, mask_hbm, *rest):
+    packs, (key_ref, value_ref, mask_ref, sems) = rest[:-4], rest[-4:]
     keys = key_ref.shape[0]
-
-    def fetch(source, target, n):
-        copy = pltpu.make_async_copy(source, target, sems.at[n])
-        copy.start()
-        return copy
-
-    def weights(i):
-        at = pl.multiple_of((ids[2] ^ ds[i]) * width, width)
-        return fetch(w_hbm.at[:, pl.ds(at, width)], w_buf.at[i], i)
-
-    text = fetch(x_hbm, x_ref, groups)
-    copies = [weights(0)]
-    tokens = [fetch(key_hbm, key_ref, groups + 1), fetch(value_hbm, value_ref, groups + 2)]
-    tokens.append(fetch(mask_hbm, mask_ref, groups + 3))
-    copies += [weights(i) for i in range(1, groups)]
-    peer = pl.multiple_of((1 - ids[0]) * half, half)
-    mine = pl.multiple_of(ids[0] * half, half)
-
-    def project(i, send_ref, keep_ref, at):
-        copies[i].wait()
-        cols = slice(at * width, (at + 1) * width)
-        w = w_buf[i]
-        send_ref[:, cols] = jnp.dot(x_ref[pl.ds(peer, half), :], w, preferred_element_type=F32)
-        keep_ref[:, cols] = jnp.dot(x_ref[pl.ds(mine, half), :], w, preferred_element_type=F32)
-
-    text.wait()
-    project(0, *first, 0)
-    for copy in tokens:
+    copies = []
+    for n, (source, target) in enumerate(((value_hbm, value_ref), (key_hbm, key_ref), (mask_hbm, mask_ref))):
+        copies.append(pltpu.make_async_copy(source, target, sems.at[n]))
+        copies[-1].start()
+    for copy in copies:
         copy.wait()
     line = lax.broadcasted_iota(I32, (TAIL, LANES), 0)
     tail = jnp.zeros((TAIL, LANES), F32)
@@ -121,15 +94,35 @@
             row = mask_ref[s : s + 1, j * LANES : (j + 1) * LANES]
             here = line == s * (text_rows // LANES) + j
             tail = jnp.where(here & (row == 1), F32(1.0), tail)
-    for d in range(groups):
+    for d in range(len(packs)):
         at = pl.multiple_of((ids[2] ^ d) * LANES, LANES)
         packs[d][:keys, :] = key_ref[:, pl.ds(at, LANES)]
         for c in range(keys // LANES):
             block = value_ref[c * LANES : (c + 1) * LANES, pl.ds(at, LANES)]
             packs[d][keys + c * LANES : keys + (c + 1) * LANES, :] = jnp.transpose(block)
         packs[d][2 * keys :, :] = tail.astype(BF16)
-    for i in range(1, groups):
-        project(i, *other, i - 1)
+
+
+def project_kernel(ds, x_hbm, w_hbm, send_ref, keep_ref, more_ref, kept_ref, x_ref, w_buf, sems):
+    half = x_ref.shape[0] // 2
+    width = w_buf.shape[2]
+    text = pltpu.make_async_copy(x_hbm, x_ref, sems.at[len(ds)])
+    text.start()
+    copies = []
+    for i, d in enumerate(ds):
+        at = pl.multiple_of((ids[2] ^ d) * width, width)
+        copies.append(pltpu.make_async_copy(w_hbm.at[:, pl.ds(at, width)], w_buf.at[i], sems.at[i]))
+        copies[-1].start()
+    peer = pl.multiple_of((1 - ids[0]) * half, half)
+    mine = pl.multiple_of(ids[0] * half, half)
+    text.wait()
+    for i in range(len(ds)):
+        copies[i].wait()
+        send, keep, at = (send_ref, keep_ref, 0) if i == 0 else (more_ref, kept_ref, i - 1)
+        cols = slice(at * width, (at + 1) * width)
+        w = w_buf[i]
+        send[:, cols] = jnp.dot(x_ref[pl.ds(peer, half), :], w, preferred_element_type=F32)
+        keep[:, cols] = jnp.dot(x_ref[pl.ds(mine, half), :], w, preferred_element_type=F32)
 
 
 def split_x_kernel(first, keep_ref, got_ref, code_ref, own_ref):
@@ -269,38 +262,47 @@
             out_ref[:, h * LANES : (h + 1) * LANES] = block[p * rows : (p + 1) * rows].astype(BF16)
 
 
-def output_part(ds, blocks, w_ref):
-    width = blocks[0][0].shape[1]
+def output_rows_kernel(ds, tail_d, w_ref, *rest):
+    blocks, (near_ref, far_ref) = rest[:-2], rest[-2:]
+    rows, width = blocks[0].shape
     groups = w_ref.shape[0] // width
-    total = None
-    for d, row_blocks in zip(ds, blocks):
-        left = jnp.concatenate([b[...] for b in row_blocks], axis=0)
+    near = far = None
+    blocks = list(blocks)
+    for d in ds:
         base = pl.multiple_of(lax.rem(ids[2] + groups - d, groups) * width, width)
-        part = jnp.dot(left, w_ref[pl.ds(base, width), :], preferred_element_type=F32)
-        total = part if total is None else total + part
-    return total
-
-
-def output_kernel(ds, begin, finish, w_ref, *rest):
-    count = 2 * len(ds)
-    blocks = [rest[2 * i : 2 * i + 2] for i in range(len(ds))]
-    rest = rest[count:]
-    total = output_part(ds, blocks, w_ref)
-    if not begin:
-        total = total + rest[0][...]
-        rest = rest[1:]
-    if not finish:
-        rest[0][...] = total
-        return
-    keep_ref, code_ref = rest
+        w = w_ref[pl.ds(base, width), :]
+        if d == tail_d:
+            part = jnp.dot(blocks.pop(0)[...], w, preferred_element_type=F32)
+        else:
+            left = jnp.concatenate([blocks.pop(0)[...], blocks.pop(0)[...]], axis=0)
+            part = jnp.dot(left, w, preferred_element_type=F32)
+            far = part[rows:] if far is None else far + part[rows:]
+        near = part[:rows] if near is None else near + part[:rows]
+    near_ref[...] = near
+    far_ref[...] = far
+
+
+def split_rows(own, other, keep_ref, code_ref):
     rows, width = keep_ref.shape
-    own, other = total[:rows], total[rows:]
     keep_own = jnp.full((rows, 1), (ids[0] == ids[3]).astype(I32), I32) == 1
     keep_ref[...] = jnp.where(keep_own, own, other)
     send = jnp.where(keep_own, other, own)
     power = power_of(jnp.max(jnp.abs(send), axis=0, keepdims=True))
     code_ref[:rows, :] = jnp.round(send * (jnp.exp2(-power) * CODE_TOP)).astype(I32).astype(I16)
     code_ref[rows:, :] = jnp.broadcast_to(power, (TAIL, width)).astype(I32).astype(I16)
+
+
+def split_near_kernel(own_ref, other_ref, keep_ref, code_ref):
+    split_rows(own_ref[...], other_ref[...], keep_ref, code_ref)
+
+
+def output_last_kernel(tail_d, w_ref, own_block, other_block, own_ref, other_ref, keep_ref, code_ref):
+    rows, width = own_block.shape
+    groups = w_ref.shape[0] // width
+    base = pl.multiple_of(lax.rem(ids[2] + groups - tail_d, groups) * width, width)
+    left = jnp.concatenate([own_block[...], other_block[...]], axis=0)
+    part = jnp.dot(left, w_ref[pl.ds(base, width), :], preferred_element_type=F32)
+    split_rows(own_ref[...] + part[:rows], other_ref[...] + part[rows:], keep_ref, code_ref)
 
 
 def finish_kernel(keep_near, got_near, keep_far, got_far, text_ref, out_ref):
@@ -340,23 +342,32 @@
     in_hbm = functools.partial(pltpu.with_memory_space_constraint, memory_space=pltpu.HBM)
     order = list(range(groups - 1, -1, -1))
     chunks = [groups - 1, *[d for d in range(1, groups - 1)], 0]
-    parts = [struct((half, width), F32)] * 2 + [struct((half, (groups - 1) * width), F32)] * 2
-    sent, kept, sent_more, kept_more, *packs = call(
-        functools.partial(begin_kernel, chunks),
-        (*parts, *[struct((2 * keys + TAIL, LANES), BF16)] * groups),
-        (in_hbm(text_states), in_hbm(q_weight), in_hbm(key_cache), in_hbm(value_cache), in_hbm(block_mask.T)),
+    packs = call(
+        pack_kernel,
+        (struct((2 * keys + TAIL, LANES), BF16),) * groups,
+        (in_hbm(key_cache), in_hbm(value_cache), in_hbm(block_mask.T)),
+        specs=[HB] * 3,
+        scratch=[
+            pltpu.VMEM(key_cache.shape, BF16),
+            pltpu.VMEM(value_cache.shape, BF16),
+            pltpu.VMEM((segments, text_rows), I32),
+            pltpu.SemaphoreType.DMA((3,)),
+        ],
+    )
+    source = after(in_hbm(text_states), packs[0])
+    packs = [packs[0]] + [swap(packs[d], 4 * d) for d in range(1, groups)]
+    sent, kept, sent_more, kept_more = call(
+        functools.partial(project_kernel, chunks),
+        (*[struct((half, width), F32)] * 2, *[struct((half, (groups - 1) * width), F32)] * 2),
+        (source, in_hbm(q_weight)),
         flops=2 * text_rows * depth * columns,
-        specs=[HB] * 5,
+        specs=[HB] * 2,
         scratch=[
             pltpu.VMEM(text_states.shape, BF16),
             pltpu.VMEM((groups, depth, width), BF16),
-            pltpu.VMEM(key_cache.shape, BF16),
-            pltpu.VMEM(value_cache.shape, BF16),
-            pltpu.VMEM((segments, text_rows), I32),
-            pltpu.SemaphoreType.DMA((groups + 4,)),
+            pltpu.SemaphoreType.DMA((groups + 1,)),
         ],
     )
-    packs = [packs[0]] + [swap(packs[d], 4 * d) for d in range(1, groups)]
     halves = (kept, swap(sent, 1))
     more = (kept_more, swap(sent_more, 1))
 
@@ -408,9 +419,7 @@
         previous = res
         outs[rel] = swap(res, rel) if rel else res
     attended = call(
-        functools.partial(merge_kernel, heads),
-        struct((rows, width), BF16),
-        (*outs[0], outs[1], outs[2], outs[3]),
+        functools.partial(merge_kernel, heads), struct((rows, width), BF16), (*outs[0], outs[1], outs[2], outs[3])
     )
 
     column = {d: turn(attended, 4 * d) if d else attended for d in order}
@@ -434,31 +443,33 @@
     moved = moved + end
     for i, d in enumerate(reversed(late)):
         blocks[d] = (column[d], beside[d], moved[2 * i], moved[2 * i + 1])
-    near = {d: (blocks[d][0], blocks[d][2]) for d in range(groups)}
-    far = {d: (blocks[d][1], blocks[d][3]) for d in range(groups)}
-
-    def output(ds, rows_of, begin, finish, *before):
-        done = (struct((rows, out_cols), F32), struct((rows + TAIL, out_cols), I16))
+    piece = struct((rows, out_cols), F32)
+    done = (piece, struct((rows + TAIL, out_cols), I16))
+
+    def output_rows(side):
+        parts = [b for d in order for b in blocks[d][2 * side : 2 * side + (1 if d == tail_d else 2)]]
         return call(
-            functools.partial(output_kernel, ds, begin, finish),
-            done if finish else struct((2 * rows, out_cols), F32),
-            (o_weight, *[b for d in ds for b in rows_of[d]], *before),
-            flops=4 * rows * width * len(ds) * out_cols,
+            functools.partial(output_rows_kernel, order, tail_d),
+            (piece, piece),
+            (o_weight, *parts),
+            flops=4 * rows * columns * out_cols,
         )
 
     def trade(code):
         return lax.ppermute(code, ("head", "tp"), [(0, 1), (1, 0)])
 
-    before = output([d for d in range(groups) if d != tail_d], far, True, False)
-    keep_near, code = output(list(range(groups)), near, True, True)
+    near_own, far_own = output_rows(0)
+    near_other, far_other = output_rows(1)
+    keep_near, code = call(split_near_kernel, done, (near_own, near_other))
     got_near = trade(code)
-    keep_far, code = output([tail_d], far, False, True, before)
+    keep_far, code = call(
+        functools.partial(output_last_kernel, tail_d),
+        done,
+        (o_weight, blocks[tail_d][1], blocks[tail_d][3], far_own, far_other),
+        flops=4 * rows * width * out_cols,
+    )
     got_far = trade(code)
-    return call(
-        finish_kernel,
-        struct((half, out_cols), BF16),
-        (keep_near, got_near, keep_far, got_far, text_states),
-    )
+    return call(finish_kernel, struct((half, out_cols), BF16), (keep_near, got_near, keep_far, got_far, text_states))
 
 
 def plain_shards(

time: 104 us -> 105 us (level)
  Pallas kernels: 19.5 us -> 21 us
    pallas_call x23 -> x25, Pallas kernels: 19.5 us -> 21 us  [call(): pl.pallas_call(kernel, out_shape=out_shape, in_specs=specs or [VM] * len(...]
  transfers between devices with their start and end apart: 30 -> 30, of which waited for: 16 -> 15; matrix products, arithmetic and copies ran while one was open for 0% -> 0% of each run, Pallas kernels for 12% -> 12%
where the time goes in v3:
time: 105 us
  waiting for transfers between devices  50.4 us (48%)
  starting transfers between devices  32.9 us (31%)
  Pallas kernels  21 us (20%)
    ppermute x25, waiting for transfers between devices, swap(): return lax.ppermute(value, 'ctx', [(i, i ^ bits) for i in range(ctx)])  38.7 us
    ppermute x25, starting transfers between devices, swap(): return lax.ppermute(value, 'ctx', [(i, i ^ bits) for i in range(ctx)])  26.7 us
    pallas_call x25, Pallas kernels, call(): pl.pallas_call(kernel, out_shape=out_shape, in_specs=specs or [VM] * len(...  21 us
    ppermute x3, waiting for transfers between devices, turn(): lax.ppermute(value, 'ctx', [(i, (i + shift) % ctx) for i in range(ctx)])  7.27 us
    ppermute x2, waiting for transfers between devices, trade(): return lax.ppermute(code, ('head', 'tp'), [(0, 1), (1, 0)])  4.45 us
    ppermute x3, starting transfers between devices, turn(): lax.ppermute(value, 'ctx', [(i, (i + shift) % ctx) for i in range(ctx)])  4.03 us
    ppermute x2, starting transfers between devices, trade(): return lax.ppermute(code, ('head', 'tp'), [(0, 1), (1, 0)])  2.16 us
  transfers between devices with their start and end apart: 30, of which 15 were waited for; matrix products, arithmetic and copies ran while one was open for 0% of the time, Pallas kernels for 12%

profile of v3, /device:TPU:0, one launch (start us, length us, event | category | flops | bytes accessed | tf_op | source)
XLA Modules:
  0.0 104.8 jit_solution(14469197964476845022)
XLA Ops:
  0.0 1.5 %shard_map.82 = (bf16[1040,128]{1,0:T(8,128)(2,1)S(1)}, bf16[1040,128]{1,0:T(8,128)(2,1)S(1)}, bf16[1040,128]{1,0:T(8,128)(2,1)S(1)}, bf16[1040,128]{1,0:T(8,128)(2,1)S(1)}) custom-call(bf16[512,512]{1,0:T(8,128)(2,1)} %key_hbm.1, bf16[512,512]{1,0:T(8,128)(2,1)} %value_hbm.1, s32[2,256]{1,0:T(2,128)} %bitcast.40), custom_call_target="tpu_custom_call" | custom-call | bytes 2115584 | tf_op jit(solution)/shard_map/pallas_call | solution.py:39
  1.5 3.2 %shard_map.83 = (f32[128,1024]{1,0:T(8,128)S(1)}, f32[128,1024]{1,0:T(8,128)S(1)}, f32[128,3072]{1,0:T(8,128)S(1)}, f32[128,3072]{1,0:T(8,128)S(1)}) custom-call(bf16[256,512]{1,0:T(8,128)(2,1)} %text_ref.1, bf16[512,4096]{1,0:T(8,128)(2,1)} %w_hbm.1), custom_call_target="tpu_custom_call" | custom-call | flops 1073741824 | bytes 8650752 | tf_op jit(solution)/shard_map/pallas_call | solution.py:39
  4.7 0.6 collective-permute-start
  5.2 0.1 collective-permute-start.6
  5.3 3.7 %collective-permute-done.6.got_ref = f32[128,1024]{1,0:T(8,128)S(1)} collective-permute-done((f32[128,1024]{1,0:T(8,128)S(1)}, f32[128,1024]{1,0:T(8,128)S(1)}, u32[]{:S(2)}, u32[]{:S(2)}) %collective-permute-start.6) | collective-permute-done | bytes 524320 | tf_op jit(solution)/shard_map/ppermute | solution.py:334
  9.0 0.3 shard_map.90
  9.3 2.9 %collective-permute-start.7 = (s16[528,128]{1,0:T(8,128)(2,1)S(1)}, s16[528,128]{1,0:T(8,128)(2,1)S(1)}, u32[]{:S(2)}, u32[]{:S(2)}) collective-permute-start(s16[528,128]{1,0:T(8,128)(2,1)S(1)} %get-tuple-element.60), channel_id=1, source_target_pairs={{0,4},{2,6},{4,0},{6,2},{8,12},{10,14},{12,8},{14,10},{16,20},{18,... | collective-permute-start | bytes 405512 | tf_op jit(solution)/shard_map/ppermute | solution.py:334
  12.3 0.3 shard_map.88
  12.6 0.1 collective-permute-start.4
  12.7 0.3 shard_map.86
  13.0 2.1 %collective-permute-start.2 = (s16[528,128]{1,0:T(8,128)(2,1)S(1)}, s16[528,128]{1,0:T(8,128)(2,1)S(1)}, u32[]{:S(2)}, u32[]{:S(2)}) collective-permute-start(s16[528,128]{1,0:T(8,128)(2,1)S(1)} %get-tuple-element.54), channel_id=1, source_target_pairs={{0,4},{2,6},{4,0},{6,2},{8,12},{10,14},{12,8},{14,10},{16,20},{18,... | collective-permute-start | bytes 405512 | tf_op jit(solution)/shard_map/ppermute | solution.py:334
  15.1 1.6 %collective-permute-done.7.got_ref = s16[528,128]{1,0:T(8,128)(2,1)S(1)} collective-permute-done((s16[528,128]{1,0:T(8,128)(2,1)S(1)}, s16[528,128]{1,0:T(8,128)(2,1)S(1)}, u32[]{:S(2)}, u32[]{:S(2)}) %collective-permute-start.7) | collective-permute-done | bytes 135200 | tf_op jit(solution)/shard_map/ppermute | solution.py:334
  16.7 0.5 shard_map.91
  17.2 4.2 %collective-permute-start.8 = (s16[528,128]{1,0:T(8,128)(2,1)S(1)}, s16[528,128]{1,0:T(8,128)(2,1)S(1)}, u32[]{:S(2)}, u32[]{:S(2)}) collective-permute-start(s16[528,128]{1,0:T(8,128)(2,1)S(1)} %shard_map.91), channel_id=1, source_target_pairs={{0,24},{2,26},{4,28},{6,30},{8,16},{10,18},{12,20},{14,22},{16,8},... | collective-permute-start | bytes 405512 | tf_op jit(solution)/shard_map/ppermute | solution.py:334
  21.4 0.9 collective-permute-start.13
  22.3 0.3 shard_map.84
  22.7 1.6 %collective-permute-start.1 = (s16[528,128]{1,0:T(8,128)(2,1)S(1)}, s16[528,128]{1,0:T(8,128)(2,1)S(1)}, u32[]{:S(2)}, u32[]{:S(2)}) collective-permute-start(s16[528,128]{1,0:T(8,128)(2,1)S(1)} %get-tuple-element.52), channel_id=1, source_target_pairs={{0,4},{2,6},{4,0},{6,2},{8,12},{10,14},{12,8},{14,10},{16,20},{18,... | collective-permute-start | bytes 405512 | tf_op jit(solution)/shard_map/ppermute | solution.py:334
  24.2 0.5 shard_map.89
  24.8 2.6 %collective-permute-start.5 = (s16[528,128]{1,0:T(8,128)(2,1)S(1)}, s16[528,128]{1,0:T(8,128)(2,1)S(1)}, u32[]{:S(2)}, u32[]{:S(2)}) collective-permute-start(s16[528,128]{1,0:T(8,128)(2,1)S(1)} %shard_map.89), channel_id=1, source_target_pairs={{0,16},{2,18},{4,20},{6,22},{8,24},{10,26},{12,28},{14,30},{16,0},... | collective-permute-start | bytes 405512 | tf_op jit(solution)/shard_map/ppermute | solution.py:334
  27.4 0.5 shard_map.87
  27.9 1.0 collective-permute-start.3
  28.9 1.4 %collective-permute-start.14 = (bf16[1040,128]{1,0:T(8,128)(2,1)S(1)}, bf16[1040,128]{1,0:T(8,128)(2,1)S(1)}, u32[]{:S(2)}, u32[]{:S(2)}) collective-permute-start(bf16[1040,128]{1,0:T(8,128)(2,1)S(1)} %get-tuple-element.75), channel_id=1, source_target_pairs={{0,16},{2,18},{4,20},{6,22},{8,24},{10,26},{12,28},{14,30},{16,0},... | collective-permute-start | bytes 798728 | tf_op jit(solution)/shard_map/ppermute | solution.py:334
  30.3 0.3 shard_map.85.own_ref
  30.6 19.0 %collective-permute-done.5.rest_1_ = s16[528,128]{1,0:T(8,128)(2,1)S(1)} collective-permute-done((s16[528,128]{1,0:T(8,128)(2,1)S(1)}, s16[528,128]{1,0:T(8,128)(2,1)S(1)}, u32[]{:S(2)}, u32[]{:S(2)}) %collective-permute-start.5) | collective-permute-done | bytes 135200 | tf_op jit(solution)/shard_map/ppermute | solution.py:334
  49.6 1.0 shard_map.92.q_ref
  50.7 1.5 %collective-permute-start.11 = (bf16[64,1024]{1,0:T(8,128)(2,1)S(1)}, bf16[64,1024]{1,0:T(8,128)(2,1)S(1)}, u32[]{:S(2)}, u32[]{:S(2)}) collective-permute-start(bf16[64,1024]{1,0:T(8,128)(2,1)S(1)} %shard_map.92.q_ref), channel_id=1, source_target_pairs={{0,4},{2,6},{4,0},{6,2},{8,12},{10,14},{12,8},{14,10},{16,20},{18,... | collective-permute-start | bytes 393224 | tf_op jit(solution)/shard_map/ppermute | solution.py:334
  52.1 0.4 collective-permute-start.10
  52.5 1.6 %shard_map.93 = (f32[128,512]{1,0:T(8,128)S(1)}, f32[8,512]{1,0:T(8,128)S(1)}) custom-call(bf16[64,1024]{1,0:T(8,128)(2,1)S(1)} %shard_map.92.q_ref, s32[2,128]{1,0:T(2,128)S(1)} %bitcast.31, bf16[1040,128]{1,0:T(8,128)(2,1)S(1)} %get-tuple-element.47.rest_0_, bf16[1040,128]{1,0:T(8,128)(2,1)S(1)} %collective-permute-done.12.rest_1_, ...), custom_call_target="tpu_custom_call" | custom-call | flops 402653184 | bytes 1209344 | tf_op jit(solution)/shard_map/pallas_call | solution.py:39
  54.1 1.6 %shard_map.94 = (f32[128,512]{1,0:T(8,128)S(1)}, f32[8,512]{1,0:T(8,128)S(1)}) custom-call(bf16[64,1024]{1,0:T(8,128)(2,1)S(1)} %collective-permute-done.9.q_ref, s32[2,128]{1,0:T(2,128)S(1)} %bitcast.32, bf16[1040,128]{1,0:T(8,128)(2,1)S(1)} %get-tuple-element.47.rest_0_, bf16[1040,128]{1,0:T(8,128)(2,1)S(1)} %collective-permute-done.12.rest_1_, ...), custom_call_target="tpu_custom_call" | custom-call | flops 402653184 | bytes 1209344 | tf_op jit(solution)/shard_map/pallas_call | solution.py:39
  55.8 1.3 %collective-permute-done.11.q_ref = bf16[64,1024]{1,0:T(8,128)(2,1)S(1)} collective-permute-done((bf16[64,1024]{1,0:T(8,128)(2,1)S(1)}, bf16[64,1024]{1,0:T(8,128)(2,1)S(1)}, u32[]{:S(2)}, u32[]{:S(2)}) %collective-permute-start.11) | collective-permute-done | bytes 131104 | tf_op jit(solution)/shard_map/ppermute | solution.py:334
  57.1 1.6 %shard_map.95 = (f32[128,512]{1,0:T(8,128)S(1)}, f32[8,512]{1,0:T(8,128)S(1)}) custom-call(bf16[64,1024]{1,0:T(8,128)(2,1)S(1)} %collective-permute-done.11.q_ref, s32[2,128]{1,0:T(2,128)S(1)} %bitcast.33, bf16[1040,128]{1,0:T(8,128)(2,1)S(1)} %get-tuple-element.47.rest_0_, bf16[1040,128]{1,0:T(8,128)(2,1)S(1)} %collective-permute-done.12.rest_1_, ...), custom_call_target="tpu_custom_call" | custom-call | flops 402653184 | bytes 1209344 | tf_op jit(solution)/shard_map/pallas_call | solution.py:39
  58.7 0.1 collective-permute-done.10.q_ref
  58.8 1.6 %shard_map.96 = (f32[128,512]{1,0:T(8,128)S(1)}, f32[8,512]{1,0:T(8,128)S(1)}) custom-call(bf16[64,1024]{1,0:T(8,128)(2,1)S(1)} %collective-permute-done.10.q_ref, s32[2,128]{1,0:T(2,128)S(1)} %bitcast.34, bf16[1040,128]{1,0:T(8,128)(2,1)S(1)} %get-tuple-element.47.rest_0_, bf16[1040,128]{1,0:T(8,128)(2,1)S(1)} %collective-permute-done.12.rest_1_, ...), custom_call_target="tpu_custom_call" | custom-call | flops 402653184 | bytes 1209344 | tf_op jit(solution)/shard_map/pallas_call | solution.py:39
  60.4 0.7 shard_map.97
  61.1 0.9 shard_map.98
  62.0 0.7 shard_map.99
  62.7 0.4 collective-permute-start.15
  63.2 1.1 %collective-permute-start.17 = (s16[144,512]{1,0:T(8,128)(2,1)S(1)}, s16[144,512]{1,0:T(8,128)(2,1)S(1)}, u32[]{:S(2)}, u32[]{:S(2)}) collective-permute-start(s16[144,512]{1,0:T(8,128)(2,1)S(1)} %shard_map.98), channel_id=1, source_target_pairs={{0,6},{2,4},{4,2},{6,0},{8,14},{10,12},{12,10},{14,8},{16,22},{18,... | collective-permute-start | bytes 442376 | tf_op jit(solution)/shard_map/ppermute | solution.py:334
  64.3 0.6 collective-permute-start.16
  64.9 0.7 shard_map.100
  65.6 3.4 %collective-permute-done.17.rest_2_ = s16[144,512]{1,0:T(8,128)(2,1)S(1)} collective-permute-done((s16[144,512]{1,0:T(8,128)(2,1)S(1)}, s16[144,512]{1,0:T(8,128)(2,1)S(1)}, u32[]{:S(2)}, u32[]{:S(2)}) %collective-permute-start.17) | collective-permute-done | bytes 147488 | tf_op jit(solution)/shard_map/ppermute | solution.py:334
  69.0 3.5 %collective-permute-done.16.rest_1_ = s16[144,512]{1,0:T(8,128)(2,1)S(1)} collective-permute-done((s16[144,512]{1,0:T(8,128)(2,1)S(1)}, s16[144,512]{1,0:T(8,128)(2,1)S(1)}, u32[]{:S(2)}, u32[]{:S(2)}) %collective-permute-start.16) | collective-permute-done | bytes 147488 | tf_op jit(solution)/shard_map/ppermute | solution.py:334
  72.5 0.2 shard_map.101.rest_5_
  72.7 3.4 %collective-permute-start.18 = (bf16[64,1024]{1,0:T(8,128)(2,1)S(1)}, bf16[64,1024]{1,0:T(8,128)(2,1)S(1)}, u32[]{:S(2)}, u32[]{:S(2)}) collective-permute-start(bf16[64,1024]{1,0:T(8,128)(2,1)S(1)} %shard_map.101.rest_5_), channel_id=1, source_target_pairs={{0,24},{2,26},{4,28},{6,30},{8,0},{10,2},{12,4},{14,6},{16,8},{18,... | collective-permute-start | bytes 393224 | tf_op jit(solution)/shard_map/ppermute | solution.py:337
  76.1 0.6 collective-permute-start.20
  76.7 3.3 %collective-permute-done.18.rest_0_ = bf16[64,1024]{1,0:T(8,128)(2,1)S(1)} collective-permute-done((bf16[64,1024]{1,0:T(8,128)(2,1)S(1)}, bf16[64,1024]{1,0:T(8,128)(2,1)S(1)}, u32[]{:S(2)}, u32[]{:S(2)}) %collective-permute-start.18) | collective-permute-done | bytes 131104 | tf_op jit(solution)/shard_map/ppermute | solution.py:337
  80.0 1.5 %collective-permute-start.19 = (bf16[64,1024]{1,0:T(8,128)(2,1)S(1)}, bf16[64,1024]{1,0:T(8,128)(2,1)S(1)}, u32[]{:S(2)}, u32[]{:S(2)}) collective-permute-start(bf16[64,1024]{1,0:T(8,128)(2,1)S(1)} %collective-permute-done.18.rest_0_), channel_id=1, source_target_pairs={{0,4},{2,6},{4,0},{6,2},{8,12},{10,14},{12,8},{14,10},{16,20},{18,... | collective-permute-start | bytes 393224 | tf_op jit(solution)/shard_map/ppermute | solution.py:334
  81.5 0.5 collective-permute-start.23
  82.0 2.3 %collective-permute-done.21.rest_3_ = bf16[64,1024]{1,0:T(8,128)(2,1)S(1)} collective-permute-done((bf16[64,1024]{1,0:T(8,128)(2,1)S(1)}, bf16[64,1024]{1,0:T(8,128)(2,1)S(1)}, u32[]{:S(2)}, u32[]{:S(2)}) %collective-permute-start.21) | collective-permute-done | bytes 131104 | tf_op jit(solution)/shard_map/ppermute | solution.py:337
  84.3 1.5 %collective-permute-start.22 = (bf16[64,1024]{1,0:T(8,128)(2,1)S(1)}, bf16[64,1024]{1,0:T(8,128)(2,1)S(1)}, u32[]{:S(2)}, u32[]{:S(2)}) collective-permute-start(bf16[64,1024]{1,0:T(8,128)(2,1)S(1)} %collective-permute-done.21.rest_3_), channel_id=1, source_target_pairs={{0,4},{2,6},{4,0},{6,2},{8,12},{10,14},{12,8},{14,10},{16,20},{18,... | collective-permute-start | bytes 393224 | tf_op jit(solution)/shard_map/ppermute | solution.py:334
  85.8 1.7 %collective-permute-done.20.rest_2_ = bf16[64,1024]{1,0:T(8,128)(2,1)S(1)} collective-permute-done((bf16[64,1024]{1,0:T(8,128)(2,1)S(1)}, bf16[64,1024]{1,0:T(8,128)(2,1)S(1)}, u32[]{:S(2)}, u32[]{:S(2)}) %collective-permute-start.20) | collective-permute-done | bytes 131104 | tf_op jit(solution)/shard_map/ppermute | solution.py:337
  87.6 0.1 collective-permute-start.24
  87.7 0.1 collective-permute-done.23.rest_6_
  87.8 1.5 %collective-permute-done.22.rest_4_ = bf16[64,1024]{1,0:T(8,128)(2,1)S(1)} collective-permute-done((bf16[64,1024]{1,0:T(8,128)(2,1)S(1)}, bf16[64,1024]{1,0:T(8,128)(2,1)S(1)}, u32[]{:S(2)}, u32[]{:S(2)}) %collective-permute-start.22) | collective-permute-done | bytes 131104 | tf_op jit(solution)/shard_map/ppermute | solution.py:334
  89.4 1.6 %collective-permute-start.27 = (bf16[64,1024]{1,0:T(8,128)(2,1)S(1)}, bf16[64,1024]{1,0:T(8,128)(2,1)S(1)}, u32[]{:S(2)}, u32[]{:S(2)}) collective-permute-start(bf16[64,1024]{1,0:T(8,128)(2,1)S(1)} %collective-permute-done.20.rest_2_), channel_id=1, source_target_pairs={{0,4},{2,6},{4,0},{6,2},{8,12},{10,14},{12,8},{14,10},{16,20},{18,... | collective-permute-start | bytes 393224 | tf_op jit(solution)/shard_map/ppermute | solution.py:334
  91.0 4.3 %collective-permute-done.27.own_block = bf16[64,1024]{1,0:T(8,128)(2,1)S(1)} collective-permute-done((bf16[64,1024]{1,0:T(8,128)(2,1)S(1)}, bf16[64,1024]{1,0:T(8,128)(2,1)S(1)}, u32[]{:S(2)}, u32[]{:S(2)}) %collective-permute-start.27) | collective-permute-done | bytes 131104 | tf_op jit(solution)/shard_map/ppermute | solution.py:334
  95.3 0.8 shard_map.102
  96.2 0.8 shard_map.103
  97.1 0.4 shard_map.105
  97.5 1.6 %collective-permute-start.29 = (s16[80,512]{1,0:T(8,128)(2,1)S(1)}, s16[80,512]{1,0:T(8,128)(2,1)S(1)}, u32[]{:S(2)}, u32[]{:S(2)}) collective-permute-start(s16[80,512]{1,0:T(8,128)(2,1)S(1)} %get-tuple-element.88), channel_id=1, source_target_pairs={{0,1},{1,0},{2,3},{3,2},{4,5},{5,4},{6,7},{7,6},{8,9},{9,8},{10,11... | collective-permute-start | bytes 245768 | tf_op jit(solution)/shard_map/ppermute | solution.py:459
  99.1 0.6 collective-permute-start.26
  99.7 3.1 %collective-permute-done.29.got_far = s16[80,512]{1,0:T(8,128)(2,1)S(1)} collective-permute-done((s16[80,512]{1,0:T(8,128)(2,1)S(1)}, s16[80,512]{1,0:T(8,128)(2,1)S(1)}, u32[]{:S(2)}, u32[]{:S(2)}) %collective-permute-start.29) | collective-permute-done | bytes 81952 | tf_op jit(solution)/shard_map/ppermute | solution.py:459
  102.8 1.4 %collective-permute-done.26.got_near = s16[80,512]{1,0:T(8,128)(2,1)S(1)} collective-permute-done((s16[80,512]{1,0:T(8,128)(2,1)S(1)}, s16[80,512]{1,0:T(8,128)(2,1)S(1)}, u32[]{:S(2)}, u32[]{:S(2)}) %collective-permute-start.26) | collective-permute-done | bytes 81952 | tf_op jit(solution)/shard_map/ppermute | solution.py:459
  104.1 0.7 shard_map.106
  (33 shorter events, 0.4 us)
Async XLA Ops:
  4.7 7.6 %collective-permute-start = (f32[128,3072]{1,0:T(8,128)S(1)}, f32[128,3072]{1,0:T(8,128)S(1)}, u32[]{:S(2)}, u32[]{:S(2)}) collective-permute-start(f32[128,3072]{1,0:T(8,128)S(1)} %get-tuple-element.50), channel_id=1, source_target_pairs={{0,2},{2,0},{4,6},{6,4},{8,10},{10,8},{12,14},{14,12},{16,18},{18,... | collective-permute-start | bytes 4718600 | tf_op jit(solution)/shard_map/ppermute | solution.py:334
  5.2 3.8 %collective-permute-start.6 = (f32[128,1024]{1,0:T(8,128)S(1)}, f32[128,1024]{1,0:T(8,128)S(1)}, u32[]{:S(2)}, u32[]{:S(2)}) collective-permute-start(f32[128,1024]{1,0:T(8,128)S(1)} %get-tuple-element.58), channel_id=1, source_target_pairs={{0,2},{2,0},{4,6},{6,4},{8,10},{10,8},{12,14},{14,12},{16,18},{18,... | collective-permute-start | bytes 1572872 | tf_op jit(solution)/shard_map/ppermute | solution.py:334
  9.3 7.4 %collective-permute-start.7 = (s16[528,128]{1,0:T(8,128)(2,1)S(1)}, s16[528,128]{1,0:T(8,128)(2,1)S(1)}, u32[]{:S(2)}, u32[]{:S(2)}) collective-permute-start(s16[528,128]{1,0:T(8,128)(2,1)S(1)} %get-tuple-element.60), channel_id=1, source_target_pairs={{0,4},{2,6},{4,0},{6,2},{8,12},{10,14},{12,8},{14,10},{16,20},{18,... | collective-permute-start | bytes 405512 | tf_op jit(solution)/shard_map/ppermute | solution.py:334
  12.6 10.1 %collective-permute-start.4 = (s16[528,128]{1,0:T(8,128)(2,1)S(1)}, s16[528,128]{1,0:T(8,128)(2,1)S(1)}, u32[]{:S(2)}, u32[]{:S(2)}) collective-permute-start(s16[528,128]{1,0:T(8,128)(2,1)S(1)} %get-tuple-element.56), channel_id=1, source_target_pairs={{0,4},{2,6},{4,0},{6,2},{8,12},{10,14},{12,8},{14,10},{16,20},{18,... | collective-permute-start | bytes 405512 | tf_op jit(solution)/shard_map/ppermute | solution.py:334
  13.0 11.7 %collective-permute-start.2 = (s16[528,128]{1,0:T(8,128)(2,1)S(1)}, s16[528,128]{1,0:T(8,128)(2,1)S(1)}, u32[]{:S(2)}, u32[]{:S(2)}) collective-permute-start(s16[528,128]{1,0:T(8,128)(2,1)S(1)} %get-tuple-element.54), channel_id=1, source_target_pairs={{0,4},{2,6},{4,0},{6,2},{8,12},{10,14},{12,8},{14,10},{16,20},{18,... | collective-permute-start | bytes 405512 | tf_op jit(solution)/shard_map/ppermute | solution.py:334
  17.2 10.7 %collective-permute-start.8 = (s16[528,128]{1,0:T(8,128)(2,1)S(1)}, s16[528,128]{1,0:T(8,128)(2,1)S(1)}, u32[]{:S(2)}, u32[]{:S(2)}) collective-permute-start(s16[528,128]{1,0:T(8,128)(2,1)S(1)} %shard_map.91), channel_id=1, source_target_pairs={{0,24},{2,26},{4,28},{6,30},{8,16},{10,18},{12,20},{14,22},{16,8},... | collective-permute-start | bytes 405512 | tf_op jit(solution)/shard_map/ppermute | solution.py:334
  21.4 30.7 %collective-permute-start.12 = (bf16[1040,128]{1,0:T(8,128)(2,1)S(1)}, bf16[1040,128]{1,0:T(8,128)(2,1)S(1)}, u32[]{:S(2)}, u32[]{:S(2)}) collective-permute-start(bf16[1040,128]{1,0:T(8,128)(2,1)S(1)} %get-tuple-element.61), channel_id=1, source_target_pairs={{0,8},{2,10},{4,12},{6,14},{8,0},{10,2},{12,4},{14,6},{16,24},{18,... | collective-permute-start | bytes 798728 | tf_op jit(solution)/shard_map/ppermute | solution.py:334
  21.4 31.1 %collective-permute-start.13 = (bf16[1040,128]{1,0:T(8,128)(2,1)S(1)}, bf16[1040,128]{1,0:T(8,128)(2,1)S(1)}, u32[]{:S(2)}, u32[]{:S(2)}) collective-permute-start(bf16[1040,128]{1,0:T(8,128)(2,1)S(1)} %get-tuple-element.62), channel_id=1, source_target_pairs={{0,24},{2,26},{4,28},{6,30},{8,16},{10,18},{12,20},{14,22},{16,8},... | collective-permute-start | bytes 798728 | tf_op jit(solution)/shard_map/ppermute | solution.py:334
  22.6 27.0 %copy-start.3 = (f32[128]{0:T(128)S(1)}, f32[128]{0:T(128)}, u32[]{:S(2)}) copy-start(f32[128]{0:T(128)} %param.10) | copy-start | bytes 1540
  22.7 29.9 %copy-start.2 = (s32[256]{0:T(256)S(1)}, s32[256]{0:T(256)}, u32[]{:S(2)}) copy-start(s32[256]{0:T(256)} %param.14) | copy-start | bytes 3076
  22.7 6.2 %collective-permute-start.1 = (s16[528,128]{1,0:T(8,128)(2,1)S(1)}, s16[528,128]{1,0:T(8,128)(2,1)S(1)}, u32[]{:S(2)}, u32[]{:S(2)}) collective-permute-start(s16[528,128]{1,0:T(8,128)(2,1)S(1)} %get-tuple-element.52), channel_id=1, source_target_pairs={{0,4},{2,6},{4,0},{6,2},{8,12},{10,14},{12,8},{14,10},{16,20},{18,... | collective-permute-start | bytes 405512 | tf_op jit(solution)/shard_map/ppermute | solution.py:334
  24.8 24.8 %collective-permute-start.5 = (s16[528,128]{1,0:T(8,128)(2,1)S(1)}, s16[528,128]{1,0:T(8,128)(2,1)S(1)}, u32[]{:S(2)}, u32[]{:S(2)}) collective-permute-start(s16[528,128]{1,0:T(8,128)(2,1)S(1)} %shard_map.89), channel_id=1, source_target_pairs={{0,16},{2,18},{4,20},{6,22},{8,24},{10,26},{12,28},{14,30},{16,0},... | collective-permute-start | bytes 405512 | tf_op jit(solution)/shard_map/ppermute | solution.py:334
  27.9 21.7 %collective-permute-start.3 = (s16[528,128]{1,0:T(8,128)(2,1)S(1)}, s16[528,128]{1,0:T(8,128)(2,1)S(1)}, u32[]{:S(2)}, u32[]{:S(2)}) collective-permute-start(s16[528,128]{1,0:T(8,128)(2,1)S(1)} %shard_map.87), channel_id=1, source_target_pairs={{0,8},{2,10},{4,12},{6,14},{8,0},{10,2},{12,4},{14,6},{16,24},{18,... | collective-permute-start | bytes 405512 | tf_op jit(solution)/shard_map/ppermute | solution.py:334
  28.9 31.5 %collective-permute-start.14 = (bf16[1040,128]{1,0:T(8,128)(2,1)S(1)}, bf16[1040,128]{1,0:T(8,128)(2,1)S(1)}, u32[]{:S(2)}, u32[]{:S(2)}) collective-permute-start(bf16[1040,128]{1,0:T(8,128)(2,1)S(1)} %get-tuple-element.75), channel_id=1, source_target_pairs={{0,16},{2,18},{4,20},{6,22},{8,24},{10,26},{12,28},{14,30},{16,0},... | collective-permute-start | bytes 798728 | tf_op jit(solution)/shard_map/ppermute | solution.py:334
  50.6 3.6 %collective-permute-start.9 = (bf16[64,1024]{1,0:T(8,128)(2,1)S(1)}, bf16[64,1024]{1,0:T(8,128)(2,1)S(1)}, u32[]{:S(2)}, u32[]{:S(2)}) collective-permute-start(bf16[64,1024]{1,0:T(8,128)(2,1)S(1)} %shard_map.92.q_ref), channel_id=1, source_target_pairs={{0,2},{2,0},{4,6},{6,4},{8,10},{10,8},{12,14},{14,12},{16,18},{18,... | collective-permute-start | bytes 393224 | tf_op jit(solution)/shard_map/ppermute | solution.py:334
  50.7 6.4 %collective-permute-start.11 = (bf16[64,1024]{1,0:T(8,128)(2,1)S(1)}, bf16[64,1024]{1,0:T(8,128)(2,1)S(1)}, u32[]{:S(2)}, u32[]{:S(2)}) collective-permute-start(bf16[64,1024]{1,0:T(8,128)(2,1)S(1)} %shard_map.92.q_ref), channel_id=1, source_target_pairs={{0,4},{2,6},{4,0},{6,2},{8,12},{10,14},{12,8},{14,10},{16,20},{18,... | collective-permute-start | bytes 393224 | tf_op jit(solution)/shard_map/ppermute | solution.py:334
  52.1 6.7 %collective-permute-start.10 = (bf16[64,1024]{1,0:T(8,128)(2,1)S(1)}, bf16[64,1024]{1,0:T(8,128)(2,1)S(1)}, u32[]{:S(2)}, u32[]{:S(2)}) collective-permute-start(bf16[64,1024]{1,0:T(8,128)(2,1)S(1)} %shard_map.92.q_ref), channel_id=1, source_target_pairs={{0,6},{2,4},{4,2},{6,0},{8,14},{10,12},{12,10},{14,8},{16,22},{18,... | collective-permute-start | bytes 393224 | tf_op jit(solution)/shard_map/ppermute | solution.py:334
  62.0 33.3 %copy-start = (bf16[4096,512]{1,0:T(8,128)(2,1)S(1)}, bf16[4096,512]{1,0:T(8,128)(2,1)}, u32[]{:S(2)}) copy-start(bf16[4096,512]{1,0:T(8,128)(2,1)} %w_ref.5) | copy-start | bytes 12582916
  62.7 2.9 %collective-permute-start.15 = (s16[144,512]{1,0:T(8,128)(2,1)S(1)}, s16[144,512]{1,0:T(8,128)(2,1)S(1)}, u32[]{:S(2)}, u32[]{:S(2)}) collective-permute-start(s16[144,512]{1,0:T(8,128)(2,1)S(1)} %shard_map.99), channel_id=1, source_target_pairs={{0,2},{2,0},{4,6},{6,4},{8,10},{10,8},{12,14},{14,12},{16,18},{18,... | collective-permute-start | bytes 442376 | tf_op jit(solution)/shard_map/ppermute | solution.py:334
  63.2 5.8 %collective-permute-start.17 = (s16[144,512]{1,0:T(8,128)(2,1)S(1)}, s16[144,512]{1,0:T(8,128)(2,1)S(1)}, u32[]{:S(2)}, u32[]{:S(2)}) collective-permute-start(s16[144,512]{1,0:T(8,128)(2,1)S(1)} %shard_map.98), channel_id=1, source_target_pairs={{0,6},{2,4},{4,2},{6,0},{8,14},{10,12},{12,10},{14,8},{16,22},{18,... | collective-permute-start | bytes 442376 | tf_op jit(solution)/shard_map/ppermute | solution.py:334
  64.3 8.2 %collective-permute-start.16 = (s16[144,512]{1,0:T(8,128)(2,1)S(1)}, s16[144,512]{1,0:T(8,128)(2,1)S(1)}, u32[]{:S(2)}, u32[]{:S(2)}) collective-permute-start(s16[144,512]{1,0:T(8,128)(2,1)S(1)} %shard_map.97), channel_id=1, source_target_pairs={{0,4},{2,6},{4,0},{6,2},{8,12},{10,14},{12,8},{14,10},{16,20},{18,... | collective-permute-start | bytes 442376 | tf_op jit(solution)/shard_map/ppermute | solution.py:334
  72.7 7.3 %collective-permute-start.18 = (bf16[64,1024]{1,0:T(8,128)(2,1)S(1)}, bf16[64,1024]{1,0:T(8,128)(2,1)S(1)}, u32[]{:S(2)}, u32[]{:S(2)}) collective-permute-start(bf16[64,1024]{1,0:T(8,128)(2,1)S(1)} %shard_map.101.rest_5_), channel_id=1, source_target_pairs={{0,24},{2,26},{4,28},{6,30},{8,0},{10,2},{12,4},{14,6},{16,8},{18,... | collective-permute-start | bytes 393224 | tf_op jit(solution)/shard_map/ppermute | solution.py:337
  76.1 8.2 %collective-permute-start.21 = (bf16[64,1024]{1,0:T(8,128)(2,1)S(1)}, bf16[64,1024]{1,0:T(8,128)(2,1)S(1)}, u32[]{:S(2)}, u32[]{:S(2)}) collective-permute-start(bf16[64,1024]{1,0:T(8,128)(2,1)S(1)} %shard_map.101.rest_5_), channel_id=1, source_target_pairs={{0,8},{2,10},{4,12},{6,14},{8,16},{10,18},{12,20},{14,22},{16,24},... | collective-permute-start | bytes 393224 | tf_op jit(solution)/shard_map/ppermute | solution.py:337
  76.1 11.4 %collective-permute-start.20 = (bf16[64,1024]{1,0:T(8,128)(2,1)S(1)}, bf16[64,1024]{1,0:T(8,128)(2,1)S(1)}, u32[]{:S(2)}, u32[]{:S(2)}) collective-permute-start(bf16[64,1024]{1,0:T(8,128)(2,1)S(1)} %shard_map.101.rest_5_), channel_id=1, source_target_pairs={{0,16},{2,18},{4,20},{6,22},{8,24},{10,26},{12,28},{14,30},{16,0},... | collective-permute-start | bytes 393224 | tf_op jit(solution)/shard_map/ppermute | solution.py:337
  80.0 7.5 %collective-permute-start.19 = (bf16[64,1024]{1,0:T(8,128)(2,1)S(1)}, bf16[64,1024]{1,0:T(8,128)(2,1)S(1)}, u32[]{:S(2)}, u32[]{:S(2)}) collective-permute-start(bf16[64,1024]{1,0:T(8,128)(2,1)S(1)} %collective-permute-done.18.rest_0_), channel_id=1, source_target_pairs={{0,4},{2,6},{4,0},{6,2},{8,12},{10,14},{12,8},{14,10},{16,20},{18,... | collective-permute-start | bytes 393224 | tf_op jit(solution)/shard_map/ppermute | solution.py:334
  81.5 6.3 %collective-permute-start.23 = (bf16[64,1024]{1,0:T(8,128)(2,1)S(1)}, bf16[64,1024]{1,0:T(8,128)(2,1)S(1)}, u32[]{:S(2)}, u32[]{:S(2)}) collective-permute-start(bf16[64,1024]{1,0:T(8,128)(2,1)S(1)} %shard_map.101.rest_5_), channel_id=1, source_target_pairs={{0,4},{2,6},{4,0},{6,2},{8,12},{10,14},{12,8},{14,10},{16,20},{18,... | collective-permute-start | bytes 393224 | tf_op jit(solution)/shard_map/ppermute | solution.py:334
  84.3 5.0 %collective-permute-start.22 = (bf16[64,1024]{1,0:T(8,128)(2,1)S(1)}, bf16[64,1024]{1,0:T(8,128)(2,1)S(1)}, u32[]{:S(2)}, u32[]{:S(2)}) collective-permute-start(bf16[64,1024]{1,0:T(8,128)(2,1)S(1)} %collective-permute-done.21.rest_3_), channel_id=1, source_target_pairs={{0,4},{2,6},{4,0},{6,2},{8,12},{10,14},{12,8},{14,10},{16,20},{18,... | collective-permute-start | bytes 393224 | tf_op jit(solution)/shard_map/ppermute | solution.py:334
  87.6 8.6 %collective-permute-start.24 = (bf16[3,64,1024]{2,1,0:T(8,128)(2,1)S(1)}, bf16[3,64,1024]{2,1,0:T(8,128)(2,1)S(1)}, u32[]{:S(2)}, u32[]{:S(2)}) collective-permute-start(bf16[3,64,1024]{2,1,0:T(8,128)(2,1)S(1)} %pad_maximum_fusion.1), channel_id=1, source_target_pairs={{0,2},{2,0},{4,6},{6,4},{8,10},{10,8},{12,14},{14,12},{16,18},{18,... | collective-permute-start | bytes 1179656 | tf_op jit(solution)/shard_map/ppermute | solution.py:334
  89.4 6.8 %collective-permute-start.25 = (bf16[4,64,1024]{2,1,0:T(8,128)(2,1)S(1)}, bf16[4,64,1024]{2,1,0:T(8,128)(2,1)S(1)}, u32[]{:S(2)}, u32[]{:S(2)}) collective-permute-start(bf16[4,64,1024]{2,1,0:T(8,128)(2,1)S(1)} %pad_maximum_fusion), channel_id=1, source_target_pairs={{0,2},{2,0},{4,6},{6,4},{8,10},{10,8},{12,14},{14,12},{16,18},{18,... | collective-permute-start | bytes 1572872 | tf_op jit(solution)/shard_map/ppermute | solution.py:334
  89.4 5.9 %collective-permute-start.27 = (bf16[64,1024]{1,0:T(8,128)(2,1)S(1)}, bf16[64,1024]{1,0:T(8,128)(2,1)S(1)}, u32[]{:S(2)}, u32[]{:S(2)}) collective-permute-start(bf16[64,1024]{1,0:T(8,128)(2,1)S(1)} %collective-permute-done.20.rest_2_), channel_id=1, source_target_pairs={{0,4},{2,6},{4,0},{6,2},{8,12},{10,14},{12,8},{14,10},{16,20},{18,... | collective-permute-start | bytes 393224 | tf_op jit(solution)/shard_map/ppermute | solution.py:334
  95.3 1.7 %collective-permute-start.28 = (bf16[64,1024]{1,0:T(8,128)(2,1)S(1)}, bf16[64,1024]{1,0:T(8,128)(2,1)S(1)}, u32[]{:S(2)}, u32[]{:S(2)}) collective-permute-start(bf16[64,1024]{1,0:T(8,128)(2,1)S(1)} %collective-permute-done.27.own_block), channel_id=1, source_target_pairs={{0,2},{2,0},{4,6},{6,4},{8,10},{10,8},{12,14},{14,12},{16,18},{18,... | collective-permute-start | bytes 393224 | tf_op jit(solution)/shard_map/ppermute | solution.py:334
  97.1 7.1 %copy-start.1 = (bf16[256,512]{1,0:T(8,128)(2,1)S(1)}, bf16[256,512]{1,0:T(8,128)(2,1)}, u32[]{:S(2)}) copy-start(bf16[256,512]{1,0:T(8,128)(2,1)} %text_ref.1) | copy-start | bytes 786436
  97.5 5.3 %collective-permute-start.29 = (s16[80,512]{1,0:T(8,128)(2,1)S(1)}, s16[80,512]{1,0:T(8,128)(2,1)S(1)}, u32[]{:S(2)}, u32[]{:S(2)}) collective-permute-start(s16[80,512]{1,0:T(8,128)(2,1)S(1)} %get-tuple-element.88), channel_id=1, source_target_pairs={{0,1},{1,0},{2,3},{3,2},{4,5},{5,4},{6,7},{7,6},{8,9},{9,8},{10,11... | collective-permute-start | bytes 245768 | tf_op jit(solution)/shard_map/ppermute | solution.py:459
  99.1 5.0 %collective-permute-start.26 = (s16[80,512]{1,0:T(8,128)(2,1)S(1)}, s16[80,512]{1,0:T(8,128)(2,1)S(1)}, u32[]{:S(2)}, u32[]{:S(2)}) collective-permute-start(s16[80,512]{1,0:T(8,128)(2,1)S(1)} %get-tuple-element.84), channel_id=1, source_target_pairs={{0,1},{1,0},{2,3},{3,2},{4,5},{5,4},{6,7},{7,6},{8,9},{9,8},{10,11... | collective-permute-start | bytes 245768 | tf_op jit(solution)/shard_map/ppermute | solution.py:459
